TPU v7x, 32 devices: a whole 2x2x4 slice. The times are simulated.
32 devices in a mesh: fsdp: 2 (over x), ctx: 4 (over z), tp: 4 (over y, core).
Axes of the slice: x: 2, y: 2, z: 4, core: 2. Of those that a mesh axis runs over, the one named last changes fastest.
Arguments:
- tokens: bfloat16 [4, 2048, 1024], P('fsdp', 'ctx'), may hold values from -6 to 6
- segment_ids: int32 [4, 2048], P('fsdp'), may hold values from 0 to 15, never falling along the last dimension, each value on 1 to 1024 neighbouring positions
- attn_gain: bfloat16 [1024], P('fsdp'), may hold values from 0.25 to 1.75
- w_query: bfloat16 [1024, 2048], P('fsdp', 'tp'), may hold values from -0.1875 to 0.1875
- w_key: bfloat16 [1024, 1024], P('fsdp', 'tp'), may hold values from -0.1875 to 0.1875
- w_value: bfloat16 [1024, 1024], P('fsdp', 'tp'), may hold values from -0.1875 to 0.1875
- query_gain: bfloat16 [128], P('fsdp'), may hold values from 0.099609375 to 1.8984375
- key_gain: bfloat16 [128], P('fsdp'), may hold values from 0.099609375 to 1.8984375
- w_out: bfloat16 [2048, 1024], P('tp', 'fsdp'), may hold values from -0.375 to 0.375
- ffn_gain: bfloat16 [1024], P('fsdp'), may hold values from 0.25 to 1.75
- w_gate: bfloat16 [1024, 3072], P('fsdp', 'tp'), may hold values from -0.1875 to 0.1875
- w_up: bfloat16 [1024, 3072], P('fsdp', 'tp'), may hold values from -0.1875 to 0.1875
- w_down: bfloat16 [3072, 1024], P('tp', 'fsdp'), may hold values from -0.21875 to 0.21875
- out_grad: bfloat16 [4, 2048, 1024], P('fsdp', 'ctx'), may hold values from -6 to 6
Outputs:
- layer_out: bfloat16 [4, 2048, 1024], P('fsdp', 'ctx')
- input_grad: float32 [4, 2048, 1024], P('fsdp', 'ctx')
- attn_gain_grad: float32 [1024], P('fsdp')
- w_query_grad: float32 [1024, 2048], P('fsdp', 'tp')
- w_key_grad: float32 [1024, 1024], P('fsdp', 'tp')
- w_value_grad: float32 [1024, 1024], P('fsdp', 'tp')
- query_gain_grad: float32 [128], P('fsdp')
- key_gain_grad: float32 [128], P('fsdp')
- w_out_grad: float32 [2048, 1024], P('tp', 'fsdp')
- ffn_gain_grad: float32 [1024], P('fsdp')
- w_gate_grad: float32 [1024, 3072], P('fsdp', 'tp')
- w_up_grad: float32 [1024, 3072], P('fsdp', 'tp')
- w_down_grad: float32 [3072, 1024], P('tp', 'fsdp')
Inputs may be any that keep to these rules, and one draw needn't show every extreme that they name: `segment_ids`: ids never fall along a sequence, every id of 0 to 15 occurs in each sequence (so the padding segment 0 comes first), a segment has 1 to 1024 positions and some segment exactly 1024.
All inputs are finite; a program needn't handle non-finite values.
Results may differ from a plain program's by a relative error of at most 0.025.
Values may be sent and summed in bfloat16 or wider, within the bound.
No kernel may reach another device: no remote copies, remote signals or barrier semaphores. Data moves between devices by JAX's collectives and lax.ppermute only.
A program may use at most 192 MiB of HBM per device.

v0:
```python
import functools
import math

import jax
import jax.numpy as jnp
from jax import lax
from jax.experimental import pallas as pl
from jax.experimental.pallas import tpu as pltpu
from jax.sharding import PartitionSpec as P

epsilon = 1e-06
rope_base = 1000000.0
longest_segment = 1024
f32 = jnp.float32
bf16 = jnp.bfloat16

NN = (((1,), (0,)), ((), ()))
NT = (((1,), (1,)), ((), ()))
TN = (((0,), (0,)), ((), ()))


def dot(left, right, dims=NN):
    return lax.dot_general(left, right, dims, preferred_element_type=f32)


def inv_scale(values):
    return lax.rsqrt(jnp.mean(values * values, -1, keepdims=True) + epsilon)


def norm_back(values, scale, gain, grad):
    scaled = grad * gain
    return scale * scaled - values * (scale * scale * scale) * jnp.mean(
        scaled * values, -1, keepdims=True
    )


def rows_of(index, size):
    return pl.ds(pl.multiple_of(index * size, size), size)


def ordered(ref, fs, np_):
    if np_ == 1:
        return ref[...]
    half = ref.shape[-1] // 2
    first = ref[:, pl.ds(pl.multiple_of(fs * half, 128), half)]
    other = ref[:, pl.ds(pl.multiple_of((1 - fs) * half, 128), half)]
    return jnp.concatenate([first, other], 1)


def whole(shape):
    return pl.BlockSpec(shape, lambda *_: (0,) * len(shape))


def columns(parts):
    width = parts[0]
    return [(i * width, (i + 1) * width) for i in range(len(parts))]


def call(kernel, name, grid, ins, outs, scratch, scalars, *args, aliases=None, waits=()):
    skip = len(waits)

    def body_(ids, *refs):
        kernel(ids, *refs[skip:])

    return pl.pallas_call(
        body_,
        name=name,
        out_shape=[o[0] for o in outs],
        grid_spec=pltpu.PrefetchScalarGridSpec(
            num_scalar_prefetch=1,
            grid=grid,
            in_specs=[pl.BlockSpec(memory_space=pl.ANY)] * skip + ins,
            out_specs=[o[1] for o in outs],
            scratch_shapes=scratch,
        ),
        input_output_aliases={k + skip: v for k, v in (aliases or {}).items()},
        compiler_params=pltpu.CompilerParams(dimension_semantics=("arbitrary",) * len(grid)),
        cost_estimate=pl.CostEstimate(flops=1, bytes_accessed=1, transcendentals=0),
    )(scalars, *waits, *args)


def project(low, weights, np_):
    width = low.shape[1] // np_
    acc = None
    for i in range(np_):
        one = dot(low[:, i * width : (i + 1) * width], weights[i][...])
        acc = one if acc is None else acc + one
    return acc


def turn(acc, count, size, g, c, s, out):
    for h in range(count):
        u = acc[:, h * size : (h + 1) * size]
        u = u * inv_scale(u) * g
        out[:, h * size : (h + 1) * size] = (u * c + pltpu.roll(u, size // 2, 1) * s).astype(bf16)


def kv_kernel(kv_heads, size, np_, passed, ids, tok, gain, cos, sin, kg, *rest):
    weights, (normed, kv_out, pre_out) = rest[:np_], rest[np_ + passed : np_ + passed + 3]
    x = ordered(tok, ids[0], np_).astype(f32)
    low = (x * inv_scale(x) * gain[...]).astype(bf16)
    normed[...] = low
    acc = project(low, weights, np_)
    pre_out[...] = acc[:, : kv_heads * size]
    turn(acc, kv_heads, size, kg[...], cos[...], sin[...], kv_out)
    kv_out[:, kv_heads * size :] = acc[:, kv_heads * size :].astype(bf16)


def query_kernel(heads, size, np_, ids, normed, cos, sin, qg, *rest):
    weights, (q_out, pre_out) = rest[:np_], rest[np_:]
    acc = project(normed[...], weights, np_)
    pre_out[...] = acc
    turn(acc, heads, size, qg[...], cos[...], sin[...], q_out)


def allowed_block(key_base, start, row_base, block, rows):
    key_index = key_base + lax.broadcasted_iota(jnp.int32, (block, rows), 0)
    row_index = row_base + lax.broadcasted_iota(jnp.int32, (block, rows), 1)
    return (key_index >= start) & (key_index <= row_index)


def attend_blocks(cfg, low, high, base, kv, q, start_row, row_base, acc, total):
    heads, kv_heads, size, block, scale2 = cfg
    group = heads // kv_heads
    rows = q.shape[0]

    def step(kb, carry):
        at = pl.ds(pl.multiple_of((kb - base) * block, block), block)
        allow = allowed_block(kb * block, start_row, row_base, block, rows)
        for g in range(kv_heads):
            k = kv[at, g * size : (g + 1) * size]
            v = kv[at, (kv_heads + g) * size : (kv_heads + g + 1) * size]
            for h in range(g * group, (g + 1) * group):
                s = dot(k, q[:, h * size : (h + 1) * size], NT)
                e = jnp.where(allow, jnp.exp2(s * scale2), 0.0)
                total[h : h + 1, :] += jnp.sum(e, 0, keepdims=True)
                acc[h * size : (h + 1) * size, :] += dot(v, e.astype(bf16), TN)
        return carry

    lax.fori_loop(low, high, step, 0)


def attend_own_kernel(cfg, back, ids, q, start, kv, acc, total):
    t = pl.program_id(0)
    rows = q.shape[0]
    base = back * kv.shape[0]
    acc[...] = jnp.zeros_like(acc)
    total[...] = jnp.zeros_like(total)
    first = base // cfg[3]
    attend_blocks(
        cfg, jnp.maximum(ids[2 + t], first), (base + (t + 1) * rows) // cfg[3], first,
        kv, q, start[...], base + t * rows, acc, total,
    )


def attend_kernel(cfg, np_, back, out_at, ids, q, start, acc_in, total_in, *rest):
    heads, _, size, block, _ = cfg
    chunks = rest[:back]
    w_out = rest[back : back + np_]
    own, oth, mixed_out, lse_out, kv, acc, total = rest[back + np_ :]
    t = pl.program_id(0)
    core = ids[1]
    rows = q.shape[0]
    length = chunks[0].shape[0]

    @pl.when(t == 0)
    def _():
        for i in range(back):
            kv[i * length : (i + 1) * length, :] = chunks[i][...]

    acc[...] = acc_in[...]
    total[...] = total_in[...]
    attend_blocks(
        cfg, ids[2 + t], back * length // block, 0, kv, q, start[...], back * length + t * rows, acc, total
    )
    sums = total[...]
    sums = jnp.where(sums > 0.0, sums, 1.0)
    lse_out[...] = jnp.log2(sums)
    inverse = 1.0 / sums
    for h in range(heads):
        part = (acc[h * size : (h + 1) * size, :] * inverse[h : h + 1, :]).astype(bf16)
        mixed_out[h * size : (h + 1) * size, :] = part
    mixed = mixed_out[...]
    width = w_out[0].shape[1]
    for i in range(np_):
        part = dot(mixed, w_out[i][out_at:, :], TN).astype(bf16)

        @pl.when(t == core)
        def _():
            own[:, i * width : (i + 1) * width] = part

        @pl.when(t != core)
        def _():
            oth[:, i * width : (i + 1) * width] = part


def ffn_kernel(np_, ids, tok, b_own, b_oth, valid, gain, grad, *rest):
    gate_w, up_w, down_w = rest[:np_], rest[np_ : 2 * np_], rest[2 * np_ : 3 * np_]
    n2_out, act_out, gg_out, gu_out, own, oth, gain_out, hat, acc = rest[3 * np_ :]
    f = pl.program_id(0)
    core = ids[1]
    half = b_own.shape[0]

    @pl.when(f == 0)
    def _():
        for ref, tile in ((b_own, core), (b_oth, 1 - core)):
            at = rows_of(tile, half)
            tokens = ordered(tok.at[at], ids[0], np_).astype(f32)
            resid = tokens + valid[at, :1] * ref[...].astype(f32)
            normal = resid * inv_scale(resid)
            hat[at, :] = normal
            n2_out[at, :] = (normal * gain[...]).astype(bf16)
        acc[...] = jnp.zeros_like(acc)

    width = tok.shape[1] // np_
    parts = [(i * width, (i + 1) * width) for i in range(np_)]
    gate = up = active_grad = None
    for i, (a, b) in enumerate(parts):
        x = n2_out[:, a:b]
        g, u, d = dot(x, gate_w[i][...]), dot(x, up_w[i][...]), dot(grad[:, a:b], down_w[i][...], NT)
        gate, up, active_grad = (g, u, d) if i == 0 else (gate + g, up + u, active_grad + d)
    sigma = jax.nn.sigmoid(gate)
    silu = gate * sigma
    act_out[...] = (silu * up).astype(bf16)
    gg = (active_grad * up * sigma * (1.0 + gate * (1.0 - sigma))).astype(bf16)
    gu = (active_grad * silu).astype(bf16)
    gg_out[...] = gg
    gu_out[...] = gu
    for i, (a, b) in enumerate(parts):
        acc[:, a:b] += dot(gg, gate_w[i][...], NT) + dot(gu, up_w[i][...], NT)

    @pl.when(f == pl.num_programs(0) - 1)
    def _():
        own[...] = acc[rows_of(core, half), :].astype(bf16)
        oth[...] = acc[rows_of(1 - core, half), :].astype(bf16)
        gain_out[...] = jnp.sum(acc[...] * hat[...], 0, keepdims=True)


def down_kernel(np_, ids, act, *rest):
    weights, (own, oth) = rest[:np_], rest[-2:]
    t = pl.program_id(0)
    width = weights[0].shape[1]
    for i in range(np_):
        part = dot(act[...], weights[i][...]).astype(bf16)

        @pl.when(t == ids[1])
        def _():
            own[:, i * width : (i + 1) * width] = part

        @pl.when(t != ids[1])
        def _():
            oth[:, i * width : (i + 1) * width] = part


def picked(ids, own, oth, t):
    return jnp.where(ids[1] == t, own[...].astype(f32), oth[...].astype(f32))


def attend_back_kernel(cfg, out_at, ids, tok, b_own, b_oth, t_own, t_oth, valid, gain, grad, mixed, lse, q, start, pre, cos, sin, qg, *rest):
    heads, kv_heads, size, np_, back, block, scale2 = cfg
    chunks = rest[: back + 1]
    w_out = rest[back + 1 : back + 1 + np_]
    outs = rest[back + 1 + np_ :]
    resid_out, branch_out, gq_out, gain_out = outs[:4]
    far = outs[4 : 4 + back + 1]
    kv, dkv, dq, dout = outs[4 + back + 1 :]
    t = pl.program_id(0)
    rows = q.shape[0]
    length = chunks[0].shape[0]
    group = heads // kv_heads
    scale = size**-0.5

    @pl.when(t == 0)
    def _():
        for i in range(back + 1):
            kv[i * length : (i + 1) * length, :] = chunks[i][...]
        dkv[...] = jnp.zeros_like(dkv)
        gain_out[...] = jnp.zeros_like(gain_out)

    resid = ordered(tok, ids[0], np_).astype(f32) + valid[:, :1] * picked(ids, b_own, b_oth, t)
    resid_grad = ordered(grad, ids[0], np_).astype(f32) + norm_back(
        resid, inv_scale(resid), gain[...], picked(ids, t_own, t_oth, t)
    )
    resid_out[...] = resid_grad
    low = (valid[:, :1] * resid_grad).astype(bf16)
    branch_out[...] = low
    width = low.shape[1] // np_
    mixed_grad = dot(w_out[0][out_at:, :], low[:, :width], NT)
    for i in range(1, np_):
        mixed_grad = mixed_grad + dot(w_out[i][out_at:, :], low[:, i * width : (i + 1) * width], NT)
    dout[...] = mixed_grad.astype(bf16)
    delta = [
        jnp.sum(
            dout[h * size : (h + 1) * size, :].astype(f32) * mixed[h * size : (h + 1) * size, :].astype(f32),
            0,
            keepdims=True,
        )
        for h in range(heads)
    ]
    dq[...] = jnp.zeros_like(dq)
    row_base = back * length + t * rows
    start_row = start[...]

    def step(kb, carry):
        at = pl.ds(pl.multiple_of(kb * block, block), block)
        allow = allowed_block(kb * block, start_row, row_base, block, rows)
        for g in range(kv_heads):
            k = kv[at, g * size : (g + 1) * size]
            v = kv[at, (kv_heads + g) * size : (kv_heads + g + 1) * size]
            dk = dv = None
            for h in range(g * group, (g + 1) * group):
                qh = q[:, h * size : (h + 1) * size]
                do = dout[h * size : (h + 1) * size, :]
                s = dot(k, qh, NT)
                p = jnp.where(allow, jnp.exp2(s * scale2 - lse[h : h + 1, :]), 0.0)
                dp = dot(v, do)
                ds = (p * (dp - delta[h])).astype(bf16)
                one_v = dot(p.astype(bf16), do, NT)
                one_k = dot(ds, qh)
                dk, dv = (one_k, one_v) if dk is None else (dk + one_k, dv + one_v)
                dq[h * size : (h + 1) * size, :] += dot(k, ds, TN)
            dkv[at, g * size : (g + 1) * size] += dk * scale
            dkv[at, (kv_heads + g) * size : (kv_heads + g + 1) * size] += dv
        return carry

    lax.fori_loop(ids[2 + t], (row_base + rows) // block, step, 0)
    c, s_ = cos[...], sin[...]
    for h in range(heads):
        u = dq[h * size : (h + 1) * size, :].T * scale
        u = u * c - pltpu.roll(u, size // 2, 1) * s_
        v = pre[:, h * size : (h + 1) * size]
        r = inv_scale(v)
        gain_out[...] += jnp.sum(u * (v * r), 0, keepdims=True)
        gq_out[:, h * size : (h + 1) * size] = norm_back(v, r, qg[...], u).astype(bf16)

    @pl.when(t == pl.num_programs(0) - 1)
    def _():
        for i in range(back + 1):
            far[i][...] = dkv[i * length : (i + 1) * length, :].astype(far[i].dtype)


def input_back_kernel(cfg, ids, tok, gain, gq, near, came, pre, cos, sin, kg, *rest):
    heads, kv_heads, size, np_ = cfg
    weights = rest[: 2 * np_]
    gkv_out, own, oth, k_gain, a_gain = rest[-5:]
    t = pl.program_id(0)
    core = ids[1]

    @pl.when(t == 0)
    def _():
        k_gain[...] = jnp.zeros_like(k_gain)
        a_gain[...] = jnp.zeros_like(a_gain)

    dkv = near[...] + came[...].astype(f32)
    c, s_ = cos[...], sin[...]
    for h in range(kv_heads):
        u = dkv[:, h * size : (h + 1) * size]
        u = u * c - pltpu.roll(u, size // 2, 1) * s_
        v = pre[:, h * size : (h + 1) * size]
        r = inv_scale(v)
        k_gain[...] += jnp.sum(u * (v * r), 0, keepdims=True)
        gkv_out[:, h * size : (h + 1) * size] = norm_back(v, r, kg[...], u).astype(bf16)
    gkv_out[:, kv_heads * size :] = dkv[:, kv_heads * size :].astype(bf16)
    x = ordered(tok, ids[0], np_).astype(f32)
    normal = x * inv_scale(x)
    width = x.shape[1] // np_
    for i in range(np_):
        at = slice(i * width, (i + 1) * width)
        part = dot(gq[...], weights[i][...], NT)
        part = part + dot(gkv_out[...], weights[np_ + i][...], NT)
        a_gain[:, at] += jnp.sum(part * normal[:, at], 0, keepdims=True)
        low = part.astype(bf16)

        @pl.when(t == core)
        def _():
            own[:, at] = low

        @pl.when(t != core)
        def _():
            oth[:, at] = low


def place(out, values, fs, np_):
    width = values.shape[1] // np_
    if np_ == 1:
        out[...] = values
        return
    for i in range(2):
        at = pl.ds(pl.multiple_of((fs if i == 0 else 1 - fs) * width, 128), width)
        out[:, at] = values[:, i * width : (i + 1) * width]


def layer_kernel(np_, fine, ids, tok, b_own, b_oth, f_own, f_oth, valid, *rest):
    out = rest[-1]
    t = pl.program_id(0) // fine
    v = valid[:, :1]
    resid = ordered(tok, ids[0], np_).astype(f32) + v * picked(ids, b_own, b_oth, t)
    place(out, (resid + v * picked(ids, f_own, f_oth, t)).astype(bf16), ids[0], np_)


def input_kernel(np_, fine, ids, tok, resid_grad, g_own, g_oth, gain, *rest):
    out = rest[-1]
    t = pl.program_id(0) // fine
    x = ordered(tok, ids[0], np_).astype(f32)
    grad = resid_grad[...] + norm_back(x, inv_scale(x), gain[...], picked(ids, g_own, g_oth, t))
    place(out, grad, ids[0], np_)


def product_kernel(pairs, groups, tiles, split, left_t, tail, ids, *rest):
    count = 1 if split is None else 2
    outs = rest[-count:]
    m = pl.program_id(0)

    def low():
        columns = []
        for j in range(groups):
            total = None
            for i in range(pairs):
                one = dot(rest[i][...], rest[pairs * (1 + j) + i][...], NN if left_t else TN)
                total = one if total is None else total + one
            columns.append(total.astype(bf16))
        return columns[0] if groups == 1 else jnp.concatenate(columns, 1)

    if split is None:
        outs[0][...] = low()
    elif split == 1:
        value = low()
        width = value.shape[1] // 2
        outs[0][...] = value[:, :width]
        outs[1][...] = value[:, width:]
    else:

        @pl.when(m < tiles // 2)
        def _():
            outs[0][...] = low()

        @pl.when((m >= tiles // 2) & (m < tiles))
        def _():
            outs[1][...] = low()

    if tail:

        @pl.when(m == tiles)
        def _():
            at = pairs * (1 + groups)
            for i in range(2):
                outs[i][: rest[at + i].shape[0], :] = rest[at + i][...]


def product(name, ids, lefts, rights, split, tile, left_t=False, at=0, height=None, into=None, tail=None, waits=()):
    pairs, groups = len(lefts), len(rights)
    m = lefts[0].shape[0 if left_t else 1]
    k = lefts[0].shape[1 if left_t else 0]
    n = sum(r[0].shape[1] for r in rights)
    tiles = m // tile
    ins, args = [], []
    for left in lefts:
        if left_t:
            ins.append(pl.BlockSpec((tile, k), lambda i, *_: (jnp.minimum(i, tiles - 1), 0)))
        else:
            ins.append(pl.BlockSpec((k, tile), lambda i, *_: (0, jnp.minimum(i, tiles - 1))))
        args.append(left)
    for group in rights:
        for right in group:
            ins.append(whole(right.shape))
            args.append(right)
    if split is None:
        shape = jax.ShapeDtypeStruct((height or m, n), bf16)
        outs = [(shape, pl.BlockSpec((tile, n), lambda i, *_: (i + at, 0)))]
    elif split == 1:
        shape = jax.ShapeDtypeStruct((height or m, n // 2), bf16)
        outs = [(shape, pl.BlockSpec((tile, n // 2), lambda i, *_: (i + at, 0)))] * 2
    else:
        half = tiles // 2
        shape = jax.ShapeDtypeStruct((height or m // 2, n), bf16)
        last = at + half if tail is not None else at + half - 1

        def own(i, *_):
            return (jnp.where(i < half, i + at, jnp.where(i < tiles, half - 1 + at, last)), 0)

        def other(i, *_):
            return (jnp.where(i < tiles, jnp.maximum(i - half, 0) + at, last), 0)

        outs = [(shape, pl.BlockSpec((tile, n), own)), (shape, pl.BlockSpec((tile, n), other))]
    if tail is not None:
        ins += [whole(v.shape) for v in tail]
        args += list(tail)
    aliases = None
    if into is not None:
        aliases = {1 + len(ins) + i: i for i in range(len(into))}
        ins += [pl.BlockSpec(memory_space=pl.ANY)] * len(into)
        args += list(into)
    return call(
        functools.partial(product_kernel, pairs, groups, tiles, split, left_t, tail is not None),
        name, (tiles + (tail is not None),), ins, outs, [], ids, *args, aliases=aliases, waits=waits,
    )


def swap(values, axis, bit, size):
    return lax.ppermute(values, axis, [(i, i ^ bit) for i in range(size)])


def plus(a, b):
    return a + b


class Line:
    def __init__(self):
        self.last = None
        self.waited = ()

    def __call__(self, fn, *args):
        if self.last is not None:
            args, _ = lax.optimization_barrier((args, self.last))
        outs = fn(*args)
        self.last = jax.tree.leaves(outs)[0]
        return outs

    def wait(self, *values):
        self.waited += values

    def take(self):
        values, self.waited = self.waited, ()
        return values

    def after(self, value):
        return lax.optimization_barrier((value, self.last, self.waited))[0]


class Steps:
    def __init__(self, steps):
        self.steps, self.value = steps, None

    def __call__(self, count=1):
        for _ in range(count):
            self.value = next(self.steps)
        return self.value


def sum_tp(line, own, oth, size):
    total = line(plus, own, swap(line.after(oth), "tp", 1, size))
    yield total
    bit = 2
    while bit < size:
        total = line(plus, total, swap(total, "tp", bit, size))
        bit *= 2
        if bit < size:
            yield total
    yield total, swap(total, "tp", 1, size)


def sum_line(line, total, axis, size):
    index = lax.axis_index(axis)
    middle = size // 2
    for i in range(middle - 1):
        came = lax.ppermute(total, axis, [(i, i + 1), (size - 1 - i, size - 2 - i)])
        total = line(plus, total, came)
        yield total
    total = line(plus, total, lax.ppermute(total, axis, [(middle - 1, middle), (middle, middle - 1)]))
    yield total
    for i in reversed(range(middle - 1)):
        came = lax.ppermute(total, axis, [(i + 1, i), (size - 2 - i, size - 1 - i)])
        total = jnp.where((index == i) | (index == size - 1 - i), came, total)
    yield total


def sum_small(values, axis, size):
    bit = 1
    while bit < size:
        values = values + swap(values, axis, bit, size)
        bit *= 2
    return values


def body(
    n_fs, n_ctx, n_tp,
    tokens, segment_ids, attn_gain, w_query, w_key, w_value, query_gain, key_gain,
    w_out, ffn_gain, w_gate, w_up, w_down, out_grad,
):
    seqs, length, model = tokens.shape
    paired = n_fs == 2
    np_ = 2 if paired else 1
    fs = lax.axis_index("fsdp")
    ctx = lax.axis_index("ctx")
    core = lax.axis_index("tp") % 2
    size = query_gain.shape[0] * n_fs
    heads = w_query.shape[1] // size
    kv_heads = w_key.shape[1] // size
    hidden = w_gate.shape[1]
    q_width, kv_width = heads * size, kv_heads * size
    rows = length // 2
    block = rows
    back = min(n_ctx - 1, -(-(longest_segment - 1) // length))
    scale2 = size**-0.5 * math.log2(math.e)

    def gather(weight, axis):
        if paired:
            return [weight, swap(weight, "fsdp", 1, 2)]
        return [lax.all_gather(weight, "fsdp", axis=axis, tiled=True)]

    kv_w = gather(jnp.concatenate([w_key, w_value], 1), 0)
    query_w = gather(w_query, 0)
    gate_w = gather(w_gate, 0)
    up_w = gather(w_up, 0)
    down_out = [jnp.concatenate([w_down, w_out], 0)] if paired else []
    out_at = hidden if paired else 0

    part, small = attn_gain.shape[0], query_gain.shape[0]
    padding = part - 2 * small
    gains = jnp.concatenate([query_gain, key_gain] + ([jnp.zeros((padding,), bf16)] if padding > 0 else []))
    gains = jnp.stack([attn_gain, ffn_gain, gains[:part]]) if padding >= 0 else None
    if paired:
        gains, kv_w[0] = lax.optimization_barrier((gains, kv_w[0]))
    both = [gains, swap(gains, "fsdp", 1, 2)] if paired else None
    if paired:
        wide = jnp.concatenate(both, 1).astype(f32)
        gain_one, gain_two = wide[:1], wide[1:2]

    def natural(first, values):
        if not paired:
            return lax.all_gather(values, "fsdp", axis=0, tiled=True)[None, :].astype(f32)
        own_first = jnp.concatenate([b[2:, first : first + small] for b in both], 1)
        return jnp.where(fs == 0, own_first, jnp.roll(own_first, small, 1)).astype(f32)

    if not paired:
        gain_one, gain_two = natural(0, attn_gain), natural(0, ffn_gain)
    qg, kg = natural(0, query_gain), natural(small, key_gain)

    def reorder(values):
        if not paired:
            return values
        half = model // 2
        return jnp.where(fs == 0, values, jnp.concatenate([values[..., half:], values[..., :half]], -1))

    index = ctx * length + jnp.arange(length, dtype=jnp.int32)
    row_seg = lax.dynamic_slice_in_dim(segment_ids, ctx * length, length, 1)
    first = jnp.sum((segment_ids[:, None, :] < row_seg[:, :, None]).astype(jnp.int32), -1)
    position = index[None, :] - first
    live = row_seg != 0
    valid = jnp.broadcast_to(live.astype(f32)[:, :, None], (seqs, length, 128))
    window = (back + 1) * length
    start = jnp.where(live, jnp.maximum(first - (ctx - back) * length, 0), window + 1)
    lowest = jnp.min(start.reshape(seqs, 2, rows), -1) // block
    frequency = rope_base ** (-(jnp.arange(size // 2, dtype=f32) * 2.0 / size))
    turned = position.astype(f32)[:, :, None] * frequency
    cosine, sine = jnp.cos(turned), jnp.sin(turned)
    cos = jnp.concatenate([cosine, cosine], -1)
    sin = jnp.concatenate([-sine, sine], -1)
    low_grad = jnp.where(live[:, :, None], reorder(out_grad), jnp.zeros((), bf16))
    start = start[:, None, :]

    def scalars(s):
        return jnp.concatenate([jnp.stack([fs, core]).astype(jnp.int32), lowest[s]])

    ids = [scalars(s) for s in range(seqs)]
    cfg = (heads, kv_heads, size, np_, back, block, scale2)
    cfg_forward = (heads, kv_heads, size, block, scale2)

    def tiled(width):
        return pl.BlockSpec((rows, width), lambda i, *_: (i, 0))

    def tiled_t(height):
        return pl.BlockSpec((height, rows), lambda i, *_: (0, i))

    def of(s, width, tile=rows):
        return pl.BlockSpec((None, tile, width), lambda i, *_: (s, i, 0))

    def all_of(s, width):
        return pl.BlockSpec((None, length, width), lambda *_: (s, 0, 0))

    def lanes(s):
        return pl.BlockSpec((None, 1, rows), lambda i, *_: (s, 0, i))

    def shape(*dims, dtype=bf16):
        return jax.ShapeDtypeStruct(dims, dtype)

    half_pair = [(shape(rows, model), whole((rows, model)))] * 2

    line = Line()
    up_perm = [(i, i + 1) for i in range(n_ctx - 1)]
    down_perm = [(i + 1, i) for i in range(n_ctx - 1)]
    kv_shape = (length, 2 * kv_width)
    sums = 8 * -(-heads // 8)

    def kernel(name, body_, grid, ins, outs, scratch, s, *args, aliases=None):
        count = len(args)

        def run(*all_args):
            return call(
                body_, name, grid, ins, outs, scratch, ids[s], *all_args[:count],
                aliases=aliases, waits=all_args[count:],
            )

        return line(run, *args, *line.take())

    normed, own_kv, pre_k, queries, pre_q = [], [], [], [], []

    def keys(s, through=()):
        first = 6 + len(kv_w)
        n, k, p, *through = kernel(
            "keys", functools.partial(kv_kernel, kv_heads, size, np_, len(through)), (2,),
            [of(s, model), whole((1, model)), of(s, size), of(s, size), whole((1, size))]
            + [whole(w.shape) for w in kv_w] + [pl.BlockSpec(memory_space=pl.ANY)] * len(through),
            [
                (shape(length, model), tiled(model)),
                (shape(*kv_shape), tiled(2 * kv_width)),
                (shape(length, kv_width, dtype=f32), tiled(kv_width)),
            ]
            + [(shape(*v.shape), pl.BlockSpec(memory_space=pl.ANY)) for v in through],
            [], s, tokens, gain_one, cos, sin, kg, *kv_w, *through,
            aliases={first + i: 3 + i for i in range(len(through))},
        )
        normed.append(n)
        own_kv.append(k)
        pre_k.append(p)
        return through

    def query(s):
        q, p = kernel(
            "query", functools.partial(query_kernel, heads, size, np_), (2,),
            [tiled(model), of(s, size), of(s, size), whole((1, size))] + [whole(w.shape) for w in query_w],
            [
                (shape(length, q_width), tiled(q_width)),
                (shape(length, q_width, dtype=f32), tiled(q_width)),
            ],
            [], s, normed[s], cos, sin, qg, *query_w,
        )
        queries.append(q)
        pre_q.append(p)

    kv = []

    def spread(s):
        chunks = [line.after(own_kv[s])]
        chunks.insert(0, lax.ppermute(chunks[0], "ctx", up_perm))
        kv.append(chunks)

    def forward(s):
        for _ in range(back - 1):
            kv[s].insert(0, lax.ppermute(line.after(kv[s][0]), "ctx", up_perm))

    sums_own, mixed, lse, branch = [], [], [], []

    def attend_own(s):
        sums_own.append(
            kernel(
                "attend_own", functools.partial(attend_own_kernel, cfg_forward, back), (2,),
                [tiled(q_width), lanes(s), whole(kv_shape)],
                [
                    (shape(q_width, length, dtype=f32), tiled_t(q_width)),
                    (shape(sums, length, dtype=f32), tiled_t(sums)),
                ],
                [], s, queries[s], start, own_kv[s],
            )
        )

    def attend(s):
        own, oth, m, l = kernel(
            "attend", functools.partial(attend_kernel, cfg_forward, np_, back, out_at), (2,),
            [tiled(q_width), lanes(s), tiled_t(q_width), tiled_t(sums)]
            + [whole(kv_shape)] * back + [whole(w.shape) for w in out_w],
            half_pair
            + [
                (shape(q_width, length), tiled_t(q_width)),
                (shape(sums, length, dtype=f32), tiled_t(sums)),
            ],
            [
                pltpu.VMEM((back * length, 2 * kv_width), bf16),
                pltpu.VMEM((q_width, rows), f32),
                pltpu.VMEM((sums, rows), f32),
            ],
            s, queries[s], start, *sums_own[s], *kv[s][:back], *out_w,
        )
        mixed.append(m)
        lse.append(l)
        branch.append(Steps(sum_tp(line, own, oth, n_tp)))

    tile = 256
    steps = hidden // tile
    normed_two, active, grad_gate, grad_up, grad_two, ffn_gains = [], [], [], [], [], []

    def ffn(s):
        col = pl.BlockSpec((length, tile), lambda i, *_: (0, i))
        w_in = [pl.BlockSpec((w.shape[0], tile), lambda i, *_: (0, i)) for w in gate_w]
        w_dn = [pl.BlockSpec((tile, w.shape[1]), lambda i, *_: (i, 0)) for w in down_w]
        n2, act, gg, gu, own, oth, fg = kernel(
            "ffn", functools.partial(ffn_kernel, np_), (steps,),
            [all_of(s, model), whole((rows, model)), whole((rows, model)), all_of(s, 128),
             whole((1, model)), all_of(s, model)] + w_in + w_in + w_dn,
            [
                (shape(length, model), whole((length, model))),
                (shape(length, hidden), col),
                (shape(length, hidden), col),
                (shape(length, hidden), col),
            ]
            + half_pair
            + [(shape(1, model, dtype=f32), whole((1, model)))],
            [pltpu.VMEM((length, model), f32), pltpu.VMEM((length, model), f32)],
            s, tokens, *branch[s].value, valid, gain_two, low_grad, *gate_w, *up_w, *down_w,
        )
        normed_two.append(n2)
        active.append(act)
        grad_gate.append(gg)
        grad_up.append(gu)
        grad_two.append(Steps(sum_tp(line, own, oth, n_tp)))
        ffn_gains.append(fg)

    both_pair = [
        (shape(seqs * rows, model), lambda s: pl.BlockSpec((rows, model), lambda *_: (s, 0))),
    ] * 2

    def pair_of(s):
        return [(one, spec(s)) for one, spec in both_pair]

    layers = []

    def down(s):
        first = 2 + len(down_w)
        into = list(layers)
        layers[:] = kernel(
            "down", functools.partial(down_kernel, np_), (2,),
            [tiled(hidden)] + [whole((hidden, w.shape[1])) for w in down_w] + [pl.BlockSpec(memory_space=pl.ANY)] * len(into),
            pair_of(s), [], s, active[s], *down_w, *into,
            aliases={first: 0, first + 1: 1} if into else None,
        )
        if s == seqs - 1:
            layers[:] = [Steps(sum_tp(line, *layers, n_tp))]

    fine = 1
    small_rows = rows // fine

    def halves(s):
        return [pl.BlockSpec((small_rows, model), lambda i, *_: (s * fine + i % fine, 0))] * 2

    finished = {}

    def output(name, body_, s, ins, dtype, *args):
        extra = [finished[name]] if name in finished else []
        finished[name] = kernel(
            name, functools.partial(body_, np_, fine), (2 * fine,),
            [of(s, model, small_rows)] + ins + [pl.BlockSpec(memory_space=pl.ANY)] * len(extra),
            [(shape(seqs, length, model, dtype=dtype), of(s, model, small_rows))],
            [], s, tokens, *args, *extra,
            aliases={2 + len(ins): 0} if extra else None,
        )[0]

    def layer_output(s):
        output(
            "layer_out", layer_kernel, s, halves(0) + halves(s) + [of(s, 128, small_rows)], bf16,
            *branch[s].value, *layers[0].value, valid,
        )

    resid_grad, grad_branch, grad_query, near, q_gains, came = [], [], [], [], [], []

    def bring(far):
        moving = None
        for one in far:
            one = line.after(one) if moving is None else line(plus, one, moving)
            moving = lax.ppermute(one, "ctx", down_perm)
            yield moving

    def attend_back(s):
        far_shapes = [(shape(*kv_shape), whole(kv_shape))] * back
        rg, gb, gq, qgain, *far, dkv = kernel(
            "attend_back", functools.partial(attend_back_kernel, cfg, out_at), (2,),
            [of(s, model)] + [whole((rows, model))] * 4 + [of(s, 128), whole((1, model)), of(s, model),
             tiled_t(q_width), tiled_t(sums), tiled(q_width), lanes(s),
             tiled(q_width), of(s, size), of(s, size), whole((1, size))]
            + [whole(kv_shape)] * (back + 1)
            + [whole(w.shape) for w in out_w],
            [
                (shape(length, model, dtype=f32), tiled(model)),
                (shape(length, model), tiled(model)),
                (shape(length, q_width), tiled(q_width)),
                (shape(1, size, dtype=f32), whole((1, size))),
            ]
            + far_shapes
            + [(shape(*kv_shape, dtype=f32), whole(kv_shape))],
            [
                pltpu.VMEM((window, 2 * kv_width), bf16),
                pltpu.VMEM((window, 2 * kv_width), f32),
                pltpu.VMEM((q_width, rows), f32),
                pltpu.VMEM((q_width, rows), bf16),
            ],
            s, tokens, *branch[s].value, *grad_two[s].value, valid, gain_two, out_grad, mixed[s], lse[s], queries[s],
            start, pre_q[s], cos, sin, qg, *kv[s], *out_w,
        )
        came.append(Steps(bring(far)))
        resid_grad.append(rg)
        grad_branch.append(gb)
        grad_query.append(gq)
        q_gains.append(qgain)
        near.append(dkv)

    grad_kv, k_gains, a_gains, grad_one = [], [], [], []
    qkv_w = query_w + kv_w

    def input_back(s):
        into = list(grad_one)
        first = 11 + len(qkv_w)
        gkv, own, oth, kgain, again = kernel(
            "input_back", functools.partial(input_back_kernel, (heads, kv_heads, size, np_)), (2,),
            [of(s, model), whole((1, model)), tiled(q_width), tiled(2 * kv_width), tiled(2 * kv_width),
             tiled(kv_width), of(s, size), of(s, size), whole((1, size))]
            + [whole(w.shape) for w in qkv_w] + [pl.BlockSpec(memory_space=pl.ANY)] * len(into),
            [(shape(*kv_shape), tiled(2 * kv_width))]
            + pair_of(s)
            + [(shape(1, size, dtype=f32), whole((1, size))), (shape(1, model, dtype=f32), whole((1, model)))],
            [], s, tokens, gain_one, grad_query[s], near[s], came[s].value, pre_k[s], cos, sin, kg, *qkv_w, *into,
            aliases={first - 1: 1, first: 2} if into else None,
        )
        grad_kv.append(gkv)
        k_gains.append(kgain)
        a_gains.append(again)
        grad_one[:] = [own, oth]
        if s == seqs - 1:
            grad_one[:] = [Steps(sum_tp(line, own, oth, n_tp))]

    def input_output(s):
        output(
            "input_grad", input_kernel, s, [pl.BlockSpec((small_rows, model), lambda i, *_: (i, 0))]
            + halves(s) + [whole((1, model))], f32,
            resid_grad[s], *grad_one[0].value, gain_one,
        )

    rows_split, cols_split = (0, 1) if paired else (None, None)

    def reduced(parts, axis):
        if paired:
            total = line(plus, parts[0], swap(parts[1], "fsdp", 1, 2))
        else:
            total = lax.psum_scatter(parts[0], "fsdp", scatter_dimension=axis, tiled=True)
        yield total
        yield from sum_line(line, total, "ctx", n_ctx)

    def weight(name, lefts, rights, split, left_t=False, **place_):
        def run(lefts, rights, place_):
            return product(name, ids[0], lefts, rights, split, 256, left_t, **place_)

        if not paired:
            place_ = {}
        numbers = {k: v for k, v in place_.items() if k in ("at", "height")}
        arrays = {k: v for k, v in place_.items() if k not in numbers and v is not None}
        arrays["waits"] = line.take()
        return line(lambda l, r, x: run(l, r, {**numbers, **x}), list(lefts), [list(r) for r in rights], arrays)

    gain_width = 2 * kv_width
    gain_rows = 16 * -(-(2 * part + 2 * small) // (16 * gain_width))

    def gain_sum():
        values = jnp.concatenate([sum(a_gains), sum(ffn_gains), sum(q_gains), sum(k_gains)], 1)
        bit = 1
        while bit < n_tp:
            values = line(jnp.add, values, swap(values, "tp", bit, n_tp))
            bit *= 2
            yield values
        yield values

    def gain_parts(values):
        def one(own):
            pieces = [values[:, (0 if own else part) :][:, :part], values[:, model + (0 if own else part) :][:, :part]]
            for at in (2 * model, 2 * model + size):
                low, high = values[:, at : at + small], values[:, at + small : at + size]
                pieces.append(jnp.where((fs == 0) == own, low, high))
            row = jnp.concatenate(pieces, 1)
            row = jnp.pad(row, ((0, 0), (0, gain_rows * gain_width - row.shape[1])))
            return row.reshape(gain_rows, gain_width).astype(bf16)

        return [one(True), one(False)]

    sums_of, parts_of = {}, {}

    def make(name):
        if name == "gate_up":
            parts_of[name] = weight("gate_up_grad", normed_two, [grad_gate, grad_up], rows_split)
        elif name == "down":
            parts_of[name] = weight(
                "down_grad", active, [[low_grad[s] for s in range(seqs)]], cols_split, height=hidden + q_width
            )
        elif name == "out":
            parts_of[name] = weight(
                "out_grad", mixed, [grad_branch], cols_split, True,
                at=hidden // 256, height=hidden + q_width, into=parts_of["down"],
            )
        elif name == "query":
            parts_of[name] = weight("query_grad", normed, [grad_query], rows_split)
        else:
            parts_of[name] = weight(
                "kv_grad", normed, [grad_kv], rows_split, height=model // 2 + gain_rows, tail=gain_parts(sums_of["gains"].value) if paired else None,
            )

    def send(*names):
        axis = 1 if names[0] in ("down", "out") else 0
        if paired:
            sums_of[names[0]] = Steps(reduced(parts_of[names[-1]], axis))
        else:
            steps = [reduced(parts_of[n], axis) for n in names]
            sums_of[names[0]] = Steps(zip(*steps))

    down_out = keys(0, down_out)
    if paired:
        down_w = out_w = gather(down_out[0], 1)
    else:
        down_w, out_w = gather(w_down, 1), gather(w_out, 1)
    line.wait(query_w[-1])
    spread(0)
    keys(1)
    spread(1)
    forward(0)
    query(0)
    query(1)
    attend_own(0)
    attend_own(1)
    forward(1)
    attend(0)
    line.wait(gate_w[-1], up_w[-1])
    branch[0]()
    attend(1)
    branch[0]()
    branch[1]()
    ffn(0)
    branch[1]()
    grad_two[0]()
    ffn(1)
    grad_two[0]()
    grad_two[1]()
    attend_back(0)
    came[0]()
    make("gate_up")
    send("gate_up")
    grad_two[1]()
    down(0)
    came[0]()
    attend_back(1)
    line.wait(came[0].value)
    came[1]()
    make("down")
    make("out")
    send("down", "out")
    make("query")
    send("query")
    came[1]()
    down(1)
    input_back(0)
    sums_of["gate_up"]()
    input_back(1)
    sums_of["down"]()
    sums_of["query"]()
    sums_of["gains"] = Steps(gain_sum())
    sums_of["gains"]()
    sums_of["gains"]()
    make("kv")
    send("kv")
    grad_one[0]()
    sums_of["gate_up"]()
    layers[0]()
    sums_of["kv"]()
    sums_of["down"]()
    sums_of["query"]()
    grad_one[0]()
    sums_of["gate_up"]()
    input_output(0)
    sums_of["kv"]()
    layers[0]()
    input_output(1)
    sums_of["down"]()
    layer_output(0)
    sums_of["query"]()
    sums_of["kv"]()
    layer_output(1)
    gate_up, down_and_out, query_sum, kv_total = (sums_of[name]() for name in ("gate_up", "down", "query", "kv"))
    if paired:
        gate_sum, up_sum = gate_up[:, :hidden], gate_up[:, hidden:]
        down_sum, out_sum = down_and_out[:hidden], down_and_out[hidden:]
        kv_total, gain_total = kv_total[: model // 2], kv_total[model // 2 :]
    else:
        gate_sum, up_sum = gate_up[0][:, :hidden], gate_up[0][:, hidden:]
        (down_sum, out_sum), (query_sum,), (kv_total,) = down_and_out, query_sum, kv_total
    if paired:
        mine_all = gain_total.reshape(1, -1)[0].astype(f32)
        gain_out = []
        at = 0
        for width in (part, part, small, small):
            gain_out.append(mine_all[at : at + width])
            at += width
    else:
        values = sums_of["gains"].value
        for axis, count in (("fsdp", n_fs), ("ctx", n_ctx)):
            values = sum_small(values, axis, count)
        gain_out = []
        for at, width in ((0, model), (model, model), (2 * model, size), (2 * model + size, size)):
            gain_out.append(lax.dynamic_slice_in_dim(values[0], at + fs * (width // n_fs), width // n_fs, 0))
    attn_out, ffn_out, query_out, key_out = gain_out

    return (
        finished["layer_out"],
        finished["input_grad"],
        attn_out,
        query_sum.astype(f32),
        kv_total[:, :kv_width].astype(f32),
        kv_total[:, kv_width:].astype(f32),
        query_out,
        key_out,
        out_sum.astype(f32),
        ffn_out,
        gate_sum.astype(f32),
        up_sum.astype(f32),
        down_sum.astype(f32),
    )


def solution(mesh):
    n_fs, n_ctx, n_tp = mesh.shape["fsdp"], mesh.shape["ctx"], mesh.shape["tp"]
    placed = (
        P("fsdp", "ctx", None),
        P("fsdp", None),
        P("fsdp"),
        P("fsdp", "tp"),
        P("fsdp", "tp"),
        P("fsdp", "tp"),
        P("fsdp"),
        P("fsdp"),
        P("tp", "fsdp"),
        P("fsdp"),
        P("fsdp", "tp"),
        P("fsdp", "tp"),
        P("tp", "fsdp"),
        P("fsdp", "ctx", None),
    )
    return jax.shard_map(
        functools.partial(body, n_fs, n_ctx, n_tp),
        mesh=mesh,
        in_specs=placed,
        out_specs=(
            P("fsdp", "ctx", None),
            P("fsdp", "ctx", None),
            P("fsdp"),
            P("fsdp", "tp"),
            P("fsdp", "tp"),
            P("fsdp", "tp"),
            P("fsdp"),
            P("fsdp"),
            P("tp", "fsdp"),
            P("fsdp"),
            P("fsdp", "tp"),
            P("fsdp", "tp"),
            P("tp", "fsdp"),
        ),
        check_vma=False,
    )
```

profile of v0, /device:TPU:0, one launch (start us, length us, event | category | flops | bytes accessed | tf_op | source)
XLA Modules:
  0.0 447.6 jit_solution(9718834142294132353)
XLA Ops:
  2.7 3.0 collective-permute-start.1
  12.6 2.2 pad_maximum_fusion.refs_7_
  20.8 4.6 %keys.2 = (bf16[512,1024]{1,0:T(8,128)(2,1)}, bf16[512,512]{1,0:T(8,128)(2,1)}, f32[512,256]{1,0:T(8,128)}, bf16[1280,512]{1,0:T(8,128)(2,1)}) custom-call(s32[4]{0:T(128)} %pad_add_fusion.2.ids, bf16[2,512,1024]{2,1,0:T(8,128)(2,1)} %refs_0_.11, f32[1,1024]{1,0:T(1,128)} %get-tuple-element.676.refs_1_.refs_2_.refs_4_, ...), custom_call_target="tpu_custom_call", output_to_operand_aliasing={{3}: (8, {})} | custom-call | flops 1 | bytes 1 | tf_op jit(solution)/shard_map/keys/pallas_call | solution.py:65
  27.2 2.6 collective-permute-done.2.refs_0_.refs_5_.refs_10_
  29.8 4.8 %collective-permute-start.8 = (bf16[512,512]{1,0:T(8,128)(2,1)}, bf16[512,512]{1,0:T(8,128)(2,1)}, u32[]{:S(2)}, u32[]{:S(2)}) collective-permute-start(bf16[512,512]{1,0:T(8,128)(2,1)} %get-tuple-element.495.refs_2_.refs_18_), channel_id=1, source_target_pairs={{0,4},{4,8},{8,12},{1,5},{5,9},{9,13},{2,6},{6,10},{10,14},{3,7},{... | collective-permute-start | bytes 1572872 | tf_op jit(solution)/shard_map/ppermute | solution.py:735
  37.2 4.6 %keys.3 = (bf16[512,1024]{1,0:T(8,128)(2,1)}, bf16[512,512]{1,0:T(8,128)(2,1)}, f32[512,256]{1,0:T(8,128)}) custom-call(s32[4]{0:T(128)} %pad_add_fusion.ids, bf16[512,512]{1,0:T(8,128)(2,1)} %copy-done.3, bf16[2,512,1024]{2,1,0:T(8,128)(2,1)} %refs_0_.11, f32[1,1024]{1,0:T(1,128)} %get-tuple-element.676.refs_1_.refs_2_.refs_4_, ...), custom_call_target="tpu_custom_call" | custom-call | flops 1 | bytes 1 | tf_op jit(solution)/shard_map/keys/pallas_call | solution.py:65
  43.3 4.4 collective-permute-start.9
  48.9 4.2 collective-permute-start.3
  53.1 4.4 query.2
  57.5 4.4 query.3
  61.9 5.9 %attend_own.2 = (f32[512,512]{1,0:T(8,128)}, f32[8,512]{1,0:T(8,128)}) custom-call(s32[4]{0:T(128)} %pad_add_fusion.2.ids, bf16[512,512]{1,0:T(8,128)(2,1)} %get-tuple-element.487.refs_0_.refs_10_, s32[2,1,512]{2,1,0:T(1,128)} %broadcast_in_dim.36.refs_1_.refs_3_.refs_11_, bf16[512,512]{1,0:T(8,128)(2,1)} %get-tuple-element.495.refs_2_.refs_18_), custom_call_target="tpu_custom_call" | custom-call | flops 1 | bytes 1 | tf_op jit(solution)/shard_map/attend_own/pallas_call | solution.py:65
  67.8 6.0 %attend_own.3 = (f32[512,512]{1,0:T(8,128)}, f32[8,512]{1,0:T(8,128)}) custom-call(s32[4]{0:T(128)} %pad_add_fusion.ids, bf16[512,512]{1,0:T(8,128)(2,1)} %get-tuple-element.531.refs_0_.refs_2_.refs_10_, s32[2,1,512]{2,1,0:T(1,128)} %broadcast_in_dim.36.refs_1_.refs_3_.refs_11_, bf16[512,512]{1,0:T(8,128)(2,1)} %get-tuple-element.539.refs_2_.refs_18_), custom_call_target="tpu_custom_call" | custom-call | flops 1 | bytes 1 | tf_op jit(solution)/shard_map/attend_own/pallas_call | solution.py:65
  75.1 5.6 %attend.2 = (bf16[256,1024]{1,0:T(8,128)(2,1)}, bf16[256,1024]{1,0:T(8,128)(2,1)}, bf16[512,512]{1,0:T(8,128)(2,1)}, f32[8,512]{1,0:T(8,128)}) custom-call(s32[4]{0:T(128)} %pad_add_fusion.2.ids, bf16[512,512]{1,0:T(8,128)(2,1)} %get-tuple-element.487.refs_0_.refs_10_, s32[2,1,512]{2,1,0:T(1,128)} %broadcast_in_dim.36.refs_1_.refs_3_.refs_11_, ...), custom_call_target="tpu_custom_call" | custom-call | flops 1 | bytes 1 | tf_op jit(solution)/shard_map/attend/pallas_call | solution.py:65
  80.7 10.0 %collective-permute-done.7.refs_1_.refs_9_ = bf16[512,768]{1,0:T(8,128)(2,1)S(1)} collective-permute-done((bf16[512,768]{1,0:T(8,128)(2,1)}, bf16[512,768]{1,0:T(8,128)(2,1)S(1)}, u32[]{:S(2)}, u32[]{:S(2)}) %collective-permute-start.7) | collective-permute-done | bytes 786464 | tf_op jit(solution)/shard_map/ppermute | solution.py:500
  90.8 4.0 collective-permute-start.4
  97.6 9.1 %collective-permute-done.4.refs_6_.refs_16_ = bf16[512,512]{1,0:T(8,128)(2,1)S(1)} collective-permute-done((bf16[512,512]{1,0:T(8,128)(2,1)}, bf16[512,512]{1,0:T(8,128)(2,1)S(1)}, u32[]{:S(2)}, u32[]{:S(2)}) %collective-permute-start.4) | collective-permute-done | bytes 524320 | tf_op jit(solution)/shard_map/ppermute | solution.py:740
  107.4 5.7 %attend.3 = (bf16[256,1024]{1,0:T(8,128)(2,1)}, bf16[256,1024]{1,0:T(8,128)(2,1)}, bf16[512,512]{1,0:T(8,128)(2,1)}, f32[8,512]{1,0:T(8,128)}) custom-call(s32[4]{0:T(128)} %pad_add_fusion.ids, bf16[512,768]{1,0:T(8,128)(2,1)} %copy-done.10, bf16[512,768]{1,0:T(8,128)(2,1)} %copy-done.11, bf16[512,512]{1,0:T(8,128)(2,1)} %get-tuple-element.531.refs_0_.refs_2_.refs_10_, ...), custom_call_target="tpu_custom_call" | custom-call | flops 1 | bytes 1 | tf_op jit(solution)/shard_map/attend/pallas_call | solution.py:65
  120.8 12.5 %ffn.2 = (bf16[512,1024]{1,0:T(8,128)(2,1)}, bf16[512,768]{1,0:T(8,128)(2,1)}, bf16[512,768]{1,0:T(8,128)(2,1)}, bf16[512,768]{1,0:T(8,128)(2,1)}, bf16[256,1024...) custom-call(s32[4]{0:T(128)} %pad_add_fusion.2.ids, bf16[2,512,1024]{2,1,0:T(8,128)(2,1)} %refs_0_.11, ...), custom_call_target="tpu_custom_call" | custom-call | flops 1 | bytes 1 | tf_op jit(solution)/shard_map/ffn/pallas_call | solution.py:65
  137.9 12.5 %ffn.3 = (bf16[512,1024]{1,0:T(8,128)(2,1)}, bf16[512,768]{1,0:T(8,128)(2,1)}, bf16[512,768]{1,0:T(8,128)(2,1)}, bf16[512,768]{1,0:T(8,128)(2,1)}, bf16[256,1024...) custom-call(s32[4]{0:T(128)} %pad_add_fusion.ids, bf16[2,512,1024]{2,1,0:T(8,128)(2,1)} %refs_0_.11, ...), custom_call_target="tpu_custom_call" | custom-call | flops 1 | bytes 1 | tf_op jit(solution)/shard_map/ffn/pallas_call | solution.py:65
  155.9 15.1 %attend_back.2 = (f32[512,1024]{1,0:T(8,128)}, bf16[512,1024]{1,0:T(8,128)(2,1)}, bf16[512,512]{1,0:T(8,128)(2,1)}, f32[1,128]{1,0:T(1,128)}, bf16[512,512]{1,0:...) custom-call(s32[4]{0:T(128)} %pad_add_fusion.2.ids, bf16[2,512,1024]{2,1,0:T(8,128)(2,1)} %refs_0_.11, ...), custom_call_target="tpu_custom_call" | custom-call | flops 1 | bytes 1 | tf_op jit(solution)/shard_map/attend_back/pallas_call | solution.py:65
  172.4 8.3 %gate_up_grad.1 = (bf16[512,1536]{1,0:T(8,128)(2,1)}, bf16[512,1536]{1,0:T(8,128)(2,1)}) custom-call(s32[4]{0:T(128)} %pad_add_fusion.2.ids, bf16[512,1024]{1,0:T(8,128)(2,1)} %get-tuple-element.499.refs_0_, bf16[512,1024]{1,0:T(8,128)(2,1)} %get-tuple-element.500.refs_1_, bf16[512,768]{1,0:T(8,128)(2,1)} %get-tuple-element.501.refs_2_, ...), custom_call_target="tpu_custom_call" | custom-call | flops 1 | bytes 1 | tf_op jit(solution)/shard_map/gate_up_grad/pallas_call | solution.py:65
  181.0 4.9 %down.2 = (bf16[512,1024]{1,0:T(8,128)(2,1)}, bf16[512,1024]{1,0:T(8,128)(2,1)}) custom-call(s32[4]{0:T(128)} %pad_add_fusion.2.ids, bf16[512,768]{1,0:T(8,128)(2,1)} %get-tuple-element.551.refs_0_.refs_1_, bf16[1280,512]{1,0:T(8,128)(2,1)} %get-tuple-element.572.refs_6_.refs_8_.refs_10_.refs_19_.refs_1_, bf16[1280,512]{1,0:T(8,128)(2,1)} %copy-done), custom_call_target="tpu_custom_call" | custom-call | flops 1 | bytes 1 | tf_op jit(solution)/shard_map/down/pallas_call | solution.py:65
  185.9 10.7 %collective-permute-done.22 = bf16[512,512]{1,0:T(8,128)(2,1)S(1)} collective-permute-done((bf16[512,512]{1,0:T(8,128)(2,1)}, bf16[512,512]{1,0:T(8,128)(2,1)S(1)}, u32[]{:S(2)}, u32[]{:S(2)}) %collective-permute-start.22) | collective-permute-done | bytes 524320 | tf_op jit(solution)/shard_map/ppermute | solution.py:859
  199.8 15.0 %attend_back.3 = (f32[512,1024]{1,0:T(8,128)}, bf16[512,1024]{1,0:T(8,128)(2,1)}, bf16[512,512]{1,0:T(8,128)(2,1)}, f32[1,128]{1,0:T(1,128)}, bf16[512,512]{1,0:...) custom-call(s32[4]{0:T(128)} %pad_add_fusion.ids, bf16[2,512,1024]{2,1,0:T(8,128)(2,1)} %refs_0_.11, ...), custom_call_target="tpu_custom_call" | custom-call | flops 1 | bytes 1 | tf_op jit(solution)/shard_map/attend_back/pallas_call | solution.py:65
  217.6 5.7 %down_grad.1 = (bf16[1280,512]{1,0:T(8,128)(2,1)}, bf16[1280,512]{1,0:T(8,128)(2,1)}) custom-call(s32[4]{0:T(128)} %pad_add_fusion.2.ids, bf16[512,512]{1,0:T(8,128)(2,1)} %copy-done.19, bf16[512,768]{1,0:T(8,128)(2,1)} %get-tuple-element.551.refs_0_.refs_1_, bf16[512,768]{1,0:T(8,128)(2,1)} %get-tuple-element.571.refs_2_.refs_0_, ...), custom_call_target="tpu_custom_call" | custom-call | flops 1 | bytes 1 | tf_op jit(solution)/shard_map/down_grad/pallas_call | solution.py:65
  223.3 4.6 %out_grad.1 = (bf16[1280,512]{1,0:T(8,128)(2,1)}, bf16[1280,512]{1,0:T(8,128)(2,1)}) custom-call(s32[4]{0:T(128)} %pad_add_fusion.2.ids, bf16[512,512]{1,0:T(8,128)(2,1)} %get-tuple-element.557.refs_8_.refs_0_, bf16[512,512]{1,0:T(8,128)(2,1)} %get-tuple-element.558.refs_8_.refs_1_, ...), custom_call_target="tpu_custom_call", output_to_operand_aliasing={{0}: (5, {}), {1}: (6, {})} | custom-call | flops 1 | bytes 1 | tf_op jit(solution)/shard_map/out_grad/pallas_call | solution.py:65
  229.8 5.7 %query_grad.1 = (bf16[512,512]{1,0:T(8,128)(2,1)}, bf16[512,512]{1,0:T(8,128)(2,1)}) custom-call(s32[4]{0:T(128)} %pad_add_fusion.2.ids, bf16[512,1024]{1,0:T(8,128)(2,1)} %get-tuple-element.637.refs_0_, bf16[512,1024]{1,0:T(8,128)(2,1)} %get-tuple-element.638.refs_0_.refs_1_, bf16[512,512]{1,0:T(8,128)(2,1)} %get-tuple-element.583.refs_2_, ...), custom_call_target="tpu_custom_call" | custom-call | flops 1 | bytes 1 | tf_op jit(solution)/shard_map/query_grad/pallas_call | solution.py:65
  238.8 4.7 %down.3 = (bf16[512,1024]{1,0:T(8,128)(2,1)}, bf16[512,1024]{1,0:T(8,128)(2,1)}) custom-call(s32[4]{0:T(128)} %pad_add_fusion.ids, bf16[512,768]{1,0:T(8,128)(2,1)} %get-tuple-element.571.refs_2_.refs_0_, bf16[1280,512]{1,0:T(8,128)(2,1)} %get-tuple-element.572.refs_6_.refs_8_.refs_10_.refs_19_.refs_1_, ...), custom_call_target="tpu_custom_call", output_to_operand_aliasing={{0}: (4, {}), {1}: (5, {})} | custom-call | flops 1 | bytes 1 | tf_op jit(solution)/shard_map/down/pallas_call | solution.py:65
  243.6 7.2 %input_back.2 = (bf16[512,512]{1,0:T(8,128)(2,1)}, bf16[512,1024]{1,0:T(8,128)(2,1)}, bf16[512,1024]{1,0:T(8,128)(2,1)}, f32[1,128]{1,0:T(1,128)}, f32[1,1024]{1,0:T(1,128)}) custom-call(s32[4]{0:T(128)} %pad_add_fusion.2.ids, bf16[2,512,1024]{2,1,0:T(8,128)(2,1)} %refs_0_.11, f32[1,1024]{1,0:T(1,128)} %get-tuple-element.676.refs_1_.refs_2_.refs_4_, ...), custom_call_target="tpu_custom_call" | custom-call | flops 1 | bytes 1 | tf_op jit(solution)/shard_map/input_back/pallas_call | solution.py:65
  252.6 11.1 %collective-permute-start.26 = (bf16[512,1536]{1,0:T(8,128)(2,1)S(1)}, bf16[512,1536]{1,0:T(8,128)(2,1)}, u32[]{:S(2)}, u32[]{:S(2)}) collective-permute-start(bf16[512,1536]{1,0:T(8,128)(2,1)S(1)} %add.133), channel_id=1, source_target_pairs={{0,4},{12,8},{1,5},{13,9},{2,6},{14,10},{3,7},{15,11},{16,20},{28,... | collective-permute-start | bytes 4718600 | tf_op jit(solution)/shard_map/ppermute | solution.py:556
  263.7 7.2 %input_back.3 = (bf16[512,512]{1,0:T(8,128)(2,1)}, bf16[512,1024]{1,0:T(8,128)(2,1)}, bf16[512,1024]{1,0:T(8,128)(2,1)}, f32[1,128]{1,0:T(1,128)}, f32[1,1024]{1,0:T(1,128)}) custom-call(s32[4]{0:T(128)} %pad_add_fusion.ids, bf16[2,512,1024]{2,1,0:T(8,128)(2,1)} %refs_0_.11, ...), custom_call_target="tpu_custom_call", output_to_operand_aliasing={{1}: (14, {}), {2}: (15, {})} | custom-call | flops 1 | bytes 1 | tf_op jit(solution)/shard_map/input_back/pallas_call | solution.py:65
  277.3 2.9 collective-permute-done.31
  281.9 5.6 %kv_grad.1 = (bf16[528,512]{1,0:T(8,128)(2,1)}, bf16[528,512]{1,0:T(8,128)(2,1)}) custom-call(s32[4]{0:T(128)} %pad_add_fusion.2.ids, bf16[512,1024]{1,0:T(8,128)(2,1)} %get-tuple-element.637.refs_0_, bf16[512,1024]{1,0:T(8,128)(2,1)} %get-tuple-element.638.refs_0_.refs_1_, bf16[512,512]{1,0:T(8,128)(2,1)} %get-tuple-element.639.refs_2_, ...), custom_call_target="tpu_custom_call" | custom-call | flops 1 | bytes 1 | tf_op jit(solution)/shard_map/kv_grad/pallas_call | solution.py:65
  287.5 2.9 collective-permute-done.32
  292.0 3.6 collective-permute-done.26
  297.5 4.6 %collective-permute-start.39 = (bf16[1280,512]{1,0:T(8,128)(2,1)S(1)}, bf16[1280,512]{1,0:T(8,128)(2,1)S(1)}, u32[]{:S(2)}, u32[]{:S(2)}) collective-permute-start(bf16[1280,512]{1,0:T(8,128)(2,1)S(1)} %add.138), channel_id=1, source_target_pairs={{0,4},{12,8},{1,5},{13,9},{2,6},{14,10},{3,7},{15,11},{16,20},{28,... | collective-permute-start | bytes 3932168 | tf_op jit(solution)/shard_map/ppermute | solution.py:556
  303.8 6.6 %collective-permute-start.38 = (bf16[512,512]{1,0:T(8,128)(2,1)}, bf16[512,512]{1,0:T(8,128)(2,1)S(1)}, u32[]{:S(2)}, u32[]{:S(2)}) collective-permute-start(bf16[512,512]{1,0:T(8,128)(2,1)} %add.139), channel_id=1, source_target_pairs={{0,4},{12,8},{1,5},{13,9},{2,6},{14,10},{3,7},{15,11},{16,20},{28,... | collective-permute-start | bytes 1572872 | tf_op jit(solution)/shard_map/ppermute | solution.py:556
  310.8 6.8 %collective-permute-done.35 = bf16[528,512]{1,0:T(8,128)(2,1)S(1)} collective-permute-done((bf16[528,512]{1,0:T(8,128)(2,1)S(1)}, bf16[528,512]{1,0:T(8,128)(2,1)S(1)}, u32[]{:S(2)}, u32[]{:S(2)}) %collective-permute-start.35) | collective-permute-done | bytes 540704 | tf_op jit(solution)/shard_map/ppermute | solution.py:500
  317.7 13.4 %collective-permute-done.39 = bf16[1280,512]{1,0:T(8,128)(2,1)S(1)} collective-permute-done((bf16[1280,512]{1,0:T(8,128)(2,1)S(1)}, bf16[1280,512]{1,0:T(8,128)(2,1)S(1)}, u32[]{:S(2)}, u32[]{:S(2)}) %collective-permute-start.39) | collective-permute-done | bytes 1310752 | tf_op jit(solution)/shard_map/ppermute | solution.py:556
  332.6 9.4 %collective-permute-done.38 = bf16[512,512]{1,0:T(8,128)(2,1)S(1)} collective-permute-done((bf16[512,512]{1,0:T(8,128)(2,1)}, bf16[512,512]{1,0:T(8,128)(2,1)S(1)}, u32[]{:S(2)}, u32[]{:S(2)}) %collective-permute-start.38) | collective-permute-done | bytes 524320 | tf_op jit(solution)/shard_map/ppermute | solution.py:556
  345.0 4.3 collective-permute-start.36
  355.0 4.5 %input_grad.2.refs_5_ = f32[2,512,1024]{2,1,0:T(8,128)} custom-call(s32[4]{0:T(128)} %pad_add_fusion.2.ids, bf16[2,512,1024]{2,1,0:T(8,128)(2,1)} %refs_0_.11, f32[512,1024]{1,0:T(8,128)} %get-tuple-element.664.refs_1_, bf16[512,1024]{1,0:T(8,128)(2,1)} %copy-done.6, bf16[512,1024]{1,0:T(8,128)(2,1)} %copy-done.15, ...), custom_call_target="tpu_custom_call" | custom-call | flops 1 | bytes 1 | tf_op jit(solution)/shard_map/input_grad/pallas_call | solution.py:65
  362.1 8.1 %collective-permute-done.34 = bf16[512,1024]{1,0:T(8,128)(2,1)} collective-permute-done((bf16[512,1024]{1,0:T(8,128)(2,1)S(1)}, bf16[512,1024]{1,0:T(8,128)(2,1)}, u32[]{:S(2)}, u32[]{:S(2)}) %collective-permute-start.34) | collective-permute-done | bytes 1048608 | tf_op jit(solution)/shard_map/ppermute | solution.py:500
  374.8 4.5 %input_grad.3 = f32[2,512,1024]{2,1,0:T(8,128)} custom-call(s32[4]{0:T(128)} %pad_add_fusion.ids, bf16[2,512,1024]{2,1,0:T(8,128)(2,1)} %refs_0_.11, f32[512,1024]{1,0:T(8,128)} %get-tuple-element.673.refs_1_, bf16[512,1024]{1,0:T(8,128)(2,1)} %copy-done.6, bf16[512,1024]{1,0:T(8,128)(2,1)} %copy-done.15, ...), custom_call_target="tpu_custom_call", output_to_operand_aliasing={{}: (6, {})} | custom-call | flops 1 | bytes 1 | tf_op jit(solution)/shard_map/input_grad/pallas_call | solution.py:65
  383.9 4.1 layer_out.2.refs_6_
  393.3 4.1 layer_out.3
  400.9 35.4 %collective-permute-done.47 = bf16[512,512]{1,0:T(8,128)(2,1)S(1)} collective-permute-done((bf16[512,512]{1,0:T(8,128)(2,1)S(1)}, bf16[512,512]{1,0:T(8,128)(2,1)S(1)}, u32[]{:S(2)}, u32[]{:S(2)}) %collective-permute-start.47) | collective-permute-done | bytes 524320 | tf_op jit(solution)/shard_map/ppermute | solution.py:562
  441.2 3.8 collective-permute-done.46
  (250 shorter events, 110.6 us)
Async XLA Ops:
  2.7 17.3 %collective-permute-start.1 = (bf16[512,512]{1,0:T(8,128)(2,1)S(1)}, bf16[512,512]{1,0:T(8,128)(2,1)S(1)}, u32[]{:S(2)}, u32[]{:S(2)}) collective-permute-start(bf16[512,512]{1,0:T(8,128)(2,1)S(1)} %constant_dynamic-update-slice_fusion.refs_5_.refs_6_.refs_11_), channel_id=1, source_target_pairs={{0,16},{16,0},{1,17},{17,1},{2,18},{18,2},{3,19},{19,3},{4,20},{20... | collective-permute-start | bytes 1572872 | tf_op jit(solution)/shard_map/ppermute | solution.py:500
  7.9 10.8 %collective-permute-start = (bf16[3,512]{1,0:T(4,128)(2,1)S(1)}, bf16[3,512]{1,0:T(4,128)(2,1)S(1)}, u32[]{:S(2)}, u32[]{:S(2)}) collective-permute-start(bf16[3,512]{1,0:T(4,128)(2,1)S(1)} %pad_maximum_fusion.5), channel_id=1, source_target_pairs={{0,16},{16,0},{1,17},{17,1},{2,18},{18,2},{3,19},{19,3},{4,20},{20... | collective-permute-start | bytes 9224 | tf_op jit(solution)/shard_map/ppermute | solution.py:500
  8.0 21.8 %collective-permute-start.2 = (bf16[512,512]{1,0:T(8,128)(2,1)}, bf16[512,512]{1,0:T(8,128)(2,1)S(1)}, u32[]{:S(2)}, u32[]{:S(2)}) collective-permute-start(bf16[512,512]{1,0:T(8,128)(2,1)} %refs_9_.1), channel_id=1, source_target_pairs={{0,16},{16,0},{1,17},{17,1},{2,18},{18,2},{3,19},{19,3},{4,20},{20... | collective-permute-start | bytes 1572872 | tf_op jit(solution)/shard_map/ppermute | solution.py:500
  25.3 48.5 %collective-permute-start.5 = (bf16[1280,512]{1,0:T(8,128)(2,1)}, bf16[1280,512]{1,0:T(8,128)(2,1)S(1)}, u32[]{:S(2)}, u32[]{:S(2)}) collective-permute-start(bf16[1280,512]{1,0:T(8,128)(2,1)} %get-tuple-element.572.refs_6_.refs_8_.refs_10_.refs_19_.refs_1_), channel_id=1, source_target_pairs={{0,16},{16,0},{1,17},{17,1},{2,18},{18,2},{3,19},{19,3},{4,20},{20... | collective-permute-start | bytes 3932168 | tf_op jit(solution)/shard_map/ppermute | solution.py:500
  29.8 13.5 %collective-permute-start.8 = (bf16[512,512]{1,0:T(8,128)(2,1)}, bf16[512,512]{1,0:T(8,128)(2,1)}, u32[]{:S(2)}, u32[]{:S(2)}) collective-permute-start(bf16[512,512]{1,0:T(8,128)(2,1)} %get-tuple-element.495.refs_2_.refs_18_), channel_id=1, source_target_pairs={{0,4},{4,8},{8,12},{1,5},{5,9},{9,13},{2,6},{6,10},{10,14},{3,7},{... | collective-permute-start | bytes 1572872 | tf_op jit(solution)/shard_map/ppermute | solution.py:735
  34.6 46.1 %collective-permute-start.6 = (bf16[512,768]{1,0:T(8,128)(2,1)}, bf16[512,768]{1,0:T(8,128)(2,1)S(1)}, u32[]{:S(2)}, u32[]{:S(2)}) collective-permute-start(bf16[512,768]{1,0:T(8,128)(2,1)} %refs_6_.1), channel_id=1, source_target_pairs={{0,16},{16,0},{1,17},{17,1},{2,18},{18,2},{3,19},{19,3},{4,20},{20... | collective-permute-start | bytes 2359304 | tf_op jit(solution)/shard_map/ppermute | solution.py:500
  36.1 54.6 %collective-permute-start.7 = (bf16[512,768]{1,0:T(8,128)(2,1)}, bf16[512,768]{1,0:T(8,128)(2,1)S(1)}, u32[]{:S(2)}, u32[]{:S(2)}) collective-permute-start(bf16[512,768]{1,0:T(8,128)(2,1)} %refs_8_.1), channel_id=1, source_target_pairs={{0,16},{16,0},{1,17},{17,1},{2,18},{18,2},{3,19},{19,3},{4,20},{20... | collective-permute-start | bytes 2359304 | tf_op jit(solution)/shard_map/ppermute | solution.py:500
  43.3 30.5 %collective-permute-start.9 = (bf16[512,512]{1,0:T(8,128)(2,1)}, bf16[512,512]{1,0:T(8,128)(2,1)S(1)}, u32[]{:S(2)}, u32[]{:S(2)}) collective-permute-start(bf16[512,512]{1,0:T(8,128)(2,1)} %collective-permute-done.8.refs_5_.refs_17_), channel_id=1, source_target_pairs={{0,4},{4,8},{8,12},{1,5},{5,9},{9,13},{2,6},{6,10},{10,14},{3,7},{... | collective-permute-start | bytes 1572872 | tf_op jit(solution)/shard_map/ppermute | solution.py:740
  48.9 41.9 %collective-permute-start.3 = (bf16[512,512]{1,0:T(8,128)(2,1)}, bf16[512,512]{1,0:T(8,128)(2,1)}, u32[]{:S(2)}, u32[]{:S(2)}) collective-permute-start(bf16[512,512]{1,0:T(8,128)(2,1)} %get-tuple-element.539.refs_2_.refs_18_), channel_id=1, source_target_pairs={{0,4},{4,8},{8,12},{1,5},{5,9},{9,13},{2,6},{6,10},{10,14},{3,7},{... | collective-permute-start | bytes 1572872 | tf_op jit(solution)/shard_map/ppermute | solution.py:735
  90.8 4.0 collective-permute-start.10
  90.8 15.9 %collective-permute-start.4 = (bf16[512,512]{1,0:T(8,128)(2,1)}, bf16[512,512]{1,0:T(8,128)(2,1)S(1)}, u32[]{:S(2)}, u32[]{:S(2)}) collective-permute-start(bf16[512,512]{1,0:T(8,128)(2,1)} %collective-permute-done.3.refs_7_.refs_17_), channel_id=1, source_target_pairs={{0,4},{4,8},{8,12},{1,5},{5,9},{9,13},{2,6},{6,10},{10,14},{3,7},{... | collective-permute-start | bytes 1572872 | tf_op jit(solution)/shard_map/ppermute | solution.py:740
  96.0 17.1 %collective-permute-start.11 = (bf16[256,1024]{1,0:T(8,128)(2,1)S(1)}, bf16[256,1024]{1,0:T(8,128)(2,1)S(1)}, u32[]{:S(2)}, u32[]{:S(2)}) collective-permute-start(bf16[256,1024]{1,0:T(8,128)(2,1)S(1)} %add.123), channel_id=1, source_target_pairs={{0,2},{1,3},{2,0},{3,1},{4,6},{5,7},{6,4},{7,5},{8,10},{9,11},{10,... | collective-permute-start | bytes 1572872 | tf_op jit(solution)/shard_map/ppermute | solution.py:500
  114.2 5.6 %collective-permute-start.14 = (bf16[256,1024]{1,0:T(8,128)(2,1)S(1)}, bf16[256,1024]{1,0:T(8,128)(2,1)S(1)}, u32[]{:S(2)}, u32[]{:S(2)}) collective-permute-start(bf16[256,1024]{1,0:T(8,128)(2,1)S(1)} %add.124.refs_1_), channel_id=1, source_target_pairs={{0,1},{1,0},{2,3},{3,2},{4,5},{5,4},{6,7},{7,6},{8,9},{9,8},{10,11... | collective-permute-start | bytes 1572872 | tf_op jit(solution)/shard_map/ppermute | solution.py:500
  116.3 17.1 %collective-permute-start.13 = (bf16[256,1024]{1,0:T(8,128)(2,1)S(1)}, bf16[256,1024]{1,0:T(8,128)(2,1)S(1)}, u32[]{:S(2)}, u32[]{:S(2)}) collective-permute-start(bf16[256,1024]{1,0:T(8,128)(2,1)S(1)} %add.125), channel_id=1, source_target_pairs={{0,2},{1,3},{2,0},{3,1},{4,6},{5,7},{6,4},{7,5},{8,10},{9,11},{10,... | collective-permute-start | bytes 1572872 | tf_op jit(solution)/shard_map/ppermute | solution.py:500
  134.4 1.9 collective-permute-start.16
  134.4 2.7 collective-permute-start.15
  136.5 14.0 %collective-permute-start.17 = (bf16[256,1024]{1,0:T(8,128)(2,1)S(1)}, bf16[256,1024]{1,0:T(8,128)(2,1)S(1)}, u32[]{:S(2)}, u32[]{:S(2)}) collective-permute-start(bf16[256,1024]{1,0:T(8,128)(2,1)S(1)} %add.127), channel_id=1, source_target_pairs={{0,2},{1,3},{2,0},{3,1},{4,6},{5,7},{6,4},{7,5},{8,10},{9,11},{10,... | collective-permute-start | bytes 1572872 | tf_op jit(solution)/shard_map/ppermute | solution.py:500
  151.6 3.6 collective-permute-start.20
  153.6 27.1 %collective-permute-start.19 = (bf16[256,1024]{1,0:T(8,128)(2,1)S(1)}, bf16[256,1024]{1,0:T(8,128)(2,1)S(1)}, u32[]{:S(2)}, u32[]{:S(2)}) collective-permute-start(bf16[256,1024]{1,0:T(8,128)(2,1)S(1)} %add.129), channel_id=1, source_target_pairs={{0,2},{1,3},{2,0},{3,1},{4,6},{5,7},{6,4},{7,5},{8,10},{9,11},{10,... | collective-permute-start | bytes 1572872 | tf_op jit(solution)/shard_map/ppermute | solution.py:500
  171.1 25.5 %collective-permute-start.22 = (bf16[512,512]{1,0:T(8,128)(2,1)}, bf16[512,512]{1,0:T(8,128)(2,1)S(1)}, u32[]{:S(2)}, u32[]{:S(2)}) collective-permute-start(bf16[512,512]{1,0:T(8,128)(2,1)} %get-tuple-element.518), channel_id=1, source_target_pairs={{4,0},{8,4},{12,8},{5,1},{9,5},{13,9},{6,2},{10,6},{14,10},{7,3},{... | collective-permute-start | bytes 1572872 | tf_op jit(solution)/shard_map/ppermute | solution.py:859
  180.9 18.1 %collective-permute-start.21 = (bf16[256,1024]{1,0:T(8,128)(2,1)S(1)}, bf16[256,1024]{1,0:T(8,128)(2,1)S(1)}, u32[]{:S(2)}, u32[]{:S(2)}) collective-permute-start(bf16[256,1024]{1,0:T(8,128)(2,1)S(1)} %add.130.refs_3_), channel_id=1, source_target_pairs={{0,1},{1,0},{2,3},{3,2},{4,5},{5,4},{6,7},{7,6},{8,9},{9,8},{10,11... | collective-permute-start | bytes 1572872 | tf_op jit(solution)/shard_map/ppermute | solution.py:500
  197.6 17.1 %collective-permute-start.23 = (bf16[512,512]{1,0:T(8,128)(2,1)}, bf16[512,512]{1,0:T(8,128)(2,1)S(1)}, u32[]{:S(2)}, u32[]{:S(2)}) collective-permute-start(bf16[512,512]{1,0:T(8,128)(2,1)} %add.131), channel_id=1, source_target_pairs={{4,0},{8,4},{12,8},{5,1},{9,5},{13,9},{6,2},{10,6},{14,10},{7,3},{... | collective-permute-start | bytes 1572872 | tf_op jit(solution)/shard_map/ppermute | solution.py:859
  198.9 51.9 %collective-permute-start.25 = (bf16[512,1536]{1,0:T(8,128)(2,1)}, bf16[512,1536]{1,0:T(8,128)(2,1)}, u32[]{:S(2)}, u32[]{:S(2)}) collective-permute-start(bf16[512,1536]{1,0:T(8,128)(2,1)} %get-tuple-element.578), channel_id=1, source_target_pairs={{0,16},{16,0},{1,17},{17,1},{2,18},{18,2},{3,19},{19,3},{4,20},{20... | collective-permute-start | bytes 4718600 | tf_op jit(solution)/shard_map/ppermute | solution.py:500
  214.8 21.5 %collective-permute-start.24 = (bf16[512,512]{1,0:T(8,128)(2,1)}, bf16[512,512]{1,0:T(8,128)(2,1)S(1)}, u32[]{:S(2)}, u32[]{:S(2)}) collective-permute-start(bf16[512,512]{1,0:T(8,128)(2,1)} %get-tuple-element.545), channel_id=1, source_target_pairs={{4,0},{8,4},{12,8},{5,1},{9,5},{13,9},{6,2},{10,6},{14,10},{7,3},{... | collective-permute-start | bytes 1572872 | tf_op jit(solution)/shard_map/ppermute | solution.py:859
  227.8 44.5 %collective-permute-start.30 = (bf16[1280,512]{1,0:T(8,128)(2,1)}, bf16[1280,512]{1,0:T(8,128)(2,1)}, u32[]{:S(2)}, u32[]{:S(2)}) collective-permute-start(bf16[1280,512]{1,0:T(8,128)(2,1)} %get-tuple-element.628), channel_id=1, source_target_pairs={{0,16},{16,0},{1,17},{17,1},{2,18},{18,2},{3,19},{19,3},{4,20},{20... | collective-permute-start | bytes 3932168 | tf_op jit(solution)/shard_map/ppermute | solution.py:500
  237.2 26.4 %collective-permute-start.27 = (bf16[512,512]{1,0:T(8,128)(2,1)}, bf16[512,512]{1,0:T(8,128)(2,1)}, u32[]{:S(2)}, u32[]{:S(2)}) collective-permute-start(bf16[512,512]{1,0:T(8,128)(2,1)} %add.132), channel_id=1, source_target_pairs={{4,0},{8,4},{12,8},{5,1},{9,5},{13,9},{6,2},{10,6},{14,10},{7,3},{... | collective-permute-start | bytes 1572872 | tf_op jit(solution)/shard_map/ppermute | solution.py:859
  238.7 35.8 %collective-permute-start.29 = (bf16[512,512]{1,0:T(8,128)(2,1)}, bf16[512,512]{1,0:T(8,128)(2,1)}, u32[]{:S(2)}, u32[]{:S(2)}) collective-permute-start(bf16[512,512]{1,0:T(8,128)(2,1)} %get-tuple-element.627), channel_id=1, source_target_pairs={{0,16},{16,0},{1,17},{17,1},{2,18},{18,2},{3,19},{19,3},{4,20},{20... | collective-permute-start | bytes 1572872 | tf_op jit(solution)/shard_map/ppermute | solution.py:500
  252.6 43.0 %collective-permute-start.26 = (bf16[512,1536]{1,0:T(8,128)(2,1)S(1)}, bf16[512,1536]{1,0:T(8,128)(2,1)}, u32[]{:S(2)}, u32[]{:S(2)}) collective-permute-start(bf16[512,1536]{1,0:T(8,128)(2,1)S(1)} %add.133), channel_id=1, source_target_pairs={{0,4},{12,8},{1,5},{13,9},{2,6},{14,10},{3,7},{15,11},{16,20},{28,... | collective-permute-start | bytes 4718600 | tf_op jit(solution)/shard_map/ppermute | solution.py:556
  272.2 4.2 collective-permute-start.28
  276.5 3.7 collective-permute-start.31
  287.5 2.9 collective-permute-start.32
  297.4 6.4 %collective-permute-start.33 = (bf16[512,1024]{1,0:T(8,128)(2,1)S(1)}, bf16[512,1024]{1,0:T(8,128)(2,1)S(1)}, u32[]{:S(2)}, u32[]{:S(2)}) collective-permute-start(bf16[512,1024]{1,0:T(8,128)(2,1)S(1)} %copy-done.23), channel_id=1, source_target_pairs={{0,1},{1,0},{2,3},{3,2},{4,5},{5,4},{6,7},{7,6},{8,9},{9,8},{10,11... | collective-permute-start | bytes 3145736 | tf_op jit(solution)/shard_map/ppermute | solution.py:500
  297.5 33.6 %collective-permute-start.39 = (bf16[1280,512]{1,0:T(8,128)(2,1)S(1)}, bf16[1280,512]{1,0:T(8,128)(2,1)S(1)}, u32[]{:S(2)}, u32[]{:S(2)}) collective-permute-start(bf16[1280,512]{1,0:T(8,128)(2,1)S(1)} %add.138), channel_id=1, source_target_pairs={{0,4},{12,8},{1,5},{13,9},{2,6},{14,10},{3,7},{15,11},{16,20},{28,... | collective-permute-start | bytes 3932168 | tf_op jit(solution)/shard_map/ppermute | solution.py:556
  302.1 41.9 %collective-permute-start.37 = (bf16[512,1024]{1,0:T(8,128)(2,1)S(1)}, bf16[512,1024]{1,0:T(8,128)(2,1)S(1)}, u32[]{:S(2)}, u32[]{:S(2)}) collective-permute-start(bf16[512,1024]{1,0:T(8,128)(2,1)S(1)} %add.142), channel_id=1, source_target_pairs={{0,2},{1,3},{2,0},{3,1},{4,6},{5,7},{6,4},{7,5},{8,10},{9,11},{10,... | collective-permute-start | bytes 3145736 | tf_op jit(solution)/shard_map/ppermute | solution.py:500
  302.6 46.7 %collective-permute-start.41 = (bf16[512,1536]{1,0:T(8,128)(2,1)S(1)}, bf16[512,1536]{1,0:T(8,128)(2,1)S(1)}, u32[]{:S(2)}, u32[]{:S(2)}) collective-permute-start(bf16[512,1536]{1,0:T(8,128)(2,1)S(1)} %add.143), channel_id=1, source_target_pairs={{4,8},{8,4},{5,9},{9,5},{6,10},{10,6},{7,11},{11,7},{20,24},{24,20... | collective-permute-start | bytes 4718600 | tf_op jit(solution)/shard_map/ppermute | solution.py:559
  303.4 14.2 %collective-permute-start.35 = (bf16[528,512]{1,0:T(8,128)(2,1)S(1)}, bf16[528,512]{1,0:T(8,128)(2,1)S(1)}, u32[]{:S(2)}, u32[]{:S(2)}) collective-permute-start(bf16[528,512]{1,0:T(8,128)(2,1)S(1)} %copy-done.37), channel_id=1, source_target_pairs={{0,16},{16,0},{1,17},{17,1},{2,18},{18,2},{3,19},{19,3},{4,20},{20... | collective-permute-start | bytes 1622024 | tf_op jit(solution)/shard_map/ppermute | solution.py:500
  303.8 38.2 %collective-permute-start.38 = (bf16[512,512]{1,0:T(8,128)(2,1)}, bf16[512,512]{1,0:T(8,128)(2,1)S(1)}, u32[]{:S(2)}, u32[]{:S(2)}) collective-permute-start(bf16[512,512]{1,0:T(8,128)(2,1)} %add.139), channel_id=1, source_target_pairs={{0,4},{12,8},{1,5},{13,9},{2,6},{14,10},{3,7},{15,11},{16,20},{28,... | collective-permute-start | bytes 1572872 | tf_op jit(solution)/shard_map/ppermute | solution.py:556
  344.4 9.6 %collective-permute-start.40 = (bf16[512,1024]{1,0:T(8,128)(2,1)S(1)}, bf16[512,1024]{1,0:T(8,128)(2,1)S(1)}, u32[]{:S(2)}, u32[]{:S(2)}) collective-permute-start(bf16[512,1024]{1,0:T(8,128)(2,1)S(1)} %add.148.refs_2_), channel_id=1, source_target_pairs={{0,1},{1,0},{2,3},{3,2},{4,5},{5,4},{6,7},{7,6},{8,9},{9,8},{10,11... | collective-permute-start | bytes 3145736 | tf_op jit(solution)/shard_map/ppermute | solution.py:500
  344.5 25.7 %collective-permute-start.34 = (bf16[512,1024]{1,0:T(8,128)(2,1)S(1)}, bf16[512,1024]{1,0:T(8,128)(2,1)}, u32[]{:S(2)}, u32[]{:S(2)}) collective-permute-start(bf16[512,1024]{1,0:T(8,128)(2,1)S(1)} %add.144), channel_id=1, source_target_pairs={{0,2},{1,3},{2,0},{3,1},{4,6},{5,7},{6,4},{7,5},{8,10},{9,11},{10,... | collective-permute-start | bytes 3145736 | tf_op jit(solution)/shard_map/ppermute | solution.py:500
  345.0 16.1 %collective-permute-start.36 = (bf16[528,512]{1,0:T(8,128)(2,1)S(1)}, bf16[528,512]{1,0:T(8,128)(2,1)S(1)}, u32[]{:S(2)}, u32[]{:S(2)}) collective-permute-start(bf16[528,512]{1,0:T(8,128)(2,1)S(1)} %add.145), channel_id=1, source_target_pairs={{0,4},{12,8},{1,5},{13,9},{2,6},{14,10},{3,7},{15,11},{16,20},{28,... | collective-permute-start | bytes 1622024 | tf_op jit(solution)/shard_map/ppermute | solution.py:556
  350.9 46.5 %collective-permute-start.49 = (bf16[512,1536]{1,0:T(8,128)(2,1)}, bf16[512,1536]{1,0:T(8,128)(2,1)}, u32[]{:S(2)}, u32[]{:S(2)}) collective-permute-start(bf16[512,1536]{1,0:T(8,128)(2,1)} %add.149), channel_id=1, source_target_pairs={{4,0},{8,12},{5,1},{9,13},{6,2},{10,14},{7,3},{11,15},{20,16},{24,... | collective-permute-start | bytes 4718600 | tf_op jit(solution)/shard_map/ppermute | solution.py:562
  352.2 27.2 %collective-permute-start.43 = (bf16[1280,512]{1,0:T(8,128)(2,1)}, bf16[1280,512]{1,0:T(8,128)(2,1)}, u32[]{:S(2)}, u32[]{:S(2)}) collective-permute-start(bf16[1280,512]{1,0:T(8,128)(2,1)} %add.146), channel_id=1, source_target_pairs={{4,8},{8,4},{5,9},{9,5},{6,10},{10,6},{7,11},{11,7},{20,24},{24,20... | collective-permute-start | bytes 3932168 | tf_op jit(solution)/shard_map/ppermute | solution.py:559
  371.8 11.2 %collective-permute-start.42 = (bf16[512,1024]{1,0:T(8,128)(2,1)S(1)}, bf16[512,1024]{1,0:T(8,128)(2,1)S(1)}, u32[]{:S(2)}, u32[]{:S(2)}) collective-permute-start(bf16[512,1024]{1,0:T(8,128)(2,1)S(1)} %add.151.refs_3_), channel_id=1, source_target_pairs={{0,1},{1,0},{2,3},{3,2},{4,5},{5,4},{6,7},{7,6},{8,9},{9,8},{10,11... | collective-permute-start | bytes 3145736 | tf_op jit(solution)/shard_map/ppermute | solution.py:500
  371.9 18.8 %collective-permute-start.44 = (bf16[528,512]{1,0:T(8,128)(2,1)}, bf16[528,512]{1,0:T(8,128)(2,1)}, u32[]{:S(2)}, u32[]{:S(2)}) collective-permute-start(bf16[528,512]{1,0:T(8,128)(2,1)} %add.150), channel_id=1, source_target_pairs={{4,8},{8,4},{5,9},{9,5},{6,10},{10,6},{7,11},{11,7},{20,24},{24,20... | collective-permute-start | bytes 1622024 | tf_op jit(solution)/shard_map/ppermute | solution.py:559
  373.4 14.6 %collective-permute-start.45 = (bf16[512,512]{1,0:T(8,128)(2,1)}, bf16[512,512]{1,0:T(8,128)(2,1)}, u32[]{:S(2)}, u32[]{:S(2)}) collective-permute-start(bf16[512,512]{1,0:T(8,128)(2,1)} %add.147), channel_id=1, source_target_pairs={{4,8},{8,4},{5,9},{9,5},{6,10},{10,6},{7,11},{11,7},{20,24},{24,20... | collective-permute-start | bytes 1572872 | tf_op jit(solution)/shard_map/ppermute | solution.py:559
  381.4 55.9 %collective-permute-start.48 = (bf16[1280,512]{1,0:T(8,128)(2,1)S(1)}, bf16[1280,512]{1,0:T(8,128)(2,1)}, u32[]{:S(2)}, u32[]{:S(2)}) collective-permute-start(bf16[1280,512]{1,0:T(8,128)(2,1)S(1)} %add.152), channel_id=1, source_target_pairs={{4,0},{8,12},{5,1},{9,13},{6,2},{10,14},{7,3},{11,15},{20,16},{24,... | collective-permute-start | bytes 3932168 | tf_op jit(solution)/shard_map/ppermute | solution.py:562
  389.4 46.9 %collective-permute-start.47 = (bf16[512,512]{1,0:T(8,128)(2,1)S(1)}, bf16[512,512]{1,0:T(8,128)(2,1)S(1)}, u32[]{:S(2)}, u32[]{:S(2)}) collective-permute-start(bf16[512,512]{1,0:T(8,128)(2,1)S(1)} %add.153), channel_id=1, source_target_pairs={{4,0},{8,12},{5,1},{9,13},{6,2},{10,14},{7,3},{11,15},{20,16},{24,... | collective-permute-start | bytes 1572872 | tf_op jit(solution)/shard_map/ppermute | solution.py:562
  392.0 53.0 %collective-permute-start.46 = (bf16[528,512]{1,0:T(8,128)(2,1)S(1)}, bf16[528,512]{1,0:T(8,128)(2,1)S(1)}, u32[]{:S(2)}, u32[]{:S(2)}) collective-permute-start(bf16[528,512]{1,0:T(8,128)(2,1)S(1)} %add.154), channel_id=1, source_target_pairs={{4,0},{8,12},{5,1},{9,13},{6,2},{10,14},{7,3},{11,15},{20,16},{24,... | collective-permute-start | bytes 1622024 | tf_op jit(solution)/shard_map/ppermute | solution.py:562
  (46 other events, 264.3 us)
where the time goes:
time: 455 us; the launch traced here: 448 us
  Pallas kernels  167 us (37%)
  waiting for transfers between devices  127 us (28%)
  starting transfers between devices  81 us (18%)
  other arithmetic  51.4 us (11%)
  local copies, waits for them, and re-layouts  19.2 us (4%)
    pallas_call x25, Pallas kernels, call(): pl.pallas_call(body_, name=name, out_shape=[o[0] for o in outs], grid_spe...  167 us
    ppermute x4, waiting for transfers between devices, sum_line(): came = lax.ppermute(total, axis, [(i + 1, i), (size - 2 - i, size - 1 - i)])  39.2 us
    ppermute x30, waiting for transfers between devices, swap(): return lax.ppermute(values, axis, [(i, i ^ bit) for i in range(size)])  37.6 us
    ppermute x4, waiting for transfers between devices, sum_line(): came = lax.ppermute(total, axis, [(i, i + 1), (size - 1 - i, size - 2 - i)])  28.1 us
    add x26, other arithmetic, plus(): return a + b  27 us
    ppermute x4, starting transfers between devices, sum_line(): came = lax.ppermute(total, axis, [(i, i + 1), (size - 1 - i, size - 2 - i)])  26.5 us
    ppermute x30, starting transfers between devices, swap(): return lax.ppermute(values, axis, [(i, i ^ bit) for i in range(size)])  20.7 us
    ppermute x4, waiting for transfers between devices, bring(): moving = lax.ppermute(one, 'ctx', down_perm)  11.4 us
  transfers between devices with their start and end apart: 50, of which 20 were waited for; matrix products, arithmetic and copies ran while one was open for 12% of the time, Pallas kernels for 37%

commit v1 on v0

--- a/solution.py
+++ b/solution.py
@@ -558,10 +558,12 @@
         yield total
     total = line(plus, total, lax.ppermute(total, axis, [(middle - 1, middle), (middle, middle - 1)]))
     yield total
+    came, outer = total, index < 0
     for i in reversed(range(middle - 1)):
+        total = jnp.where(outer, came, total)
         came = lax.ppermute(total, axis, [(i + 1, i), (size - 2 - i, size - 1 - i)])
-        total = jnp.where((index == i) | (index == size - 1 - i), came, total)
-    yield total
+        outer = (index == i) | (index == size - 1 - i)
+    yield came, total, outer
 
 
 def sum_small(values, axis, size):
@@ -1013,10 +1015,11 @@
     attend_own(1)
     forward(1)
     attend(0)
-    line.wait(gate_w[-1], up_w[-1])
+    line.wait(gate_w[-1])
     branch[0]()
     attend(1)
     branch[0]()
+    line.wait(up_w[-1])
     branch[1]()
     ffn(0)
     branch[1]()
@@ -1054,30 +1057,54 @@
     grad_one[0]()
     sums_of["gate_up"]()
     layers[0]()
-    sums_of["kv"]()
+    grad_one[0]()
+    input_output(0)
     sums_of["down"]()
+    sums_of["gate_up"]()
     sums_of["query"]()
-    grad_one[0]()
-    sums_of["gate_up"]()
-    input_output(0)
     sums_of["kv"]()
     layers[0]()
     input_output(1)
     sums_of["down"]()
+    sums_of["kv"]()
     layer_output(0)
     sums_of["query"]()
     sums_of["kv"]()
-    layer_output(1)
-    gate_up, down_and_out, query_sum, kv_total = (sums_of[name]() for name in ("gate_up", "down", "query", "kv"))
+    half = model // 2
+
+    def wide_type(value):
+        return (value.astype(f32),)
+
+    def columns_of(width):
+        return lambda value: (value[:, :width].astype(f32), value[:, width:].astype(f32))
+
+    def rows_at(height):
+        return lambda value: (value[:height].astype(f32), value[height:].astype(f32))
+
+    def keys_values(value):
+        return columns_of(kv_width)(value[:half]) + (value[half:].astype(f32),)
+
+    def finish(name, *after):
+        steps_ = sums_of[name]()
+        outs = []
+        for (came_, total, outer), to in zip([steps_] if paired else steps_, after):
+            outs += line(lambda c, v: to(jnp.where(outer, c, v)), came_, total)
+        return outs
+
     if paired:
-        gate_sum, up_sum = gate_up[:, :hidden], gate_up[:, hidden:]
-        down_sum, out_sum = down_and_out[:hidden], down_and_out[hidden:]
-        kv_total, gain_total = kv_total[: model // 2], kv_total[model // 2 :]
+        gate_sum, up_sum = finish("gate_up", columns_of(hidden))
+        layer_output(1)
+        down_sum, out_sum = finish("down", rows_at(hidden))
+        (query_sum,) = finish("query", wide_type)
+        key_sum, value_sum, gain_total = finish("kv", keys_values)
     else:
-        gate_sum, up_sum = gate_up[0][:, :hidden], gate_up[0][:, hidden:]
-        (down_sum, out_sum), (query_sum,), (kv_total,) = down_and_out, query_sum, kv_total
+        layer_output(1)
+        gate_sum, up_sum = finish("gate_up", columns_of(hidden))
+        down_sum, out_sum = finish("down", wide_type, wide_type)
+        (query_sum,) = finish("query", wide_type)
+        key_sum, value_sum = finish("kv", columns_of(kv_width))
     if paired:
-        mine_all = gain_total.reshape(1, -1)[0].astype(f32)
+        mine_all = gain_total.reshape(1, -1)[0]
         gain_out = []
         at = 0
         for width in (part, part, small, small):
@@ -1096,16 +1123,16 @@
         finished["layer_out"],
         finished["input_grad"],
         attn_out,
-        query_sum.astype(f32),
-        kv_total[:, :kv_width].astype(f32),
-        kv_total[:, kv_width:].astype(f32),
+        query_sum,
+        key_sum,
+        value_sum,
         query_out,
         key_out,
-        out_sum.astype(f32),
+        out_sum,
         ffn_out,
-        gate_sum.astype(f32),
-        up_sum.astype(f32),
-        down_sum.astype(f32),
+        gate_sum,
+        up_sum,
+        down_sum,
     )
 
 

time: 455 us -> 442 us (0.971)
  waiting for transfers between devices: 127 us -> 95.3 us
  starting transfers between devices: 81 us -> 99.5 us
  other arithmetic: 51.4 us -> 57 us
    ppermute x4, waiting for transfers between devices: 28.1 us -> 11.8 us  [sum_line(): came = lax.ppermute(total, axis, [(i, i + 1), (size - 1 - i, size - 2 - i)])]
    ppermute x30, starting transfers between devices: 20.7 us -> 32.2 us  [swap(): return lax.ppermute(values, axis, [(i, i ^ bit) for i in range(size)])]
    ppermute x30, waiting for transfers between devices: 37.6 us -> 30.6 us  [swap(): return lax.ppermute(values, axis, [(i, i ^ bit) for i in range(size)])]
    add x26, other arithmetic: 27 us -> 31.6 us  [plus(): return a + b]
    ppermute x4, waiting for transfers between devices: 39.2 us -> 34.6 us  [sum_line(): came = lax.ppermute(total, axis, [(i + 1, i), (size - 2 - i, size - 1 - i)])]
    unnamed x90 -> x92, local copies, waits for them, and re-layouts: 10.7 us -> 8.82 us
  transfers between devices with their start and end apart: 50 -> 50, of which waited for: 20 -> 17; matrix products, arithmetic and copies ran while one was open for 12% -> 14% of each run, Pallas kernels for 37% -> 38%
where the time goes in v1:
time: 442 us; the launch traced here: 434 us
  Pallas kernels  163 us (37%)
  starting transfers between devices  99.5 us (23%)
  waiting for transfers between devices  95.3 us (22%)
  other arithmetic  57 us (13%)
  local copies, waits for them, and re-layouts  17.3 us (4%)
    pallas_call x25, Pallas kernels, call(): pl.pallas_call(body_, name=name, out_shape=[o[0] for o in outs], grid_spe...  163 us
    ppermute x4, waiting for transfers between devices, sum_line(): came = lax.ppermute(total, axis, [(i + 1, i), (size - 2 - i, size - 1 - i)])  34.6 us
    ppermute x30, starting transfers between devices, swap(): return lax.ppermute(values, axis, [(i, i ^ bit) for i in range(size)])  32.2 us
    add x26, other arithmetic, plus(): return a + b  31.6 us
    ppermute x30, waiting for transfers between devices, swap(): return lax.ppermute(values, axis, [(i, i ^ bit) for i in range(size)])  30.6 us
    ppermute x4, starting transfers between devices, sum_line(): came = lax.ppermute(total, axis, [(i, i + 1), (size - 1 - i, size - 2 - i)])  29.2 us
    ppermute x4, waiting for transfers between devices, sum_line(): came = lax.ppermute(total, axis, [(i, i + 1), (size - 1 - i, size - 2 - i)])  11.8 us
    ppermute x2, starting transfers between devices, forward(): kv[s].insert(0, lax.ppermute(line.after(kv[s][0]), 'ctx', up_perm))  11.6 us
  transfers between devices with their start and end apart: 50, of which 17 were waited for; matrix products, arithmetic and copies ran while one was open for 14% of the time, Pallas kernels for 38%

profile of v1, /device:TPU:0, one launch (start us, length us, event | category | flops | bytes accessed | tf_op | source)
XLA Modules:
  0.0 433.9 jit_solution(1710496763729861944)
XLA Ops:
  2.7 3.0 collective-permute-start.1
  20.8 4.7 %keys.2 = (bf16[512,1024]{1,0:T(8,128)(2,1)}, bf16[512,512]{1,0:T(8,128)(2,1)}, f32[512,256]{1,0:T(8,128)}, bf16[1280,512]{1,0:T(8,128)(2,1)}) custom-call(s32[4]{0:T(128)} %pad_add_fusion.2.ids, bf16[2,512,1024]{2,1,0:T(8,128)(2,1)} %refs_0_.10, f32[1,1024]{1,0:T(1,128)} %get-tuple-element.682.refs_1_.refs_2_.refs_4_, ...), custom_call_target="tpu_custom_call", output_to_operand_aliasing={{3}: (8, {})} | custom-call | flops 1 | bytes 1 | tf_op jit(solution)/shard_map/keys/pallas_call | solution.py:65
  29.8 4.8 %collective-permute-start.7 = (bf16[512,512]{1,0:T(8,128)(2,1)}, bf16[512,512]{1,0:T(8,128)(2,1)}, u32[]{:S(2)}, u32[]{:S(2)}) collective-permute-start(bf16[512,512]{1,0:T(8,128)(2,1)} %get-tuple-element.503.refs_2_.refs_18_), channel_id=1, source_target_pairs={{0,4},{4,8},{8,12},{1,5},{5,9},{9,13},{2,6},{6,10},{10,14},{3,7},{... | collective-permute-start | bytes 1572872 | tf_op jit(solution)/shard_map/ppermute | solution.py:737
  36.7 4.6 %keys.3 = (bf16[512,1024]{1,0:T(8,128)(2,1)}, bf16[512,512]{1,0:T(8,128)(2,1)}, f32[512,256]{1,0:T(8,128)}) custom-call(s32[4]{0:T(128)} %pad_add_fusion.ids, bf16[512,512]{1,0:T(8,128)(2,1)} %copy-done.3, bf16[2,512,1024]{2,1,0:T(8,128)(2,1)} %refs_0_.10, f32[1,1024]{1,0:T(1,128)} %get-tuple-element.682.refs_1_.refs_2_.refs_4_, ...), custom_call_target="tpu_custom_call" | custom-call | flops 1 | bytes 1 | tf_op jit(solution)/shard_map/keys/pallas_call | solution.py:65
  43.3 4.4 %collective-permute-start.8 = (bf16[512,512]{1,0:T(8,128)(2,1)}, bf16[512,512]{1,0:T(8,128)(2,1)S(1)}, u32[]{:S(2)}, u32[]{:S(2)}) collective-permute-start(bf16[512,512]{1,0:T(8,128)(2,1)} %collective-permute-done.7.refs_5_.refs_17_), channel_id=1, source_target_pairs={{0,4},{4,8},{8,12},{1,5},{5,9},{9,13},{2,6},{6,10},{10,14},{3,7},{... | collective-permute-start | bytes 1572872 | tf_op jit(solution)/shard_map/ppermute | solution.py:742
  48.9 4.2 collective-permute-start.3
  53.1 4.4 %query.2 = (bf16[512,512]{1,0:T(8,128)(2,1)}, f32[512,512]{1,0:T(8,128)}) custom-call(s32[4]{0:T(128)} %pad_add_fusion.2.ids, bf16[512,1024]{1,0:T(8,128)(2,1)} %get-tuple-element.645.refs_0_, f32[2,512,128]{2,1,0:T(8,128)} %get-tuple-element.615.refs_2_.refs_3_.refs_1_.refs_13_.refs_6_, ...), custom_call_target="tpu_custom_call" | custom-call | flops 1 | bytes 1 | tf_op jit(solution)/shard_map/query/pallas_call | solution.py:65
  57.5 4.4 %query.3 = (bf16[512,512]{1,0:T(8,128)(2,1)}, f32[512,512]{1,0:T(8,128)}) custom-call(s32[4]{0:T(128)} %pad_add_fusion.ids, bf16[512,1024]{1,0:T(8,128)(2,1)} %get-tuple-element.646.refs_0_.refs_1_, f32[2,512,128]{2,1,0:T(8,128)} %get-tuple-element.615.refs_2_.refs_3_.refs_1_.refs_13_.refs_6_, ...), custom_call_target="tpu_custom_call" | custom-call | flops 1 | bytes 1 | tf_op jit(solution)/shard_map/query/pallas_call | solution.py:65
  61.9 3.8 attend_own.2
  65.7 6.0 %attend_own.3 = (f32[512,512]{1,0:T(8,128)}, f32[8,512]{1,0:T(8,128)}) custom-call(s32[4]{0:T(128)} %pad_add_fusion.ids, bf16[512,512]{1,0:T(8,128)(2,1)} %get-tuple-element.539.refs_0_.refs_1_.refs_10_, s32[2,1,512]{2,1,0:T(1,128)} %broadcast_in_dim.36.refs_1_.refs_2_.refs_11_, bf16[512,512]{1,0:T(8,128)(2,1)} %get-tuple-element.547.refs_2_.refs_18_), custom_call_target="tpu_custom_call" | custom-call | flops 1 | bytes 1 | tf_op jit(solution)/shard_map/attend_own/pallas_call | solution.py:65
  72.9 5.6 %attend.2 = (bf16[256,1024]{1,0:T(8,128)(2,1)}, bf16[256,1024]{1,0:T(8,128)(2,1)}, bf16[512,512]{1,0:T(8,128)(2,1)}, f32[8,512]{1,0:T(8,128)}) custom-call(s32[4]{0:T(128)} %pad_add_fusion.2.ids, bf16[512,512]{1,0:T(8,128)(2,1)} %get-tuple-element.495.refs_0_.refs_10_, s32[2,1,512]{2,1,0:T(1,128)} %broadcast_in_dim.36.refs_1_.refs_2_.refs_11_, ...), custom_call_target="tpu_custom_call" | custom-call | flops 1 | bytes 1 | tf_op jit(solution)/shard_map/attend/pallas_call | solution.py:65
  78.6 3.7 collective-permute-start.11
  82.3 7.2 %collective-permute-start.4 = (bf16[512,512]{1,0:T(8,128)(2,1)}, bf16[512,512]{1,0:T(8,128)(2,1)S(1)}, u32[]{:S(2)}, u32[]{:S(2)}) collective-permute-start(bf16[512,512]{1,0:T(8,128)(2,1)} %collective-permute-done.3.refs_6_.refs_17_), channel_id=1, source_target_pairs={{0,4},{4,8},{8,12},{1,5},{5,9},{9,13},{2,6},{6,10},{10,14},{3,7},{... | collective-permute-start | bytes 1572872 | tf_op jit(solution)/shard_map/ppermute | solution.py:742
  92.4 8.7 %collective-permute-done.4.refs_5_.refs_16_ = bf16[512,512]{1,0:T(8,128)(2,1)S(1)} collective-permute-done((bf16[512,512]{1,0:T(8,128)(2,1)}, bf16[512,512]{1,0:T(8,128)(2,1)S(1)}, u32[]{:S(2)}, u32[]{:S(2)}) %collective-permute-start.4) | collective-permute-done | bytes 524320 | tf_op jit(solution)/shard_map/ppermute | solution.py:742
  102.0 5.7 %attend.3 = (bf16[256,1024]{1,0:T(8,128)(2,1)}, bf16[256,1024]{1,0:T(8,128)(2,1)}, bf16[512,512]{1,0:T(8,128)(2,1)}, f32[8,512]{1,0:T(8,128)}) custom-call(s32[4]{0:T(128)} %pad_add_fusion.ids, bf16[512,768]{1,0:T(8,128)(2,1)} %copy-done.11, bf16[512,512]{1,0:T(8,128)(2,1)} %get-tuple-element.539.refs_0_.refs_1_.refs_10_, ...), custom_call_target="tpu_custom_call" | custom-call | flops 1 | bytes 1 | tf_op jit(solution)/shard_map/attend/pallas_call | solution.py:65
  115.3 12.7 %ffn.2 = (bf16[512,1024]{1,0:T(8,128)(2,1)}, bf16[512,768]{1,0:T(8,128)(2,1)}, bf16[512,768]{1,0:T(8,128)(2,1)}, bf16[512,768]{1,0:T(8,128)(2,1)}, bf16[256,1024...) custom-call(s32[4]{0:T(128)} %pad_add_fusion.2.ids, bf16[512,768]{1,0:T(8,128)(2,1)} %copy-done.10, ...), custom_call_target="tpu_custom_call" | custom-call | flops 1 | bytes 1 | tf_op jit(solution)/shard_map/ffn/pallas_call | solution.py:65
  132.5 12.6 %ffn.3 = (bf16[512,1024]{1,0:T(8,128)(2,1)}, bf16[512,768]{1,0:T(8,128)(2,1)}, bf16[512,768]{1,0:T(8,128)(2,1)}, bf16[512,768]{1,0:T(8,128)(2,1)}, bf16[256,1024...) custom-call(s32[4]{0:T(128)} %pad_add_fusion.ids, bf16[2,512,1024]{2,1,0:T(8,128)(2,1)} %refs_0_.10, ...), custom_call_target="tpu_custom_call" | custom-call | flops 1 | bytes 1 | tf_op jit(solution)/shard_map/ffn/pallas_call | solution.py:65
  150.6 12.7 %attend_back.2 = (f32[512,1024]{1,0:T(8,128)}, bf16[512,1024]{1,0:T(8,128)(2,1)}, bf16[512,512]{1,0:T(8,128)(2,1)}, f32[1,128]{1,0:T(1,128)}, bf16[512,512]{1,0:...) custom-call(s32[4]{0:T(128)} %pad_add_fusion.2.ids, bf16[2,512,1024]{2,1,0:T(8,128)(2,1)} %refs_0_.10, ...), custom_call_target="tpu_custom_call" | custom-call | flops 1 | bytes 1 | tf_op jit(solution)/shard_map/attend_back/pallas_call | solution.py:65
  164.6 8.3 %gate_up_grad.1 = (bf16[512,1536]{1,0:T(8,128)(2,1)}, bf16[512,1536]{1,0:T(8,128)(2,1)}) custom-call(s32[4]{0:T(128)} %pad_add_fusion.2.ids, bf16[512,1024]{1,0:T(8,128)(2,1)} %get-tuple-element.507.refs_0_, bf16[512,1024]{1,0:T(8,128)(2,1)} %get-tuple-element.508.refs_1_, bf16[512,768]{1,0:T(8,128)(2,1)} %get-tuple-element.509.refs_2_, ...), custom_call_target="tpu_custom_call" | custom-call | flops 1 | bytes 1 | tf_op jit(solution)/shard_map/gate_up_grad/pallas_call | solution.py:65
  173.3 4.9 %down.2 = (bf16[512,1024]{1,0:T(8,128)(2,1)}, bf16[512,1024]{1,0:T(8,128)(2,1)}) custom-call(s32[4]{0:T(128)} %pad_add_fusion.2.ids, bf16[512,768]{1,0:T(8,128)(2,1)} %get-tuple-element.559.refs_0_.refs_1_, bf16[1280,512]{1,0:T(8,128)(2,1)} %get-tuple-element.580.refs_6_.refs_7_.refs_11_.refs_10_.refs_19_.refs_1_, bf16[1280,512]{1,0:T(8,128)(2,1)} %copy-done), custom_call_target="tpu_custom_call" | custom-call | flops 1 | bytes 1 | tf_op jit(solution)/shard_map/down/pallas_call | solution.py:65
  178.1 7.4 %collective-permute-done.22 = bf16[512,512]{1,0:T(8,128)(2,1)S(1)} collective-permute-done((bf16[512,512]{1,0:T(8,128)(2,1)}, bf16[512,512]{1,0:T(8,128)(2,1)S(1)}, u32[]{:S(2)}, u32[]{:S(2)}) %collective-permute-start.22) | collective-permute-done | bytes 524320 | tf_op jit(solution)/shard_map/ppermute | solution.py:861
  187.8 6.1 %collective-permute-start.25 = (bf16[512,1536]{1,0:T(8,128)(2,1)}, bf16[512,1536]{1,0:T(8,128)(2,1)}, u32[]{:S(2)}, u32[]{:S(2)}) collective-permute-start(bf16[512,1536]{1,0:T(8,128)(2,1)} %get-tuple-element.586), channel_id=1, source_target_pairs={{0,16},{16,0},{1,17},{17,1},{2,18},{18,2},{3,19},{19,3},{4,20},{20... | collective-permute-start | bytes 4718600 | tf_op jit(solution)/shard_map/ppermute | solution.py:500
  194.6 15.0 %attend_back.3 = (f32[512,1024]{1,0:T(8,128)}, bf16[512,1024]{1,0:T(8,128)(2,1)}, bf16[512,512]{1,0:T(8,128)(2,1)}, f32[1,128]{1,0:T(1,128)}, bf16[512,512]{1,0:...) custom-call(s32[4]{0:T(128)} %pad_add_fusion.ids, bf16[2,512,1024]{2,1,0:T(8,128)(2,1)} %refs_0_.10, ...), custom_call_target="tpu_custom_call" | custom-call | flops 1 | bytes 1 | tf_op jit(solution)/shard_map/attend_back/pallas_call | solution.py:65
  212.4 5.7 %down_grad.1 = (bf16[1280,512]{1,0:T(8,128)(2,1)}, bf16[1280,512]{1,0:T(8,128)(2,1)}) custom-call(s32[4]{0:T(128)} %pad_add_fusion.2.ids, bf16[512,512]{1,0:T(8,128)(2,1)} %copy-done.19, bf16[512,768]{1,0:T(8,128)(2,1)} %get-tuple-element.559.refs_0_.refs_1_, bf16[512,768]{1,0:T(8,128)(2,1)} %get-tuple-element.579.refs_2_.refs_0_, ...), custom_call_target="tpu_custom_call" | custom-call | flops 1 | bytes 1 | tf_op jit(solution)/shard_map/down_grad/pallas_call | solution.py:65
  218.2 4.6 %out_grad.1 = (bf16[1280,512]{1,0:T(8,128)(2,1)}, bf16[1280,512]{1,0:T(8,128)(2,1)}) custom-call(s32[4]{0:T(128)} %pad_add_fusion.2.ids, bf16[512,512]{1,0:T(8,128)(2,1)} %get-tuple-element.565.refs_8_.refs_0_, bf16[512,512]{1,0:T(8,128)(2,1)} %get-tuple-element.566.refs_8_.refs_1_, ...), custom_call_target="tpu_custom_call", output_to_operand_aliasing={{0}: (5, {}), {1}: (6, {})} | custom-call | flops 1 | bytes 1 | tf_op jit(solution)/shard_map/out_grad/pallas_call | solution.py:65
  222.7 5.7 %query_grad.1 = (bf16[512,512]{1,0:T(8,128)(2,1)}, bf16[512,512]{1,0:T(8,128)(2,1)}) custom-call(s32[4]{0:T(128)} %pad_add_fusion.2.ids, bf16[512,1024]{1,0:T(8,128)(2,1)} %get-tuple-element.645.refs_0_, bf16[512,1024]{1,0:T(8,128)(2,1)} %get-tuple-element.646.refs_0_.refs_1_, bf16[512,512]{1,0:T(8,128)(2,1)} %get-tuple-element.591.refs_2_, ...), custom_call_target="tpu_custom_call" | custom-call | flops 1 | bytes 1 | tf_op jit(solution)/shard_map/query_grad/pallas_call | solution.py:65
  233.7 4.7 %down.3 = (bf16[512,1024]{1,0:T(8,128)(2,1)}, bf16[512,1024]{1,0:T(8,128)(2,1)}) custom-call(s32[4]{0:T(128)} %pad_add_fusion.ids, bf16[512,768]{1,0:T(8,128)(2,1)} %get-tuple-element.579.refs_2_.refs_0_, bf16[1280,512]{1,0:T(8,128)(2,1)} %get-tuple-element.580.refs_6_.refs_7_.refs_11_.refs_10_.refs_19_.refs_1_, ...), custom_call_target="tpu_custom_call", output_to_operand_aliasing={{0}: (4, {}), {1}: (5, {})} | custom-call | flops 1 | bytes 1 | tf_op jit(solution)/shard_map/down/pallas_call | solution.py:65
  238.4 7.2 %input_back.2 = (bf16[512,512]{1,0:T(8,128)(2,1)}, bf16[512,1024]{1,0:T(8,128)(2,1)}, bf16[512,1024]{1,0:T(8,128)(2,1)}, f32[1,128]{1,0:T(1,128)}, f32[1,1024]{1,0:T(1,128)}) custom-call(s32[4]{0:T(128)} %pad_add_fusion.2.ids, bf16[2,512,1024]{2,1,0:T(8,128)(2,1)} %refs_0_.10, f32[1,1024]{1,0:T(1,128)} %get-tuple-element.682.refs_1_.refs_2_.refs_4_, ...), custom_call_target="tpu_custom_call" | custom-call | flops 1 | bytes 1 | tf_op jit(solution)/shard_map/input_back/pallas_call | solution.py:65
  247.4 9.1 %collective-permute-start.26 = (bf16[512,1536]{1,0:T(8,128)(2,1)S(1)}, bf16[512,1536]{1,0:T(8,128)(2,1)}, u32[]{:S(2)}, u32[]{:S(2)}) collective-permute-start(bf16[512,1536]{1,0:T(8,128)(2,1)S(1)} %add.133), channel_id=1, source_target_pairs={{0,4},{12,8},{1,5},{13,9},{2,6},{14,10},{3,7},{15,11},{16,20},{28,... | collective-permute-start | bytes 4718600 | tf_op jit(solution)/shard_map/ppermute | solution.py:556
  256.5 7.2 %input_back.3 = (bf16[512,512]{1,0:T(8,128)(2,1)}, bf16[512,1024]{1,0:T(8,128)(2,1)}, bf16[512,1024]{1,0:T(8,128)(2,1)}, f32[1,128]{1,0:T(1,128)}, f32[1,1024]{1,0:T(1,128)}) custom-call(s32[4]{0:T(128)} %pad_add_fusion.ids, bf16[2,512,1024]{2,1,0:T(8,128)(2,1)} %refs_0_.10, ...), custom_call_target="tpu_custom_call", output_to_operand_aliasing={{1}: (14, {}), {2}: (15, {})} | custom-call | flops 1 | bytes 1 | tf_op jit(solution)/shard_map/input_back/pallas_call | solution.py:65
  273.9 5.6 %kv_grad.1 = (bf16[528,512]{1,0:T(8,128)(2,1)}, bf16[528,512]{1,0:T(8,128)(2,1)}) custom-call(s32[4]{0:T(128)} %pad_add_fusion.2.ids, bf16[512,1024]{1,0:T(8,128)(2,1)} %get-tuple-element.645.refs_0_, bf16[512,1024]{1,0:T(8,128)(2,1)} %get-tuple-element.646.refs_0_.refs_1_, bf16[512,512]{1,0:T(8,128)(2,1)} %get-tuple-element.647.refs_2_, ...), custom_call_target="tpu_custom_call" | custom-call | flops 1 | bytes 1 | tf_op jit(solution)/shard_map/kv_grad/pallas_call | solution.py:65
  279.6 2.9 collective-permute-done.32
  284.1 4.6 %collective-permute-done.26 = bf16[512,1536]{1,0:T(8,128)(2,1)} collective-permute-done((bf16[512,1536]{1,0:T(8,128)(2,1)S(1)}, bf16[512,1536]{1,0:T(8,128)(2,1)}, u32[]{:S(2)}, u32[]{:S(2)}) %collective-permute-start.26) | collective-permute-done | bytes 1572896 | tf_op jit(solution)/shard_map/ppermute | solution.py:556
  288.7 2.9 add.143
  292.1 5.7 %collective-permute-start.38 = (bf16[1280,512]{1,0:T(8,128)(2,1)S(1)}, bf16[1280,512]{1,0:T(8,128)(2,1)}, u32[]{:S(2)}, u32[]{:S(2)}) collective-permute-start(bf16[1280,512]{1,0:T(8,128)(2,1)S(1)} %add.138), channel_id=1, source_target_pairs={{0,4},{12,8},{1,5},{13,9},{2,6},{14,10},{3,7},{15,11},{16,20},{28,... | collective-permute-start | bytes 3932168 | tf_op jit(solution)/shard_map/ppermute | solution.py:556
  301.0 16.2 %collective-permute-done.39 = bf16[512,1024]{1,0:T(8,128)(2,1)S(1)} collective-permute-done((bf16[512,1024]{1,0:T(8,128)(2,1)S(1)}, bf16[512,1024]{1,0:T(8,128)(2,1)S(1)}, u32[]{:S(2)}, u32[]{:S(2)}) %collective-permute-start.39) | collective-permute-done | bytes 1048608 | tf_op jit(solution)/shard_map/ppermute | solution.py:500
  320.5 4.5 %input_grad.2.refs_5_ = f32[2,512,1024]{2,1,0:T(8,128)} custom-call(s32[4]{0:T(128)} %pad_add_fusion.2.ids, bf16[2,512,1024]{2,1,0:T(8,128)(2,1)} %refs_0_.10, f32[512,1024]{1,0:T(8,128)} %get-tuple-element.664.refs_1_, bf16[512,1024]{1,0:T(8,128)(2,1)} %copy-done.6, bf16[512,1024]{1,0:T(8,128)(2,1)} %collective-permute-done.40.refs_3_, ...), custom_call_target="tpu_custom_call" | custom-call | flops 1 | bytes 1 | tf_op jit(solution)/shard_map/input_grad/pallas_call | solution.py:65
  325.0 2.8 add.146
  331.4 9.2 %collective-permute-start.36 = (bf16[512,512]{1,0:T(8,128)(2,1)S(1)}, bf16[512,512]{1,0:T(8,128)(2,1)S(1)}, u32[]{:S(2)}, u32[]{:S(2)}) collective-permute-start(bf16[512,512]{1,0:T(8,128)(2,1)S(1)} %add.139), channel_id=1, source_target_pairs={{0,4},{12,8},{1,5},{13,9},{2,6},{14,10},{3,7},{15,11},{16,20},{28,... | collective-permute-start | bytes 1572872 | tf_op jit(solution)/shard_map/ppermute | solution.py:556
  344.3 7.1 %collective-permute-done.36 = bf16[512,512]{1,0:T(8,128)(2,1)S(1)} collective-permute-done((bf16[512,512]{1,0:T(8,128)(2,1)S(1)}, bf16[512,512]{1,0:T(8,128)(2,1)S(1)}, u32[]{:S(2)}, u32[]{:S(2)}) %collective-permute-start.36) | collective-permute-done | bytes 524320 | tf_op jit(solution)/shard_map/ppermute | solution.py:556
  352.5 5.2 %collective-permute-start.42 = (bf16[528,512]{1,0:T(8,128)(2,1)S(1)}, bf16[528,512]{1,0:T(8,128)(2,1)}, u32[]{:S(2)}, u32[]{:S(2)}) collective-permute-start(bf16[528,512]{1,0:T(8,128)(2,1)S(1)} %add.149), channel_id=1, source_target_pairs={{0,4},{12,8},{1,5},{13,9},{2,6},{14,10},{3,7},{15,11},{16,20},{28,... | collective-permute-start | bytes 1622024 | tf_op jit(solution)/shard_map/ppermute | solution.py:556
  359.8 4.5 %input_grad.3 = f32[2,512,1024]{2,1,0:T(8,128)} custom-call(s32[4]{0:T(128)} %pad_add_fusion.ids, bf16[2,512,1024]{2,1,0:T(8,128)(2,1)} %refs_0_.10, f32[512,1024]{1,0:T(8,128)} %get-tuple-element.679.refs_1_, bf16[512,1024]{1,0:T(8,128)(2,1)} %copy-done.6, bf16[512,1024]{1,0:T(8,128)(2,1)} %collective-permute-done.40.refs_3_, ...), custom_call_target="tpu_custom_call", output_to_operand_aliasing={{}: (6, {})} | custom-call | flops 1 | bytes 1 | tf_op jit(solution)/shard_map/input_grad/pallas_call | solution.py:65
  364.3 3.2 add.151
  373.1 4.1 layer_out.2.refs_6_
  386.6 4.1 layer_out.3
  390.7 19.3 %collective-permute-done.49 = bf16[1280,512]{1,0:T(8,128)(2,1)} collective-permute-done((bf16[1280,512]{1,0:T(8,128)(2,1)}, bf16[1280,512]{1,0:T(8,128)(2,1)}, u32[]{:S(2)}, u32[]{:S(2)}) %collective-permute-start.49) | collective-permute-done | bytes 1310752 | tf_op jit(solution)/shard_map/ppermute | solution.py:564
  412.9 8.4 %collective-permute-done.48 = bf16[512,512]{1,0:T(8,128)(2,1)} collective-permute-done((bf16[512,512]{1,0:T(8,128)(2,1)}, bf16[512,512]{1,0:T(8,128)(2,1)}, u32[]{:S(2)}, u32[]{:S(2)}) %collective-permute-start.48) | collective-permute-done | bytes 524320 | tf_op jit(solution)/shard_map/ppermute | solution.py:564
  424.5 6.9 %collective-permute-done.47 = bf16[528,512]{1,0:T(8,128)(2,1)S(1)} collective-permute-done((bf16[528,512]{1,0:T(8,128)(2,1)S(1)}, bf16[528,512]{1,0:T(8,128)(2,1)S(1)}, u32[]{:S(2)}, u32[]{:S(2)}) %collective-permute-start.47) | collective-permute-done | bytes 540704 | tf_op jit(solution)/shard_map/ppermute | solution.py:564
  (252 shorter events, 116.0 us)
Async XLA Ops:
  2.7 17.3 %collective-permute-start.1 = (bf16[512,512]{1,0:T(8,128)(2,1)S(1)}, bf16[512,512]{1,0:T(8,128)(2,1)S(1)}, u32[]{:S(2)}, u32[]{:S(2)}) collective-permute-start(bf16[512,512]{1,0:T(8,128)(2,1)S(1)} %constant_dynamic-update-slice_fusion.refs_5_.refs_6_.refs_11_), channel_id=1, source_target_pairs={{0,16},{16,0},{1,17},{17,1},{2,18},{18,2},{3,19},{19,3},{4,20},{20... | collective-permute-start | bytes 1572872 | tf_op jit(solution)/shard_map/ppermute | solution.py:500
  7.9 10.8 %collective-permute-start = (bf16[3,512]{1,0:T(4,128)(2,1)S(1)}, bf16[3,512]{1,0:T(4,128)(2,1)S(1)}, u32[]{:S(2)}, u32[]{:S(2)}) collective-permute-start(bf16[3,512]{1,0:T(4,128)(2,1)S(1)} %pad_maximum_fusion.5), channel_id=1, source_target_pairs={{0,16},{16,0},{1,17},{17,1},{2,18},{18,2},{3,19},{19,3},{4,20},{20... | collective-permute-start | bytes 9224 | tf_op jit(solution)/shard_map/ppermute | solution.py:500
  8.0 21.8 %collective-permute-start.2 = (bf16[512,512]{1,0:T(8,128)(2,1)}, bf16[512,512]{1,0:T(8,128)(2,1)S(1)}, u32[]{:S(2)}, u32[]{:S(2)}) collective-permute-start(bf16[512,512]{1,0:T(8,128)(2,1)} %refs_9_.2), channel_id=1, source_target_pairs={{0,16},{16,0},{1,17},{17,1},{2,18},{18,2},{3,19},{19,3},{4,20},{20... | collective-permute-start | bytes 1572872 | tf_op jit(solution)/shard_map/ppermute | solution.py:500
  25.5 46.2 %collective-permute-start.5 = (bf16[1280,512]{1,0:T(8,128)(2,1)}, bf16[1280,512]{1,0:T(8,128)(2,1)S(1)}, u32[]{:S(2)}, u32[]{:S(2)}) collective-permute-start(bf16[1280,512]{1,0:T(8,128)(2,1)} %get-tuple-element.580.refs_6_.refs_7_.refs_11_.refs_10_.refs_19_.refs_1_), channel_id=1, source_target_pairs={{0,16},{16,0},{1,17},{17,1},{2,18},{18,2},{3,19},{19,3},{4,20},{20... | collective-permute-start | bytes 3932168 | tf_op jit(solution)/shard_map/ppermute | solution.py:500
  29.8 13.5 %collective-permute-start.7 = (bf16[512,512]{1,0:T(8,128)(2,1)}, bf16[512,512]{1,0:T(8,128)(2,1)}, u32[]{:S(2)}, u32[]{:S(2)}) collective-permute-start(bf16[512,512]{1,0:T(8,128)(2,1)} %get-tuple-element.503.refs_2_.refs_18_), channel_id=1, source_target_pairs={{0,4},{4,8},{8,12},{1,5},{5,9},{9,13},{2,6},{6,10},{10,14},{3,7},{... | collective-permute-start | bytes 1572872 | tf_op jit(solution)/shard_map/ppermute | solution.py:737
  34.6 43.9 %collective-permute-start.6 = (bf16[512,768]{1,0:T(8,128)(2,1)S(1)}, bf16[512,768]{1,0:T(8,128)(2,1)S(1)}, u32[]{:S(2)}, u32[]{:S(2)}) collective-permute-start(bf16[512,768]{1,0:T(8,128)(2,1)S(1)} %copy-done.15), channel_id=1, source_target_pairs={{0,16},{16,0},{1,17},{17,1},{2,18},{18,2},{3,19},{19,3},{4,20},{20... | collective-permute-start | bytes 2359304 | tf_op jit(solution)/shard_map/ppermute | solution.py:500
  43.3 28.4 %collective-permute-start.8 = (bf16[512,512]{1,0:T(8,128)(2,1)}, bf16[512,512]{1,0:T(8,128)(2,1)S(1)}, u32[]{:S(2)}, u32[]{:S(2)}) collective-permute-start(bf16[512,512]{1,0:T(8,128)(2,1)} %collective-permute-done.7.refs_5_.refs_17_), channel_id=1, source_target_pairs={{0,4},{4,8},{8,12},{1,5},{5,9},{9,13},{2,6},{6,10},{10,14},{3,7},{... | collective-permute-start | bytes 1572872 | tf_op jit(solution)/shard_map/ppermute | solution.py:742
  48.9 33.4 %collective-permute-start.3 = (bf16[512,512]{1,0:T(8,128)(2,1)}, bf16[512,512]{1,0:T(8,128)(2,1)}, u32[]{:S(2)}, u32[]{:S(2)}) collective-permute-start(bf16[512,512]{1,0:T(8,128)(2,1)} %get-tuple-element.547.refs_2_.refs_18_), channel_id=1, source_target_pairs={{0,4},{4,8},{8,12},{1,5},{5,9},{9,13},{2,6},{6,10},{10,14},{3,7},{... | collective-permute-start | bytes 1572872 | tf_op jit(solution)/shard_map/ppermute | solution.py:737
  78.6 11.0 %collective-permute-start.9 = (bf16[256,1024]{1,0:T(8,128)(2,1)}, bf16[256,1024]{1,0:T(8,128)(2,1)S(1)}, u32[]{:S(2)}, u32[]{:S(2)}) collective-permute-start(bf16[256,1024]{1,0:T(8,128)(2,1)} %get-tuple-element.416), channel_id=1, source_target_pairs={{0,1},{1,0},{2,3},{3,2},{4,5},{5,4},{6,7},{7,6},{8,9},{9,8},{10,11... | collective-permute-start | bytes 1572872 | tf_op jit(solution)/shard_map/ppermute | solution.py:500
  78.6 29.3 %collective-permute-start.11 = (bf16[512,768]{1,0:T(8,128)(2,1)}, bf16[512,768]{1,0:T(8,128)(2,1)S(1)}, u32[]{:S(2)}, u32[]{:S(2)}) collective-permute-start(bf16[512,768]{1,0:T(8,128)(2,1)} %refs_8_), channel_id=1, source_target_pairs={{0,16},{16,0},{1,17},{17,1},{2,18},{18,2},{3,19},{19,3},{4,20},{20... | collective-permute-start | bytes 2359304 | tf_op jit(solution)/shard_map/ppermute | solution.py:500
  82.3 18.8 %collective-permute-start.4 = (bf16[512,512]{1,0:T(8,128)(2,1)}, bf16[512,512]{1,0:T(8,128)(2,1)S(1)}, u32[]{:S(2)}, u32[]{:S(2)}) collective-permute-start(bf16[512,512]{1,0:T(8,128)(2,1)} %collective-permute-done.3.refs_6_.refs_17_), channel_id=1, source_target_pairs={{0,4},{4,8},{8,12},{1,5},{5,9},{9,13},{2,6},{6,10},{10,14},{3,7},{... | collective-permute-start | bytes 1572872 | tf_op jit(solution)/shard_map/ppermute | solution.py:742
  90.8 16.9 %collective-permute-start.10 = (bf16[256,1024]{1,0:T(8,128)(2,1)S(1)}, bf16[256,1024]{1,0:T(8,128)(2,1)S(1)}, u32[]{:S(2)}, u32[]{:S(2)}) collective-permute-start(bf16[256,1024]{1,0:T(8,128)(2,1)S(1)} %add.123), channel_id=1, source_target_pairs={{0,2},{1,3},{2,0},{3,1},{4,6},{5,7},{6,4},{7,5},{8,10},{9,11},{10,... | collective-permute-start | bytes 1572872 | tf_op jit(solution)/shard_map/ppermute | solution.py:500
  108.7 1.9 collective-permute-start.12
  108.7 5.6 %collective-permute-start.14 = (bf16[256,1024]{1,0:T(8,128)(2,1)S(1)}, bf16[256,1024]{1,0:T(8,128)(2,1)S(1)}, u32[]{:S(2)}, u32[]{:S(2)}) collective-permute-start(bf16[256,1024]{1,0:T(8,128)(2,1)S(1)} %add.124.refs_2_.refs_1_), channel_id=1, source_target_pairs={{0,1},{1,0},{2,3},{3,2},{4,5},{5,4},{6,7},{7,6},{8,9},{9,8},{10,11... | collective-permute-start | bytes 1572872 | tf_op jit(solution)/shard_map/ppermute | solution.py:500
  110.8 17.2 %collective-permute-start.13 = (bf16[256,1024]{1,0:T(8,128)(2,1)S(1)}, bf16[256,1024]{1,0:T(8,128)(2,1)S(1)}, u32[]{:S(2)}, u32[]{:S(2)}) collective-permute-start(bf16[256,1024]{1,0:T(8,128)(2,1)S(1)} %add.125), channel_id=1, source_target_pairs={{0,2},{1,3},{2,0},{3,1},{4,6},{5,7},{6,4},{7,5},{8,10},{9,11},{10,... | collective-permute-start | bytes 1572872 | tf_op jit(solution)/shard_map/ppermute | solution.py:500
  129.0 2.7 collective-permute-start.15
  131.1 14.0 %collective-permute-start.17 = (bf16[256,1024]{1,0:T(8,128)(2,1)S(1)}, bf16[256,1024]{1,0:T(8,128)(2,1)S(1)}, u32[]{:S(2)}, u32[]{:S(2)}) collective-permute-start(bf16[256,1024]{1,0:T(8,128)(2,1)S(1)} %add.127), channel_id=1, source_target_pairs={{0,2},{1,3},{2,0},{3,1},{4,6},{5,7},{6,4},{7,5},{8,10},{9,11},{10,... | collective-permute-start | bytes 1572872 | tf_op jit(solution)/shard_map/ppermute | solution.py:500
  146.3 3.6 collective-permute-start.20
  148.3 24.7 %collective-permute-start.19 = (bf16[256,1024]{1,0:T(8,128)(2,1)S(1)}, bf16[256,1024]{1,0:T(8,128)(2,1)S(1)}, u32[]{:S(2)}, u32[]{:S(2)}) collective-permute-start(bf16[256,1024]{1,0:T(8,128)(2,1)S(1)} %add.129), channel_id=1, source_target_pairs={{0,2},{1,3},{2,0},{3,1},{4,6},{5,7},{6,4},{7,5},{8,10},{9,11},{10,... | collective-permute-start | bytes 1572872 | tf_op jit(solution)/shard_map/ppermute | solution.py:500
  163.3 22.2 %collective-permute-start.22 = (bf16[512,512]{1,0:T(8,128)(2,1)}, bf16[512,512]{1,0:T(8,128)(2,1)S(1)}, u32[]{:S(2)}, u32[]{:S(2)}) collective-permute-start(bf16[512,512]{1,0:T(8,128)(2,1)} %get-tuple-element.526), channel_id=1, source_target_pairs={{4,0},{8,4},{12,8},{5,1},{9,5},{13,9},{6,2},{10,6},{14,10},{7,3},{... | collective-permute-start | bytes 1572872 | tf_op jit(solution)/shard_map/ppermute | solution.py:861
  173.2 20.7 %collective-permute-start.21 = (bf16[256,1024]{1,0:T(8,128)(2,1)S(1)}, bf16[256,1024]{1,0:T(8,128)(2,1)S(1)}, u32[]{:S(2)}, u32[]{:S(2)}) collective-permute-start(bf16[256,1024]{1,0:T(8,128)(2,1)S(1)} %add.130.refs_3_), channel_id=1, source_target_pairs={{0,1},{1,0},{2,3},{3,2},{4,5},{5,4},{6,7},{7,6},{8,9},{9,8},{10,11... | collective-permute-start | bytes 1572872 | tf_op jit(solution)/shard_map/ppermute | solution.py:500
  186.5 23.2 %collective-permute-start.23 = (bf16[512,512]{1,0:T(8,128)(2,1)}, bf16[512,512]{1,0:T(8,128)(2,1)S(1)}, u32[]{:S(2)}, u32[]{:S(2)}) collective-permute-start(bf16[512,512]{1,0:T(8,128)(2,1)} %add.131), channel_id=1, source_target_pairs={{4,0},{8,4},{12,8},{5,1},{9,5},{13,9},{6,2},{10,6},{14,10},{7,3},{... | collective-permute-start | bytes 1572872 | tf_op jit(solution)/shard_map/ppermute | solution.py:861
  187.8 57.8 %collective-permute-start.25 = (bf16[512,1536]{1,0:T(8,128)(2,1)}, bf16[512,1536]{1,0:T(8,128)(2,1)}, u32[]{:S(2)}, u32[]{:S(2)}) collective-permute-start(bf16[512,1536]{1,0:T(8,128)(2,1)} %get-tuple-element.586), channel_id=1, source_target_pairs={{0,16},{16,0},{1,17},{17,1},{2,18},{18,2},{3,19},{19,3},{4,20},{20... | collective-permute-start | bytes 4718600 | tf_op jit(solution)/shard_map/ppermute | solution.py:500
  209.6 18.8 %collective-permute-start.24 = (bf16[512,512]{1,0:T(8,128)(2,1)}, bf16[512,512]{1,0:T(8,128)(2,1)S(1)}, u32[]{:S(2)}, u32[]{:S(2)}) collective-permute-start(bf16[512,512]{1,0:T(8,128)(2,1)} %get-tuple-element.553), channel_id=1, source_target_pairs={{4,0},{8,4},{12,8},{5,1},{9,5},{13,9},{6,2},{10,6},{14,10},{7,3},{... | collective-permute-start | bytes 1572872 | tf_op jit(solution)/shard_map/ppermute | solution.py:861
  222.7 42.4 %collective-permute-start.30 = (bf16[1280,512]{1,0:T(8,128)(2,1)}, bf16[1280,512]{1,0:T(8,128)(2,1)}, u32[]{:S(2)}, u32[]{:S(2)}) collective-permute-start(bf16[1280,512]{1,0:T(8,128)(2,1)} %get-tuple-element.636), channel_id=1, source_target_pairs={{0,16},{16,0},{1,17},{17,1},{2,18},{18,2},{3,19},{19,3},{4,20},{20... | collective-permute-start | bytes 3932168 | tf_op jit(solution)/shard_map/ppermute | solution.py:500
  229.4 27.1 %collective-permute-start.27 = (bf16[512,512]{1,0:T(8,128)(2,1)}, bf16[512,512]{1,0:T(8,128)(2,1)}, u32[]{:S(2)}, u32[]{:S(2)}) collective-permute-start(bf16[512,512]{1,0:T(8,128)(2,1)} %add.132), channel_id=1, source_target_pairs={{4,0},{8,4},{12,8},{5,1},{9,5},{13,9},{6,2},{10,6},{14,10},{7,3},{... | collective-permute-start | bytes 1572872 | tf_op jit(solution)/shard_map/ppermute | solution.py:861
  230.9 36.4 %collective-permute-start.29 = (bf16[512,512]{1,0:T(8,128)(2,1)}, bf16[512,512]{1,0:T(8,128)(2,1)}, u32[]{:S(2)}, u32[]{:S(2)}) collective-permute-start(bf16[512,512]{1,0:T(8,128)(2,1)} %get-tuple-element.635), channel_id=1, source_target_pairs={{0,16},{16,0},{1,17},{17,1},{2,18},{18,2},{3,19},{19,3},{4,20},{20... | collective-permute-start | bytes 1572872 | tf_op jit(solution)/shard_map/ppermute | solution.py:500
  247.4 41.3 %collective-permute-start.26 = (bf16[512,1536]{1,0:T(8,128)(2,1)S(1)}, bf16[512,1536]{1,0:T(8,128)(2,1)}, u32[]{:S(2)}, u32[]{:S(2)}) collective-permute-start(bf16[512,1536]{1,0:T(8,128)(2,1)S(1)} %add.133), channel_id=1, source_target_pairs={{0,4},{12,8},{1,5},{13,9},{2,6},{14,10},{3,7},{15,11},{16,20},{28,... | collective-permute-start | bytes 4718600 | tf_op jit(solution)/shard_map/ppermute | solution.py:556
  265.1 3.4 collective-permute-start.28
  268.5 3.7 collective-permute-start.31
  279.5 2.9 collective-permute-start.32
  291.6 8.0 %collective-permute-start.33 = (bf16[512,1024]{1,0:T(8,128)(2,1)S(1)}, bf16[512,1024]{1,0:T(8,128)(2,1)S(1)}, u32[]{:S(2)}, u32[]{:S(2)}) collective-permute-start(bf16[512,1024]{1,0:T(8,128)(2,1)S(1)} %copy-done.24), channel_id=1, source_target_pairs={{0,1},{1,0},{2,3},{3,2},{4,5},{5,4},{6,7},{7,6},{8,9},{9,8},{10,11... | collective-permute-start | bytes 3145736 | tf_op jit(solution)/shard_map/ppermute | solution.py:500
  291.6 25.6 %collective-permute-start.39 = (bf16[512,1024]{1,0:T(8,128)(2,1)S(1)}, bf16[512,1024]{1,0:T(8,128)(2,1)S(1)}, u32[]{:S(2)}, u32[]{:S(2)}) collective-permute-start(bf16[512,1024]{1,0:T(8,128)(2,1)S(1)} %add.142), channel_id=1, source_target_pairs={{0,2},{1,3},{2,0},{3,1},{4,6},{5,7},{6,4},{7,5},{8,10},{9,11},{10,... | collective-permute-start | bytes 3145736 | tf_op jit(solution)/shard_map/ppermute | solution.py:500
  292.1 32.9 %collective-permute-start.38 = (bf16[1280,512]{1,0:T(8,128)(2,1)S(1)}, bf16[1280,512]{1,0:T(8,128)(2,1)}, u32[]{:S(2)}, u32[]{:S(2)}) collective-permute-start(bf16[1280,512]{1,0:T(8,128)(2,1)S(1)} %add.138), channel_id=1, source_target_pairs={{0,4},{12,8},{1,5},{13,9},{2,6},{14,10},{3,7},{15,11},{16,20},{28,... | collective-permute-start | bytes 3932168 | tf_op jit(solution)/shard_map/ppermute | solution.py:556
  297.8 42.8 %collective-permute-start.37 = (bf16[512,1536]{1,0:T(8,128)(2,1)}, bf16[512,1536]{1,0:T(8,128)(2,1)}, u32[]{:S(2)}, u32[]{:S(2)}) collective-permute-start(bf16[512,1536]{1,0:T(8,128)(2,1)} %add.143), channel_id=1, source_target_pairs={{4,8},{8,4},{5,9},{9,5},{6,10},{10,6},{7,11},{11,7},{20,24},{24,20... | collective-permute-start | bytes 4718600 | tf_op jit(solution)/shard_map/ppermute | solution.py:559
  317.6 2.9 collective-permute-start.40
  317.7 40.0 %collective-permute-start.34 = (bf16[512,1024]{1,0:T(8,128)(2,1)}, bf16[512,1024]{1,0:T(8,128)(2,1)}, u32[]{:S(2)}, u32[]{:S(2)}) collective-permute-start(bf16[512,1024]{1,0:T(8,128)(2,1)} %add.144), channel_id=1, source_target_pairs={{0,2},{1,3},{2,0},{3,1},{4,6},{5,7},{6,4},{7,5},{8,10},{9,11},{10,... | collective-permute-start | bytes 3145736 | tf_op jit(solution)/shard_map/ppermute | solution.py:500
  327.8 36.5 %collective-permute-start.43 = (bf16[1280,512]{1,0:T(8,128)(2,1)}, bf16[1280,512]{1,0:T(8,128)(2,1)}, u32[]{:S(2)}, u32[]{:S(2)}) collective-permute-start(bf16[1280,512]{1,0:T(8,128)(2,1)} %add.146), channel_id=1, source_target_pairs={{4,8},{8,4},{5,9},{9,5},{6,10},{10,6},{7,11},{11,7},{20,24},{24,20... | collective-permute-start | bytes 3932168 | tf_op jit(solution)/shard_map/ppermute | solution.py:559
  329.7 22.7 %collective-permute-start.35 = (bf16[528,512]{1,0:T(8,128)(2,1)S(1)}, bf16[528,512]{1,0:T(8,128)(2,1)S(1)}, u32[]{:S(2)}, u32[]{:S(2)}) collective-permute-start(bf16[528,512]{1,0:T(8,128)(2,1)S(1)} %copy-done.38), channel_id=1, source_target_pairs={{0,16},{16,0},{1,17},{17,1},{2,18},{18,2},{3,19},{19,3},{4,20},{20... | collective-permute-start | bytes 1622024 | tf_op jit(solution)/shard_map/ppermute | solution.py:500
  331.4 20.1 %collective-permute-start.36 = (bf16[512,512]{1,0:T(8,128)(2,1)S(1)}, bf16[512,512]{1,0:T(8,128)(2,1)S(1)}, u32[]{:S(2)}, u32[]{:S(2)}) collective-permute-start(bf16[512,512]{1,0:T(8,128)(2,1)S(1)} %add.139), channel_id=1, source_target_pairs={{0,4},{12,8},{1,5},{13,9},{2,6},{14,10},{3,7},{15,11},{16,20},{28,... | collective-permute-start | bytes 1572872 | tf_op jit(solution)/shard_map/ppermute | solution.py:556
  342.9 40.3 %collective-permute-start.44 = (bf16[512,1536]{1,0:T(8,128)(2,1)S(1)}, bf16[512,1536]{1,0:T(8,128)(2,1)}, u32[]{:S(2)}, u32[]{:S(2)}) collective-permute-start(bf16[512,1536]{1,0:T(8,128)(2,1)S(1)} %add.147), channel_id=1, source_target_pairs={{4,0},{8,12},{5,1},{9,13},{6,2},{10,14},{7,3},{11,15},{20,16},{24,... | collective-permute-start | bytes 4718600 | tf_op jit(solution)/shard_map/ppermute | solution.py:564
  352.5 15.0 %collective-permute-start.42 = (bf16[528,512]{1,0:T(8,128)(2,1)S(1)}, bf16[528,512]{1,0:T(8,128)(2,1)}, u32[]{:S(2)}, u32[]{:S(2)}) collective-permute-start(bf16[528,512]{1,0:T(8,128)(2,1)S(1)} %add.149), channel_id=1, source_target_pairs={{0,4},{12,8},{1,5},{13,9},{2,6},{14,10},{3,7},{15,11},{16,20},{28,... | collective-permute-start | bytes 1622024 | tf_op jit(solution)/shard_map/ppermute | solution.py:556
  359.7 13.4 %collective-permute-start.41 = (bf16[512,1024]{1,0:T(8,128)(2,1)S(1)}, bf16[512,1024]{1,0:T(8,128)(2,1)}, u32[]{:S(2)}, u32[]{:S(2)}) collective-permute-start(bf16[512,1024]{1,0:T(8,128)(2,1)S(1)} %add.150.refs_3_), channel_id=1, source_target_pairs={{0,1},{1,0},{2,3},{3,2},{4,5},{5,4},{6,7},{7,6},{8,9},{9,8},{10,11... | collective-permute-start | bytes 3145736 | tf_op jit(solution)/shard_map/ppermute | solution.py:500
  368.7 12.0 %collective-permute-start.45 = (bf16[528,512]{1,0:T(8,128)(2,1)S(1)}, bf16[528,512]{1,0:T(8,128)(2,1)}, u32[]{:S(2)}, u32[]{:S(2)}) collective-permute-start(bf16[528,512]{1,0:T(8,128)(2,1)S(1)} %add.152), channel_id=1, source_target_pairs={{4,8},{8,4},{5,9},{9,5},{6,10},{10,6},{7,11},{11,7},{20,24},{24,20... | collective-permute-start | bytes 1622024 | tf_op jit(solution)/shard_map/ppermute | solution.py:559
  370.1 7.1 %collective-permute-start.46 = (bf16[512,512]{1,0:T(8,128)(2,1)}, bf16[512,512]{1,0:T(8,128)(2,1)}, u32[]{:S(2)}, u32[]{:S(2)}) collective-permute-start(bf16[512,512]{1,0:T(8,128)(2,1)} %add.148), channel_id=1, source_target_pairs={{4,8},{8,4},{5,9},{9,5},{6,10},{10,6},{7,11},{11,7},{20,24},{24,20... | collective-permute-start | bytes 1572872 | tf_op jit(solution)/shard_map/ppermute | solution.py:559
  371.6 38.4 %collective-permute-start.49 = (bf16[1280,512]{1,0:T(8,128)(2,1)}, bf16[1280,512]{1,0:T(8,128)(2,1)}, u32[]{:S(2)}, u32[]{:S(2)}) collective-permute-start(bf16[1280,512]{1,0:T(8,128)(2,1)} %add.151), channel_id=1, source_target_pairs={{4,0},{8,12},{5,1},{9,13},{6,2},{10,14},{7,3},{11,15},{20,16},{24,... | collective-permute-start | bytes 3932168 | tf_op jit(solution)/shard_map/ppermute | solution.py:564
  379.4 41.9 %collective-permute-start.48 = (bf16[512,512]{1,0:T(8,128)(2,1)}, bf16[512,512]{1,0:T(8,128)(2,1)}, u32[]{:S(2)}, u32[]{:S(2)}) collective-permute-start(bf16[512,512]{1,0:T(8,128)(2,1)} %add.153), channel_id=1, source_target_pairs={{4,0},{8,12},{5,1},{9,13},{6,2},{10,14},{7,3},{11,15},{20,16},{24,... | collective-permute-start | bytes 1572872 | tf_op jit(solution)/shard_map/ppermute | solution.py:564
  381.9 49.5 %collective-permute-start.47 = (bf16[528,512]{1,0:T(8,128)(2,1)S(1)}, bf16[528,512]{1,0:T(8,128)(2,1)S(1)}, u32[]{:S(2)}, u32[]{:S(2)}) collective-permute-start(bf16[528,512]{1,0:T(8,128)(2,1)S(1)} %add.154), channel_id=1, source_target_pairs={{4,0},{8,12},{5,1},{9,13},{6,2},{10,14},{7,3},{11,15},{20,16},{24,... | collective-permute-start | bytes 1622024 | tf_op jit(solution)/shard_map/ppermute | solution.py:564
  (47 other events, 256.7 us)

commit v2 on v1

--- a/solution.py
+++ b/solution.py
@@ -1017,6 +1017,7 @@
     attend(0)
     line.wait(gate_w[-1])
     branch[0]()
+    line.wait(low_grad, valid)
     attend(1)
     branch[0]()
     line.wait(up_w[-1])

time: 442 us -> 442 us (level)
  Pallas kernels: 163 us -> 168 us
    ppermute x30, starting transfers between devices: 32.2 us -> 26.5 us  [swap(): return lax.ppermute(values, axis, [(i, i ^ bit) for i in range(size)])]
    ppermute x4, starting transfers between devices: 29.2 us -> 33.7 us  [sum_line(): came = lax.ppermute(total, axis, [(i, i + 1), (size - 1 - i, size - 2 - i)])]
    pallas_call x25, Pallas kernels: 163 us -> 168 us  [call(): pl.pallas_call(body_, name=name, out_shape=[o[0] for o in outs], grid_spe...]
  transfers between devices with their start and end apart: 50 -> 50, of which waited for: 17 -> 18; matrix products, arithmetic and copies ran while one was open for 14% -> 14% of each run, Pallas kernels for 38% -> 39%
where the time goes in v2:
time: 442 us; the launch traced here: 433 us
  Pallas kernels  168 us (38%)
  starting transfers between devices  98.2 us (22%)
  waiting for transfers between devices  91.1 us (21%)
  other arithmetic  57.8 us (13%)
  local copies, waits for them, and re-layouts  16.4 us (4%)
    pallas_call x25, Pallas kernels, call(): pl.pallas_call(body_, name=name, out_shape=[o[0] for o in outs], grid_spe...  168 us
    ppermute x4, waiting for transfers between devices, sum_line(): came = lax.ppermute(total, axis, [(i + 1, i), (size - 2 - i, size - 1 - i)])  34.8 us
    ppermute x4, starting transfers between devices, sum_line(): came = lax.ppermute(total, axis, [(i, i + 1), (size - 1 - i, size - 2 - i)])  33.7 us
    ppermute x30, waiting for transfers between devices, swap(): return lax.ppermute(values, axis, [(i, i ^ bit) for i in range(size)])  32.8 us
    add x26, other arithmetic, plus(): return a + b  32.4 us
    ppermute x30, starting transfers between devices, swap(): return lax.ppermute(values, axis, [(i, i ^ bit) for i in range(size)])  26.5 us
    ppermute x2, starting transfers between devices, forward(): kv[s].insert(0, lax.ppermute(line.after(kv[s][0]), 'ctx', up_perm))  12.3 us
    ppermute x4, waiting for transfers between devices, sum_line(): came = lax.ppermute(total, axis, [(i, i + 1), (size - 1 - i, size - 2 - i)])  10.7 us
  transfers between devices with their start and end apart: 50, of which 18 were waited for; matrix products, arithmetic and copies ran while one was open for 14% of the time, Pallas kernels for 39%

profile of v2, /device:TPU:0, one launch (start us, length us, event | category | flops | bytes accessed | tf_op | source)
XLA Modules:
  0.0 432.9 jit_solution(6263828158964147674)
XLA Ops:
  2.7 3.0 collective-permute-start.1
  20.8 4.6 %keys.2 = (bf16[512,1024]{1,0:T(8,128)(2,1)}, bf16[512,512]{1,0:T(8,128)(2,1)}, f32[512,256]{1,0:T(8,128)}, bf16[1280,512]{1,0:T(8,128)(2,1)}) custom-call(s32[4]{0:T(128)} %pad_add_fusion.2.ids, bf16[2,512,1024]{2,1,0:T(8,128)(2,1)} %refs_0_.10, f32[1,1024]{1,0:T(1,128)} %get-tuple-element.686.refs_1_.refs_2_.refs_4_, ...), custom_call_target="tpu_custom_call", output_to_operand_aliasing={{3}: (8, {})} | custom-call | flops 1 | bytes 1 | tf_op jit(solution)/shard_map/keys/pallas_call | solution.py:65
  29.8 4.0 collective-permute-start.7
  36.0 4.5 %keys.3 = (bf16[512,1024]{1,0:T(8,128)(2,1)}, bf16[512,512]{1,0:T(8,128)(2,1)}, f32[512,256]{1,0:T(8,128)}) custom-call(s32[4]{0:T(128)} %pad_add_fusion.ids, bf16[512,512]{1,0:T(8,128)(2,1)} %copy-done.3, bf16[2,512,1024]{2,1,0:T(8,128)(2,1)} %refs_0_.10, f32[1,1024]{1,0:T(1,128)} %get-tuple-element.686.refs_1_.refs_2_.refs_4_, ...), custom_call_target="tpu_custom_call" | custom-call | flops 1 | bytes 1 | tf_op jit(solution)/shard_map/keys/pallas_call | solution.py:65
  43.3 4.3 collective-permute-start.8
  48.8 4.2 collective-permute-start.3
  53.1 4.4 %query.2 = (bf16[512,512]{1,0:T(8,128)(2,1)}, f32[512,512]{1,0:T(8,128)}) custom-call(s32[4]{0:T(128)} %pad_add_fusion.2.ids, bf16[512,1024]{1,0:T(8,128)(2,1)} %get-tuple-element.649.refs_0_, f32[2,512,128]{2,1,0:T(8,128)} %get-tuple-element.619.refs_2_.refs_3_.refs_1_.refs_13_.refs_6_, ...), custom_call_target="tpu_custom_call" | custom-call | flops 1 | bytes 1 | tf_op jit(solution)/shard_map/query/pallas_call | solution.py:65
  57.4 4.4 %query.3 = (bf16[512,512]{1,0:T(8,128)(2,1)}, f32[512,512]{1,0:T(8,128)}) custom-call(s32[4]{0:T(128)} %pad_add_fusion.ids, bf16[512,1024]{1,0:T(8,128)(2,1)} %get-tuple-element.650.refs_0_.refs_1_, f32[2,512,128]{2,1,0:T(8,128)} %get-tuple-element.619.refs_2_.refs_3_.refs_1_.refs_13_.refs_6_, ...), custom_call_target="tpu_custom_call" | custom-call | flops 1 | bytes 1 | tf_op jit(solution)/shard_map/query/pallas_call | solution.py:65
  61.8 5.9 %attend_own.2 = (f32[512,512]{1,0:T(8,128)}, f32[8,512]{1,0:T(8,128)}) custom-call(s32[4]{0:T(128)} %pad_add_fusion.2.ids, bf16[512,512]{1,0:T(8,128)(2,1)} %get-tuple-element.499.refs_0_.refs_10_, s32[2,1,512]{2,1,0:T(1,128)} %broadcast_in_dim.36.refs_1_.refs_4_.refs_11_, bf16[512,512]{1,0:T(8,128)(2,1)} %get-tuple-element.507.refs_2_.refs_18_), custom_call_target="tpu_custom_call" | custom-call | flops 1 | bytes 1 | tf_op jit(solution)/shard_map/attend_own/pallas_call | solution.py:65
  67.8 6.0 %attend_own.3 = (f32[512,512]{1,0:T(8,128)}, f32[8,512]{1,0:T(8,128)}) custom-call(s32[4]{0:T(128)} %pad_add_fusion.ids, bf16[512,512]{1,0:T(8,128)(2,1)} %get-tuple-element.543.refs_0_.refs_3_.refs_10_, s32[2,1,512]{2,1,0:T(1,128)} %broadcast_in_dim.36.refs_1_.refs_4_.refs_11_, bf16[512,512]{1,0:T(8,128)(2,1)} %get-tuple-element.551.refs_2_.refs_18_), custom_call_target="tpu_custom_call" | custom-call | flops 1 | bytes 1 | tf_op jit(solution)/shard_map/attend_own/pallas_call | solution.py:65
  75.0 5.8 %attend.2 = (bf16[256,1024]{1,0:T(8,128)(2,1)}, bf16[256,1024]{1,0:T(8,128)(2,1)}, bf16[512,512]{1,0:T(8,128)(2,1)}, f32[8,512]{1,0:T(8,128)}) custom-call(s32[4]{0:T(128)} %pad_add_fusion.2.ids, bf16[512,512]{1,0:T(8,128)(2,1)} %get-tuple-element.499.refs_0_.refs_10_, s32[2,1,512]{2,1,0:T(1,128)} %broadcast_in_dim.36.refs_1_.refs_4_.refs_11_, ...), custom_call_target="tpu_custom_call" | custom-call | flops 1 | bytes 1 | tf_op jit(solution)/shard_map/attend/pallas_call | solution.py:65
  82.4 8.0 %collective-permute-start.4 = (bf16[512,512]{1,0:T(8,128)(2,1)}, bf16[512,512]{1,0:T(8,128)(2,1)}, u32[]{:S(2)}, u32[]{:S(2)}) collective-permute-start(bf16[512,512]{1,0:T(8,128)(2,1)} %collective-permute-done.3.refs_8_.refs_17_), channel_id=1, source_target_pairs={{0,4},{4,8},{8,12},{1,5},{5,9},{9,13},{2,6},{6,10},{10,14},{3,7},{... | collective-permute-start | bytes 1572872 | tf_op jit(solution)/shard_map/ppermute | solution.py:742
  95.1 6.0 %collective-permute-done.4.refs_7_.refs_16_ = bf16[512,512]{1,0:T(8,128)(2,1)} collective-permute-done((bf16[512,512]{1,0:T(8,128)(2,1)}, bf16[512,512]{1,0:T(8,128)(2,1)}, u32[]{:S(2)}, u32[]{:S(2)}) %collective-permute-start.4) | collective-permute-done | bytes 524320 | tf_op jit(solution)/shard_map/ppermute | solution.py:742
  102.2 5.7 %attend.3 = (bf16[256,1024]{1,0:T(8,128)(2,1)}, bf16[256,1024]{1,0:T(8,128)(2,1)}, bf16[512,512]{1,0:T(8,128)(2,1)}, f32[8,512]{1,0:T(8,128)}) custom-call(s32[4]{0:T(128)} %pad_add_fusion.ids, bf16[512,768]{1,0:T(8,128)(2,1)} %collective-permute-done.6.refs_0_.refs_8_.refs_7_, bf16[2,512,1024]{2,1,0:T(8,128)(2,1)} %fusion.refs_1_.refs_6_.refs_5_, ...), custom_call_target="tpu_custom_call" | custom-call | flops 1 | bytes 1 | tf_op jit(solution)/shard_map/attend/pallas_call | solution.py:65
  113.8 12.6 %ffn.2 = (bf16[512,1024]{1,0:T(8,128)(2,1)}, bf16[512,768]{1,0:T(8,128)(2,1)}, bf16[512,768]{1,0:T(8,128)(2,1)}, bf16[512,768]{1,0:T(8,128)(2,1)}, bf16[256,1024...) custom-call(s32[4]{0:T(128)} %pad_add_fusion.2.ids, bf16[512,768]{1,0:T(8,128)(2,1)} %copy-done.10, ...), custom_call_target="tpu_custom_call" | custom-call | flops 1 | bytes 1 | tf_op jit(solution)/shard_map/ffn/pallas_call | solution.py:65
  130.9 12.6 %ffn.3 = (bf16[512,1024]{1,0:T(8,128)(2,1)}, bf16[512,768]{1,0:T(8,128)(2,1)}, bf16[512,768]{1,0:T(8,128)(2,1)}, bf16[512,768]{1,0:T(8,128)(2,1)}, bf16[256,1024...) custom-call(s32[4]{0:T(128)} %pad_add_fusion.ids, bf16[2,512,1024]{2,1,0:T(8,128)(2,1)} %refs_0_.10, ...), custom_call_target="tpu_custom_call" | custom-call | flops 1 | bytes 1 | tf_op jit(solution)/shard_map/ffn/pallas_call | solution.py:65
  149.0 15.1 %attend_back.2 = (f32[512,1024]{1,0:T(8,128)}, bf16[512,1024]{1,0:T(8,128)(2,1)}, bf16[512,512]{1,0:T(8,128)(2,1)}, f32[1,128]{1,0:T(1,128)}, bf16[512,512]{1,0:...) custom-call(s32[4]{0:T(128)} %pad_add_fusion.2.ids, bf16[2,512,1024]{2,1,0:T(8,128)(2,1)} %refs_0_.10, ...), custom_call_target="tpu_custom_call" | custom-call | flops 1 | bytes 1 | tf_op jit(solution)/shard_map/attend_back/pallas_call | solution.py:65
  165.4 8.3 %gate_up_grad.1 = (bf16[512,1536]{1,0:T(8,128)(2,1)}, bf16[512,1536]{1,0:T(8,128)(2,1)}) custom-call(s32[4]{0:T(128)} %pad_add_fusion.2.ids, bf16[512,1024]{1,0:T(8,128)(2,1)} %get-tuple-element.511.refs_0_, bf16[512,1024]{1,0:T(8,128)(2,1)} %get-tuple-element.512.refs_1_, bf16[512,768]{1,0:T(8,128)(2,1)} %get-tuple-element.513.refs_2_, ...), custom_call_target="tpu_custom_call" | custom-call | flops 1 | bytes 1 | tf_op jit(solution)/shard_map/gate_up_grad/pallas_call | solution.py:65
  174.0 4.9 %down.2 = (bf16[512,1024]{1,0:T(8,128)(2,1)}, bf16[512,1024]{1,0:T(8,128)(2,1)}) custom-call(s32[4]{0:T(128)} %pad_add_fusion.2.ids, bf16[512,768]{1,0:T(8,128)(2,1)} %get-tuple-element.563.refs_0_.refs_1_, bf16[1280,512]{1,0:T(8,128)(2,1)} %get-tuple-element.584.refs_6_.refs_9_.refs_11_.refs_10_.refs_19_.refs_1_, bf16[1280,512]{1,0:T(8,128)(2,1)} %copy-done), custom_call_target="tpu_custom_call" | custom-call | flops 1 | bytes 1 | tf_op jit(solution)/shard_map/down/pallas_call | solution.py:65
  178.9 4.0 collective-permute-done.22
  185.1 5.0 %collective-permute-start.25 = (bf16[512,1536]{1,0:T(8,128)(2,1)}, bf16[512,1536]{1,0:T(8,128)(2,1)}, u32[]{:S(2)}, u32[]{:S(2)}) collective-permute-start(bf16[512,1536]{1,0:T(8,128)(2,1)} %get-tuple-element.590), channel_id=1, source_target_pairs={{0,16},{16,0},{1,17},{17,1},{2,18},{18,2},{3,19},{19,3},{4,20},{20... | collective-permute-start | bytes 4718600 | tf_op jit(solution)/shard_map/ppermute | solution.py:500
  191.0 15.0 %attend_back.3 = (f32[512,1024]{1,0:T(8,128)}, bf16[512,1024]{1,0:T(8,128)(2,1)}, bf16[512,512]{1,0:T(8,128)(2,1)}, f32[1,128]{1,0:T(1,128)}, bf16[512,512]{1,0:...) custom-call(s32[4]{0:T(128)} %pad_add_fusion.ids, bf16[2,512,1024]{2,1,0:T(8,128)(2,1)} %refs_0_.10, ...), custom_call_target="tpu_custom_call" | custom-call | flops 1 | bytes 1 | tf_op jit(solution)/shard_map/attend_back/pallas_call | solution.py:65
  208.7 5.7 %down_grad.1 = (bf16[1280,512]{1,0:T(8,128)(2,1)}, bf16[1280,512]{1,0:T(8,128)(2,1)}) custom-call(s32[4]{0:T(128)} %pad_add_fusion.2.ids, bf16[512,512]{1,0:T(8,128)(2,1)} %copy-done.21, bf16[512,768]{1,0:T(8,128)(2,1)} %get-tuple-element.563.refs_0_.refs_1_, bf16[512,768]{1,0:T(8,128)(2,1)} %get-tuple-element.583.refs_2_.refs_0_, ...), custom_call_target="tpu_custom_call" | custom-call | flops 1 | bytes 1 | tf_op jit(solution)/shard_map/down_grad/pallas_call | solution.py:65
  214.5 4.6 %out_grad.1 = (bf16[1280,512]{1,0:T(8,128)(2,1)}, bf16[1280,512]{1,0:T(8,128)(2,1)}) custom-call(s32[4]{0:T(128)} %pad_add_fusion.2.ids, bf16[512,512]{1,0:T(8,128)(2,1)} %get-tuple-element.569.refs_8_.refs_0_, bf16[512,512]{1,0:T(8,128)(2,1)} %get-tuple-element.570.refs_8_.refs_1_, ...), custom_call_target="tpu_custom_call", output_to_operand_aliasing={{0}: (5, {}), {1}: (6, {})} | custom-call | flops 1 | bytes 1 | tf_op jit(solution)/shard_map/out_grad/pallas_call | solution.py:65
  219.9 5.7 %query_grad.1 = (bf16[512,512]{1,0:T(8,128)(2,1)}, bf16[512,512]{1,0:T(8,128)(2,1)}) custom-call(s32[4]{0:T(128)} %pad_add_fusion.2.ids, bf16[512,1024]{1,0:T(8,128)(2,1)} %get-tuple-element.649.refs_0_, bf16[512,1024]{1,0:T(8,128)(2,1)} %get-tuple-element.650.refs_0_.refs_1_, bf16[512,512]{1,0:T(8,128)(2,1)} %get-tuple-element.595.refs_2_, ...), custom_call_target="tpu_custom_call" | custom-call | flops 1 | bytes 1 | tf_op jit(solution)/shard_map/query_grad/pallas_call | solution.py:65
  229.5 4.7 %down.3 = (bf16[512,1024]{1,0:T(8,128)(2,1)}, bf16[512,1024]{1,0:T(8,128)(2,1)}) custom-call(s32[4]{0:T(128)} %pad_add_fusion.ids, bf16[512,768]{1,0:T(8,128)(2,1)} %get-tuple-element.583.refs_2_.refs_0_, bf16[1280,512]{1,0:T(8,128)(2,1)} %get-tuple-element.584.refs_6_.refs_9_.refs_11_.refs_10_.refs_19_.refs_1_, ...), custom_call_target="tpu_custom_call", output_to_operand_aliasing={{0}: (4, {}), {1}: (5, {})} | custom-call | flops 1 | bytes 1 | tf_op jit(solution)/shard_map/down/pallas_call | solution.py:65
  234.3 7.2 %input_back.2 = (bf16[512,512]{1,0:T(8,128)(2,1)}, bf16[512,1024]{1,0:T(8,128)(2,1)}, bf16[512,1024]{1,0:T(8,128)(2,1)}, f32[1,128]{1,0:T(1,128)}, f32[1,1024]{1,0:T(1,128)}) custom-call(s32[4]{0:T(128)} %pad_add_fusion.2.ids, bf16[2,512,1024]{2,1,0:T(8,128)(2,1)} %refs_0_.10, f32[1,1024]{1,0:T(1,128)} %get-tuple-element.686.refs_1_.refs_2_.refs_4_, ...), custom_call_target="tpu_custom_call" | custom-call | flops 1 | bytes 1 | tf_op jit(solution)/shard_map/input_back/pallas_call | solution.py:65
  243.3 11.1 %collective-permute-start.26 = (bf16[512,1536]{1,0:T(8,128)(2,1)S(1)}, bf16[512,1536]{1,0:T(8,128)(2,1)}, u32[]{:S(2)}, u32[]{:S(2)}) collective-permute-start(bf16[512,1536]{1,0:T(8,128)(2,1)S(1)} %add.133), channel_id=1, source_target_pairs={{0,4},{12,8},{1,5},{13,9},{2,6},{14,10},{3,7},{15,11},{16,20},{28,... | collective-permute-start | bytes 4718600 | tf_op jit(solution)/shard_map/ppermute | solution.py:556
  254.4 7.2 %input_back.3 = (bf16[512,512]{1,0:T(8,128)(2,1)}, bf16[512,1024]{1,0:T(8,128)(2,1)}, bf16[512,1024]{1,0:T(8,128)(2,1)}, f32[1,128]{1,0:T(1,128)}, f32[1,1024]{1,0:T(1,128)}) custom-call(s32[4]{0:T(128)} %pad_add_fusion.ids, bf16[2,512,1024]{2,1,0:T(8,128)(2,1)} %refs_0_.10, ...), custom_call_target="tpu_custom_call", output_to_operand_aliasing={{1}: (14, {}), {2}: (15, {})} | custom-call | flops 1 | bytes 1 | tf_op jit(solution)/shard_map/input_back/pallas_call | solution.py:65
  267.8 3.2 collective-permute-done.31
  272.6 5.6 %kv_grad.1 = (bf16[528,512]{1,0:T(8,128)(2,1)}, bf16[528,512]{1,0:T(8,128)(2,1)}) custom-call(s32[4]{0:T(128)} %pad_add_fusion.2.ids, bf16[512,1024]{1,0:T(8,128)(2,1)} %get-tuple-element.649.refs_0_, bf16[512,1024]{1,0:T(8,128)(2,1)} %get-tuple-element.650.refs_0_.refs_1_, bf16[512,512]{1,0:T(8,128)(2,1)} %get-tuple-element.651.refs_2_, ...), custom_call_target="tpu_custom_call" | custom-call | flops 1 | bytes 1 | tf_op jit(solution)/shard_map/kv_grad/pallas_call | solution.py:65
  278.2 2.9 collective-permute-done.32
  282.7 3.4 collective-permute-done.26
  286.2 2.9 add.143
  289.3 5.7 %collective-permute-start.38 = (bf16[1280,512]{1,0:T(8,128)(2,1)S(1)}, bf16[1280,512]{1,0:T(8,128)(2,1)}, u32[]{:S(2)}, u32[]{:S(2)}) collective-permute-start(bf16[1280,512]{1,0:T(8,128)(2,1)S(1)} %add.138), channel_id=1, source_target_pairs={{0,4},{12,8},{1,5},{13,9},{2,6},{14,10},{3,7},{15,11},{16,20},{28,... | collective-permute-start | bytes 3932168 | tf_op jit(solution)/shard_map/ppermute | solution.py:556
  297.2 17.4 %collective-permute-done.39 = bf16[512,1024]{1,0:T(8,128)(2,1)S(1)} collective-permute-done((bf16[512,1024]{1,0:T(8,128)(2,1)S(1)}, bf16[512,1024]{1,0:T(8,128)(2,1)S(1)}, u32[]{:S(2)}, u32[]{:S(2)}) %collective-permute-start.39) | collective-permute-done | bytes 1048608 | tf_op jit(solution)/shard_map/ppermute | solution.py:500
  318.0 4.5 %input_grad.2.refs_5_ = f32[2,512,1024]{2,1,0:T(8,128)} custom-call(s32[4]{0:T(128)} %pad_add_fusion.2.ids, bf16[2,512,1024]{2,1,0:T(8,128)(2,1)} %refs_0_.10, f32[512,1024]{1,0:T(8,128)} %get-tuple-element.668.refs_1_, bf16[512,1024]{1,0:T(8,128)(2,1)} %copy-done.6, bf16[512,1024]{1,0:T(8,128)(2,1)} %collective-permute-done.40.refs_3_, ...), custom_call_target="tpu_custom_call" | custom-call | flops 1 | bytes 1 | tf_op jit(solution)/shard_map/input_grad/pallas_call | solution.py:65
  322.5 2.8 add.146
  327.8 11.8 %collective-permute-start.36 = (bf16[512,512]{1,0:T(8,128)(2,1)S(1)}, bf16[512,512]{1,0:T(8,128)(2,1)S(1)}, u32[]{:S(2)}, u32[]{:S(2)}) collective-permute-start(bf16[512,512]{1,0:T(8,128)(2,1)S(1)} %copy-done.18), channel_id=1, source_target_pairs={{0,4},{12,8},{1,5},{13,9},{2,6},{14,10},{3,7},{15,11},{16,20},{28,... | collective-permute-start | bytes 1572872 | tf_op jit(solution)/shard_map/ppermute | solution.py:556
  343.3 7.1 %collective-permute-done.36 = bf16[512,512]{1,0:T(8,128)(2,1)S(1)} collective-permute-done((bf16[512,512]{1,0:T(8,128)(2,1)S(1)}, bf16[512,512]{1,0:T(8,128)(2,1)S(1)}, u32[]{:S(2)}, u32[]{:S(2)}) %collective-permute-start.36) | collective-permute-done | bytes 524320 | tf_op jit(solution)/shard_map/ppermute | solution.py:556
  351.5 5.2 %collective-permute-start.42 = (bf16[528,512]{1,0:T(8,128)(2,1)S(1)}, bf16[528,512]{1,0:T(8,128)(2,1)}, u32[]{:S(2)}, u32[]{:S(2)}) collective-permute-start(bf16[528,512]{1,0:T(8,128)(2,1)S(1)} %add.149), channel_id=1, source_target_pairs={{0,4},{12,8},{1,5},{13,9},{2,6},{14,10},{3,7},{15,11},{16,20},{28,... | collective-permute-start | bytes 1622024 | tf_op jit(solution)/shard_map/ppermute | solution.py:556
  358.4 4.5 %input_grad.3 = f32[2,512,1024]{2,1,0:T(8,128)} custom-call(s32[4]{0:T(128)} %pad_add_fusion.ids, bf16[2,512,1024]{2,1,0:T(8,128)(2,1)} %refs_0_.10, f32[512,1024]{1,0:T(8,128)} %get-tuple-element.683.refs_1_, bf16[512,1024]{1,0:T(8,128)(2,1)} %copy-done.6, bf16[512,1024]{1,0:T(8,128)(2,1)} %collective-permute-done.40.refs_3_, ...), custom_call_target="tpu_custom_call", output_to_operand_aliasing={{}: (6, {})} | custom-call | flops 1 | bytes 1 | tf_op jit(solution)/shard_map/input_grad/pallas_call | solution.py:65
  362.9 3.2 add.151
  372.0 4.1 layer_out.2.refs_6_
  385.5 4.1 layer_out.3
  389.6 19.8 %collective-permute-done.49 = bf16[1280,512]{1,0:T(8,128)(2,1)} collective-permute-done((bf16[1280,512]{1,0:T(8,128)(2,1)}, bf16[1280,512]{1,0:T(8,128)(2,1)}, u32[]{:S(2)}, u32[]{:S(2)}) %collective-permute-start.49) | collective-permute-done | bytes 1310752 | tf_op jit(solution)/shard_map/ppermute | solution.py:564
  412.2 8.4 %collective-permute-done.48 = bf16[512,512]{1,0:T(8,128)(2,1)} collective-permute-done((bf16[512,512]{1,0:T(8,128)(2,1)}, bf16[512,512]{1,0:T(8,128)(2,1)}, u32[]{:S(2)}, u32[]{:S(2)}) %collective-permute-start.48) | collective-permute-done | bytes 524320 | tf_op jit(solution)/shard_map/ppermute | solution.py:564
  423.8 6.6 %collective-permute-done.47 = bf16[528,512]{1,0:T(8,128)(2,1)S(1)} collective-permute-done((bf16[528,512]{1,0:T(8,128)(2,1)S(1)}, bf16[528,512]{1,0:T(8,128)(2,1)S(1)}, u32[]{:S(2)}, u32[]{:S(2)}) %collective-permute-start.47) | collective-permute-done | bytes 540704 | tf_op jit(solution)/shard_map/ppermute | solution.py:564
  (254 shorter events, 113.5 us)
Async XLA Ops:
  2.7 17.3 %collective-permute-start.1 = (bf16[512,512]{1,0:T(8,128)(2,1)S(1)}, bf16[512,512]{1,0:T(8,128)(2,1)S(1)}, u32[]{:S(2)}, u32[]{:S(2)}) collective-permute-start(bf16[512,512]{1,0:T(8,128)(2,1)S(1)} %constant_dynamic-update-slice_fusion.refs_5_.refs_6_.refs_11_), channel_id=1, source_target_pairs={{0,16},{16,0},{1,17},{17,1},{2,18},{18,2},{3,19},{19,3},{4,20},{20... | collective-permute-start | bytes 1572872 | tf_op jit(solution)/shard_map/ppermute | solution.py:500
  7.9 10.9 %collective-permute-start = (bf16[3,512]{1,0:T(4,128)(2,1)S(1)}, bf16[3,512]{1,0:T(4,128)(2,1)S(1)}, u32[]{:S(2)}, u32[]{:S(2)}) collective-permute-start(bf16[3,512]{1,0:T(4,128)(2,1)S(1)} %pad_maximum_fusion.5), channel_id=1, source_target_pairs={{0,16},{16,0},{1,17},{17,1},{2,18},{18,2},{3,19},{19,3},{4,20},{20... | collective-permute-start | bytes 9224 | tf_op jit(solution)/shard_map/ppermute | solution.py:500
  8.0 21.8 %collective-permute-start.2 = (bf16[512,512]{1,0:T(8,128)(2,1)}, bf16[512,512]{1,0:T(8,128)(2,1)S(1)}, u32[]{:S(2)}, u32[]{:S(2)}) collective-permute-start(bf16[512,512]{1,0:T(8,128)(2,1)} %refs_9_.2), channel_id=1, source_target_pairs={{0,16},{16,0},{1,17},{17,1},{2,18},{18,2},{3,19},{19,3},{4,20},{20... | collective-permute-start | bytes 1572872 | tf_op jit(solution)/shard_map/ppermute | solution.py:500
  25.4 48.4 %collective-permute-start.5 = (bf16[1280,512]{1,0:T(8,128)(2,1)}, bf16[1280,512]{1,0:T(8,128)(2,1)S(1)}, u32[]{:S(2)}, u32[]{:S(2)}) collective-permute-start(bf16[1280,512]{1,0:T(8,128)(2,1)} %get-tuple-element.584.refs_6_.refs_9_.refs_11_.refs_10_.refs_19_.refs_1_), channel_id=1, source_target_pairs={{0,16},{16,0},{1,17},{17,1},{2,18},{18,2},{3,19},{19,3},{4,20},{20... | collective-permute-start | bytes 3932168 | tf_op jit(solution)/shard_map/ppermute | solution.py:500
  29.8 13.5 %collective-permute-start.7 = (bf16[512,512]{1,0:T(8,128)(2,1)}, bf16[512,512]{1,0:T(8,128)(2,1)S(1)}, u32[]{:S(2)}, u32[]{:S(2)}) collective-permute-start(bf16[512,512]{1,0:T(8,128)(2,1)} %get-tuple-element.507.refs_2_.refs_18_), channel_id=1, source_target_pairs={{0,4},{4,8},{8,12},{1,5},{5,9},{9,13},{2,6},{6,10},{10,14},{3,7},{... | collective-permute-start | bytes 1572872 | tf_op jit(solution)/shard_map/ppermute | solution.py:737
  33.9 46.9 %collective-permute-start.6 = (bf16[512,768]{1,0:T(8,128)(2,1)}, bf16[512,768]{1,0:T(8,128)(2,1)}, u32[]{:S(2)}, u32[]{:S(2)}) collective-permute-start(bf16[512,768]{1,0:T(8,128)(2,1)} %refs_6_), channel_id=1, source_target_pairs={{0,16},{16,0},{1,17},{17,1},{2,18},{18,2},{3,19},{19,3},{4,20},{20... | collective-permute-start | bytes 2359304 | tf_op jit(solution)/shard_map/ppermute | solution.py:500
  43.3 30.4 %collective-permute-start.8 = (bf16[512,512]{1,0:T(8,128)(2,1)S(1)}, bf16[512,512]{1,0:T(8,128)(2,1)S(1)}, u32[]{:S(2)}, u32[]{:S(2)}) collective-permute-start(bf16[512,512]{1,0:T(8,128)(2,1)S(1)} %collective-permute-done.7.refs_5_.refs_17_), channel_id=1, source_target_pairs={{0,4},{4,8},{8,12},{1,5},{5,9},{9,13},{2,6},{6,10},{10,14},{3,7},{... | collective-permute-start | bytes 1572872 | tf_op jit(solution)/shard_map/ppermute | solution.py:742
  48.8 33.6 %collective-permute-start.3 = (bf16[512,512]{1,0:T(8,128)(2,1)}, bf16[512,512]{1,0:T(8,128)(2,1)}, u32[]{:S(2)}, u32[]{:S(2)}) collective-permute-start(bf16[512,512]{1,0:T(8,128)(2,1)} %get-tuple-element.551.refs_2_.refs_18_), channel_id=1, source_target_pairs={{0,4},{4,8},{8,12},{1,5},{5,9},{9,13},{2,6},{6,10},{10,14},{3,7},{... | collective-permute-start | bytes 1572872 | tf_op jit(solution)/shard_map/ppermute | solution.py:737
  80.8 9.7 %collective-permute-start.9 = (bf16[256,1024]{1,0:T(8,128)(2,1)}, bf16[256,1024]{1,0:T(8,128)(2,1)S(1)}, u32[]{:S(2)}, u32[]{:S(2)}) collective-permute-start(bf16[256,1024]{1,0:T(8,128)(2,1)} %get-tuple-element.418), channel_id=1, source_target_pairs={{0,1},{1,0},{2,3},{3,2},{4,5},{5,4},{6,7},{7,6},{8,9},{9,8},{10,11... | collective-permute-start | bytes 1572872 | tf_op jit(solution)/shard_map/ppermute | solution.py:500
  80.8 28.4 %collective-permute-start.11 = (bf16[512,768]{1,0:T(8,128)(2,1)}, bf16[512,768]{1,0:T(8,128)(2,1)S(1)}, u32[]{:S(2)}, u32[]{:S(2)}) collective-permute-start(bf16[512,768]{1,0:T(8,128)(2,1)} %refs_8_), channel_id=1, source_target_pairs={{0,16},{16,0},{1,17},{17,1},{2,18},{18,2},{3,19},{19,3},{4,20},{20... | collective-permute-start | bytes 2359304 | tf_op jit(solution)/shard_map/ppermute | solution.py:500
  82.4 18.8 %collective-permute-start.4 = (bf16[512,512]{1,0:T(8,128)(2,1)}, bf16[512,512]{1,0:T(8,128)(2,1)}, u32[]{:S(2)}, u32[]{:S(2)}) collective-permute-start(bf16[512,512]{1,0:T(8,128)(2,1)} %collective-permute-done.3.refs_8_.refs_17_), channel_id=1, source_target_pairs={{0,4},{4,8},{8,12},{1,5},{5,9},{9,13},{2,6},{6,10},{10,14},{3,7},{... | collective-permute-start | bytes 1572872 | tf_op jit(solution)/shard_map/ppermute | solution.py:742
  91.7 16.2 %collective-permute-start.10 = (bf16[256,1024]{1,0:T(8,128)(2,1)S(1)}, bf16[256,1024]{1,0:T(8,128)(2,1)}, u32[]{:S(2)}, u32[]{:S(2)}) collective-permute-start(bf16[256,1024]{1,0:T(8,128)(2,1)S(1)} %add.123), channel_id=1, source_target_pairs={{0,2},{1,3},{2,0},{3,1},{4,6},{5,7},{6,4},{7,5},{8,10},{9,11},{10,... | collective-permute-start | bytes 1572872 | tf_op jit(solution)/shard_map/ppermute | solution.py:500
  109.2 2.0 collective-permute-start.12
  109.3 3.7 collective-permute-start.14
  111.4 15.0 %collective-permute-start.13 = (bf16[256,1024]{1,0:T(8,128)(2,1)S(1)}, bf16[256,1024]{1,0:T(8,128)(2,1)S(1)}, u32[]{:S(2)}, u32[]{:S(2)}) collective-permute-start(bf16[256,1024]{1,0:T(8,128)(2,1)S(1)} %add.125), channel_id=1, source_target_pairs={{0,2},{1,3},{2,0},{3,1},{4,6},{5,7},{6,4},{7,5},{8,10},{9,11},{10,... | collective-permute-start | bytes 1572872 | tf_op jit(solution)/shard_map/ppermute | solution.py:500
  127.4 2.7 collective-permute-start.15
  129.5 14.0 %collective-permute-start.17 = (bf16[256,1024]{1,0:T(8,128)(2,1)S(1)}, bf16[256,1024]{1,0:T(8,128)(2,1)S(1)}, u32[]{:S(2)}, u32[]{:S(2)}) collective-permute-start(bf16[256,1024]{1,0:T(8,128)(2,1)S(1)} %add.127), channel_id=1, source_target_pairs={{0,2},{1,3},{2,0},{3,1},{4,6},{5,7},{6,4},{7,5},{8,10},{9,11},{10,... | collective-permute-start | bytes 1572872 | tf_op jit(solution)/shard_map/ppermute | solution.py:500
  144.6 3.6 collective-permute-start.20
  146.6 27.1 %collective-permute-start.19 = (bf16[256,1024]{1,0:T(8,128)(2,1)S(1)}, bf16[256,1024]{1,0:T(8,128)(2,1)S(1)}, u32[]{:S(2)}, u32[]{:S(2)}) collective-permute-start(bf16[256,1024]{1,0:T(8,128)(2,1)S(1)} %add.129), channel_id=1, source_target_pairs={{0,2},{1,3},{2,0},{3,1},{4,6},{5,7},{6,4},{7,5},{8,10},{9,11},{10,... | collective-permute-start | bytes 1572872 | tf_op jit(solution)/shard_map/ppermute | solution.py:500
  164.1 18.8 %collective-permute-start.22 = (bf16[512,512]{1,0:T(8,128)(2,1)}, bf16[512,512]{1,0:T(8,128)(2,1)S(1)}, u32[]{:S(2)}, u32[]{:S(2)}) collective-permute-start(bf16[512,512]{1,0:T(8,128)(2,1)} %get-tuple-element.530), channel_id=1, source_target_pairs={{4,0},{8,4},{12,8},{5,1},{9,5},{13,9},{6,2},{10,6},{14,10},{7,3},{... | collective-permute-start | bytes 1572872 | tf_op jit(solution)/shard_map/ppermute | solution.py:861
  173.9 16.2 %collective-permute-start.21 = (bf16[256,1024]{1,0:T(8,128)(2,1)S(1)}, bf16[256,1024]{1,0:T(8,128)(2,1)S(1)}, u32[]{:S(2)}, u32[]{:S(2)}) collective-permute-start(bf16[256,1024]{1,0:T(8,128)(2,1)S(1)} %add.130.refs_3_), channel_id=1, source_target_pairs={{0,1},{1,0},{2,3},{3,2},{4,5},{5,4},{6,7},{7,6},{8,9},{9,8},{10,11... | collective-permute-start | bytes 1572872 | tf_op jit(solution)/shard_map/ppermute | solution.py:500
  183.8 22.1 %collective-permute-start.23 = (bf16[512,512]{1,0:T(8,128)(2,1)}, bf16[512,512]{1,0:T(8,128)(2,1)S(1)}, u32[]{:S(2)}, u32[]{:S(2)}) collective-permute-start(bf16[512,512]{1,0:T(8,128)(2,1)} %add.131), channel_id=1, source_target_pairs={{4,0},{8,4},{12,8},{5,1},{9,5},{13,9},{6,2},{10,6},{14,10},{7,3},{... | collective-permute-start | bytes 1572872 | tf_op jit(solution)/shard_map/ppermute | solution.py:861
  185.1 56.3 %collective-permute-start.25 = (bf16[512,1536]{1,0:T(8,128)(2,1)}, bf16[512,1536]{1,0:T(8,128)(2,1)}, u32[]{:S(2)}, u32[]{:S(2)}) collective-permute-start(bf16[512,1536]{1,0:T(8,128)(2,1)} %get-tuple-element.590), channel_id=1, source_target_pairs={{0,16},{16,0},{1,17},{17,1},{2,18},{18,2},{3,19},{19,3},{4,20},{20... | collective-permute-start | bytes 4718600 | tf_op jit(solution)/shard_map/ppermute | solution.py:500
  205.9 19.7 %collective-permute-start.24 = (bf16[512,512]{1,0:T(8,128)(2,1)}, bf16[512,512]{1,0:T(8,128)(2,1)S(1)}, u32[]{:S(2)}, u32[]{:S(2)}) collective-permute-start(bf16[512,512]{1,0:T(8,128)(2,1)} %get-tuple-element.557), channel_id=1, source_target_pairs={{4,0},{8,4},{12,8},{5,1},{9,5},{13,9},{6,2},{10,6},{14,10},{7,3},{... | collective-permute-start | bytes 1572872 | tf_op jit(solution)/shard_map/ppermute | solution.py:861
  219.0 44.0 %collective-permute-start.30 = (bf16[1280,512]{1,0:T(8,128)(2,1)}, bf16[1280,512]{1,0:T(8,128)(2,1)}, u32[]{:S(2)}, u32[]{:S(2)}) collective-permute-start(bf16[1280,512]{1,0:T(8,128)(2,1)} %get-tuple-element.640), channel_id=1, source_target_pairs={{0,16},{16,0},{1,17},{17,1},{2,18},{18,2},{3,19},{19,3},{4,20},{20... | collective-permute-start | bytes 3932168 | tf_op jit(solution)/shard_map/ppermute | solution.py:500
  226.6 27.8 %collective-permute-start.27 = (bf16[512,512]{1,0:T(8,128)(2,1)}, bf16[512,512]{1,0:T(8,128)(2,1)}, u32[]{:S(2)}, u32[]{:S(2)}) collective-permute-start(bf16[512,512]{1,0:T(8,128)(2,1)} %add.132), channel_id=1, source_target_pairs={{4,0},{8,4},{12,8},{5,1},{9,5},{13,9},{6,2},{10,6},{14,10},{7,3},{... | collective-permute-start | bytes 1572872 | tf_op jit(solution)/shard_map/ppermute | solution.py:861
  228.1 37.1 %collective-permute-start.29 = (bf16[512,512]{1,0:T(8,128)(2,1)}, bf16[512,512]{1,0:T(8,128)(2,1)}, u32[]{:S(2)}, u32[]{:S(2)}) collective-permute-start(bf16[512,512]{1,0:T(8,128)(2,1)} %get-tuple-element.639), channel_id=1, source_target_pairs={{0,16},{16,0},{1,17},{17,1},{2,18},{18,2},{3,19},{19,3},{4,20},{20... | collective-permute-start | bytes 1572872 | tf_op jit(solution)/shard_map/ppermute | solution.py:500
  243.3 42.9 %collective-permute-start.26 = (bf16[512,1536]{1,0:T(8,128)(2,1)S(1)}, bf16[512,1536]{1,0:T(8,128)(2,1)}, u32[]{:S(2)}, u32[]{:S(2)}) collective-permute-start(bf16[512,1536]{1,0:T(8,128)(2,1)S(1)} %add.133), channel_id=1, source_target_pairs={{0,4},{12,8},{1,5},{13,9},{2,6},{14,10},{3,7},{15,11},{16,20},{28,... | collective-permute-start | bytes 4718600 | tf_op jit(solution)/shard_map/ppermute | solution.py:556
  263.0 4.2 collective-permute-start.28
  267.2 3.7 collective-permute-start.31
  278.2 2.9 collective-permute-start.32
  289.1 7.7 %collective-permute-start.33 = (bf16[512,1024]{1,0:T(8,128)(2,1)S(1)}, bf16[512,1024]{1,0:T(8,128)(2,1)S(1)}, u32[]{:S(2)}, u32[]{:S(2)}) collective-permute-start(bf16[512,1024]{1,0:T(8,128)(2,1)S(1)} %copy-done.25), channel_id=1, source_target_pairs={{0,1},{1,0},{2,3},{3,2},{4,5},{5,4},{6,7},{7,6},{8,9},{9,8},{10,11... | collective-permute-start | bytes 3145736 | tf_op jit(solution)/shard_map/ppermute | solution.py:500
  289.1 25.6 %collective-permute-start.39 = (bf16[512,1024]{1,0:T(8,128)(2,1)S(1)}, bf16[512,1024]{1,0:T(8,128)(2,1)S(1)}, u32[]{:S(2)}, u32[]{:S(2)}) collective-permute-start(bf16[512,1024]{1,0:T(8,128)(2,1)S(1)} %add.142), channel_id=1, source_target_pairs={{0,2},{1,3},{2,0},{3,1},{4,6},{5,7},{6,4},{7,5},{8,10},{9,11},{10,... | collective-permute-start | bytes 3145736 | tf_op jit(solution)/shard_map/ppermute | solution.py:500
  289.3 33.1 %collective-permute-start.38 = (bf16[1280,512]{1,0:T(8,128)(2,1)S(1)}, bf16[1280,512]{1,0:T(8,128)(2,1)}, u32[]{:S(2)}, u32[]{:S(2)}) collective-permute-start(bf16[1280,512]{1,0:T(8,128)(2,1)S(1)} %add.138), channel_id=1, source_target_pairs={{0,4},{12,8},{1,5},{13,9},{2,6},{14,10},{3,7},{15,11},{16,20},{28,... | collective-permute-start | bytes 3932168 | tf_op jit(solution)/shard_map/ppermute | solution.py:556
  295.0 44.5 %collective-permute-start.37 = (bf16[512,1536]{1,0:T(8,128)(2,1)}, bf16[512,1536]{1,0:T(8,128)(2,1)}, u32[]{:S(2)}, u32[]{:S(2)}) collective-permute-start(bf16[512,1536]{1,0:T(8,128)(2,1)} %add.143), channel_id=1, source_target_pairs={{4,8},{8,4},{5,9},{9,5},{6,10},{10,6},{7,11},{11,7},{20,24},{24,20... | collective-permute-start | bytes 4718600 | tf_op jit(solution)/shard_map/ppermute | solution.py:559
  315.1 2.9 collective-permute-start.40
  315.2 41.5 %collective-permute-start.34 = (bf16[512,1024]{1,0:T(8,128)(2,1)S(1)}, bf16[512,1024]{1,0:T(8,128)(2,1)}, u32[]{:S(2)}, u32[]{:S(2)}) collective-permute-start(bf16[512,1024]{1,0:T(8,128)(2,1)S(1)} %add.144), channel_id=1, source_target_pairs={{0,2},{1,3},{2,0},{3,1},{4,6},{5,7},{6,4},{7,5},{8,10},{9,11},{10,... | collective-permute-start | bytes 3145736 | tf_op jit(solution)/shard_map/ppermute | solution.py:500
  325.3 37.6 %collective-permute-start.43 = (bf16[1280,512]{1,0:T(8,128)(2,1)}, bf16[1280,512]{1,0:T(8,128)(2,1)}, u32[]{:S(2)}, u32[]{:S(2)}) collective-permute-start(bf16[1280,512]{1,0:T(8,128)(2,1)} %add.146), channel_id=1, source_target_pairs={{4,8},{8,4},{5,9},{9,5},{6,10},{10,6},{7,11},{11,7},{20,24},{24,20... | collective-permute-start | bytes 3932168 | tf_op jit(solution)/shard_map/ppermute | solution.py:559
  327.1 24.2 %collective-permute-start.35 = (bf16[528,512]{1,0:T(8,128)(2,1)S(1)}, bf16[528,512]{1,0:T(8,128)(2,1)S(1)}, u32[]{:S(2)}, u32[]{:S(2)}) collective-permute-start(bf16[528,512]{1,0:T(8,128)(2,1)S(1)} %copy-done.39), channel_id=1, source_target_pairs={{0,16},{16,0},{1,17},{17,1},{2,18},{18,2},{3,19},{19,3},{4,20},{20... | collective-permute-start | bytes 1622024 | tf_op jit(solution)/shard_map/ppermute | solution.py:500
  327.8 22.6 %collective-permute-start.36 = (bf16[512,512]{1,0:T(8,128)(2,1)S(1)}, bf16[512,512]{1,0:T(8,128)(2,1)S(1)}, u32[]{:S(2)}, u32[]{:S(2)}) collective-permute-start(bf16[512,512]{1,0:T(8,128)(2,1)S(1)} %copy-done.18), channel_id=1, source_target_pairs={{0,4},{12,8},{1,5},{13,9},{2,6},{14,10},{3,7},{15,11},{16,20},{28,... | collective-permute-start | bytes 1572872 | tf_op jit(solution)/shard_map/ppermute | solution.py:556
  341.9 40.2 %collective-permute-start.44 = (bf16[512,1536]{1,0:T(8,128)(2,1)S(1)}, bf16[512,1536]{1,0:T(8,128)(2,1)}, u32[]{:S(2)}, u32[]{:S(2)}) collective-permute-start(bf16[512,1536]{1,0:T(8,128)(2,1)S(1)} %add.147), channel_id=1, source_target_pairs={{4,0},{8,12},{5,1},{9,13},{6,2},{10,14},{7,3},{11,15},{20,16},{24,... | collective-permute-start | bytes 4718600 | tf_op jit(solution)/shard_map/ppermute | solution.py:564
  351.5 14.9 %collective-permute-start.42 = (bf16[528,512]{1,0:T(8,128)(2,1)S(1)}, bf16[528,512]{1,0:T(8,128)(2,1)}, u32[]{:S(2)}, u32[]{:S(2)}) collective-permute-start(bf16[528,512]{1,0:T(8,128)(2,1)S(1)} %add.149), channel_id=1, source_target_pairs={{0,4},{12,8},{1,5},{13,9},{2,6},{14,10},{3,7},{15,11},{16,20},{28,... | collective-permute-start | bytes 1622024 | tf_op jit(solution)/shard_map/ppermute | solution.py:556
  358.3 13.7 %collective-permute-start.41 = (bf16[512,1024]{1,0:T(8,128)(2,1)S(1)}, bf16[512,1024]{1,0:T(8,128)(2,1)}, u32[]{:S(2)}, u32[]{:S(2)}) collective-permute-start(bf16[512,1024]{1,0:T(8,128)(2,1)S(1)} %add.150.refs_3_), channel_id=1, source_target_pairs={{0,1},{1,0},{2,3},{3,2},{4,5},{5,4},{6,7},{7,6},{8,9},{9,8},{10,11... | collective-permute-start | bytes 3145736 | tf_op jit(solution)/shard_map/ppermute | solution.py:500
  367.5 12.0 %collective-permute-start.45 = (bf16[528,512]{1,0:T(8,128)(2,1)S(1)}, bf16[528,512]{1,0:T(8,128)(2,1)}, u32[]{:S(2)}, u32[]{:S(2)}) collective-permute-start(bf16[528,512]{1,0:T(8,128)(2,1)S(1)} %add.152), channel_id=1, source_target_pairs={{4,8},{8,4},{5,9},{9,5},{6,10},{10,6},{7,11},{11,7},{20,24},{24,20... | collective-permute-start | bytes 1622024 | tf_op jit(solution)/shard_map/ppermute | solution.py:559
  369.0 7.1 %collective-permute-start.46 = (bf16[512,512]{1,0:T(8,128)(2,1)}, bf16[512,512]{1,0:T(8,128)(2,1)}, u32[]{:S(2)}, u32[]{:S(2)}) collective-permute-start(bf16[512,512]{1,0:T(8,128)(2,1)} %add.148), channel_id=1, source_target_pairs={{4,8},{8,4},{5,9},{9,5},{6,10},{10,6},{7,11},{11,7},{20,24},{24,20... | collective-permute-start | bytes 1572872 | tf_op jit(solution)/shard_map/ppermute | solution.py:559
  370.5 38.9 %collective-permute-start.49 = (bf16[1280,512]{1,0:T(8,128)(2,1)}, bf16[1280,512]{1,0:T(8,128)(2,1)}, u32[]{:S(2)}, u32[]{:S(2)}) collective-permute-start(bf16[1280,512]{1,0:T(8,128)(2,1)} %add.151), channel_id=1, source_target_pairs={{4,0},{8,12},{5,1},{9,13},{6,2},{10,14},{7,3},{11,15},{20,16},{24,... | collective-permute-start | bytes 3932168 | tf_op jit(solution)/shard_map/ppermute | solution.py:564
  378.3 42.4 %collective-permute-start.48 = (bf16[512,512]{1,0:T(8,128)(2,1)}, bf16[512,512]{1,0:T(8,128)(2,1)}, u32[]{:S(2)}, u32[]{:S(2)}) collective-permute-start(bf16[512,512]{1,0:T(8,128)(2,1)} %add.153), channel_id=1, source_target_pairs={{4,0},{8,12},{5,1},{9,13},{6,2},{10,14},{7,3},{11,15},{20,16},{24,... | collective-permute-start | bytes 1572872 | tf_op jit(solution)/shard_map/ppermute | solution.py:564
  380.7 49.7 %collective-permute-start.47 = (bf16[528,512]{1,0:T(8,128)(2,1)S(1)}, bf16[528,512]{1,0:T(8,128)(2,1)S(1)}, u32[]{:S(2)}, u32[]{:S(2)}) collective-permute-start(bf16[528,512]{1,0:T(8,128)(2,1)S(1)} %add.154), channel_id=1, source_target_pairs={{4,0},{8,12},{5,1},{9,13},{6,2},{10,14},{7,3},{11,15},{20,16},{24,... | collective-permute-start | bytes 1622024 | tf_op jit(solution)/shard_map/ppermute | solution.py:564
  (48 other events, 274.2 us)
